TPU v7x, 8 devices: a whole 2x2x1 slice. The times are simulated.
8 devices in a mesh: data: 2 (over z, y), seq: 4 (over x, core).
Axes of the slice: x: 2, y: 2, z: 1, core: 2. Of those that a mesh axis runs over, the one named last changes fastest.
Arguments:
- dec_in: bfloat16 [2048, 768], P(('data', 'seq')), parts along dimension 0
- memory: bfloat16 [16384, 768], P(('data', 'seq')), parts along dimension 0
- mem_len: int32 [2], P('data'), parts along dimension 0
- grad_out: float32 [2048, 768], P(('data', 'seq')), parts along dimension 0
- norm_attn: bfloat16 [768], replicated
- wq_cross: bfloat16 [768, 12, 64], replicated
- wk_cross: bfloat16 [768, 12, 64], replicated
- wv_cross: bfloat16 [768, 12, 64], replicated
- wo_cross: bfloat16 [12, 64, 768], replicated
- norm_mlp: bfloat16 [768], replicated
- w_gate: bfloat16 [768, 3072], replicated
- w_up: bfloat16 [768, 3072], replicated
- w_down: bfloat16 [3072, 768], replicated
Outputs:
- output 1: float32 [2048, 768], P(('data', 'seq')), parts along dimension 0
- output 2: float32 [16384, 768], P(('data', 'seq')), parts along dimension 0
- output 3: float32 [1536], P('data'), parts along dimension 0
- output 4: float32 [1536, 12, 64], P('data'), parts along dimension 0
- output 5: float32 [1536, 12, 64], P('data'), parts along dimension 0
- output 6: float32 [1536, 12, 64], P('data'), parts along dimension 0
- output 7: float32 [24, 64, 768], P('data'), parts along dimension 0
- output 8: float32 [1536], P('data'), parts along dimension 0
- output 9: float32 [1536, 3072], P('data'), parts along dimension 0
- output 10: float32 [1536, 3072], P('data'), parts along dimension 0
- output 11: float32 [6144, 768], P('data'), parts along dimension 0
There are 2 independent parts. A program takes and returns all parts, laid end to end along the dimension named above; an argument that names none is the same for every part.
All inputs are finite; a program needn't handle non-finite values.
Results may differ from a plain program's by a relative error of at most 0.013332.
Values are sent between devices in bfloat16 or wider.
A program may use at most 1 GiB of HBM per device.

v0:
```python
import jax
import jax.numpy as jnp
from jax import lax
from jax.experimental import pallas as pl
from jax.experimental.pallas import tpu as pltpu
from jax.sharding import PartitionSpec as P


LOG2E = 1.4426950408889634
NEG = -1e30
BF = jnp.bfloat16
F32 = jnp.float32
FKB = 512
FQB = 512
BKB = 512
BQB = 256
PAIR = 128
OROWS = 72
FFB = 512
MB = 512


def dot(a, b):
    return jnp.dot(a, b, preferred_element_type=F32)


def dot_nt(a, b):
    return lax.dot_general(a, b, (((1,), (1,)), ((), ())), preferred_element_type=F32)


def cost(flops, bytes_accessed, exps=0):
    return pl.CostEstimate(flops=int(flops), bytes_accessed=int(bytes_accessed), transcendentals=int(exps))


def proj_kernel(core_ref, m_ref, wk_ref, wv_ref, *refs):
    k_ref, v_ref, kt_ref, vt_ref = refs[-4:]
    m = m_ref[...]
    k = dot_nt(m, wk_ref[...]).astype(BF)
    v = dot_nt(m, wv_ref[...]).astype(BF)
    k_ref[...] = k
    v_ref[...] = v
    kt_ref[...] = k.T
    vt_ref[...] = v.T


def project(core, mem, wkt, wvt, seg, before):
    rows, dim = mem.shape
    width = wkt.shape[0] // 2
    steps = rows // MB
    base = seg * steps
    weights = pl.BlockSpec((width, dim), lambda i, s: (s[0], 0))
    down = pl.BlockSpec((MB, width), lambda i, s: (base + i, 0))
    across = pl.BlockSpec((width, MB), lambda i, s: (0, base + i))
    outs = [jax.ShapeDtypeStruct((2 * rows, width), BF)] * 2 + [jax.ShapeDtypeStruct((width, 2 * rows), BF)] * 2
    return pl.pallas_call(
        proj_kernel,
        out_shape=outs,
        grid_spec=pltpu.PrefetchScalarGridSpec(
            num_scalar_prefetch=1, grid=(steps,),
            in_specs=[pl.BlockSpec((MB, dim), lambda i, s: (i, 0)), weights, weights]
                     + [pl.BlockSpec(memory_space=pl.ANY)] * len(before),
            out_specs=[down, down, across, across]),
        input_output_aliases={4 + i: i for i in range(len(before))},
        compiler_params=pltpu.CompilerParams(vmem_limit_bytes=60 << 20),
        cost_estimate=cost(4 * rows * dim * width, 12 << 20),
        name="kv_proj",
    )(core, mem, wkt, wvt, *before)


def query_kernel(place_ref, x0_ref, x1_ref, x2_ref, x3_ref, gain_ref, wq_ref, x_ref, n_ref, q_ref, qt_ref):
    for part, src in enumerate((x0_ref, x1_ref, x2_ref, x3_ref)):
        @pl.when(pl.program_id(0) == part)
        def _():
            xb = src[...]
            x = xb.astype(F32)
            n1 = (x * inv_rms(x) * gain_ref[...]).astype(BF)
            q = dot_nt(n1, wq_ref[...]).astype(BF) * jnp.asarray(0.125, BF)
            x_ref[...] = xb
            n_ref[...] = n1
            q_ref[...] = q
            qt_ref[...] = q.T


def queries(place, parts, gain, wqt):
    rows, dim = parts[0].shape
    width = wqt.shape[0] // 2
    n = len(parts)
    whole = pl.BlockSpec((rows, dim), lambda i, s: (0, 0))
    put = pl.BlockSpec((rows, dim), lambda i, s: (s[i], 0))
    return pl.pallas_call(
        query_kernel,
        out_shape=[jax.ShapeDtypeStruct((n * rows, dim), BF)] * 2
                  + [jax.ShapeDtypeStruct((n * rows, width), BF), jax.ShapeDtypeStruct((width, n * rows), BF)],
        grid_spec=pltpu.PrefetchScalarGridSpec(
            num_scalar_prefetch=1, grid=(n,),
            in_specs=[whole] * n + [pl.BlockSpec((1, dim), lambda i, s: (0, 0)),
                                    pl.BlockSpec((width, dim), lambda i, s: (s[n], 0))],
            out_specs=[put, put, pl.BlockSpec((rows, width), lambda i, s: (s[i], 0)),
                       pl.BlockSpec((width, rows), lambda i, s: (0, s[i]))]),
        compiler_params=pltpu.CompilerParams(vmem_limit_bytes=24 << 20),
        cost_estimate=cost(2 * n * rows * dim * width, 6 << 20),
        name="queries",
    )(place, *parts, gain, wqt)


def place_kernel(place_ref, x0_ref, x1_ref, x2_ref, x3_ref, o_ref):
    for part, src in enumerate((x0_ref, x1_ref, x2_ref, x3_ref)):
        @pl.when(pl.program_id(0) == part)
        def _():
            o_ref[...] = src[...]


def place_rows(place, parts):
    rows, dim = parts[0].shape
    n = len(parts)
    return pl.pallas_call(
        place_kernel,
        out_shape=jax.ShapeDtypeStruct((n * rows, dim), parts[0].dtype),
        grid_spec=pltpu.PrefetchScalarGridSpec(
            num_scalar_prefetch=1, grid=(n,),
            in_specs=[pl.BlockSpec((rows, dim), lambda i, s: (0, 0))] * n,
            out_specs=pl.BlockSpec((rows, dim), lambda i, s: (s[i], 0))),
        compiler_params=pltpu.CompilerParams(vmem_limit_bytes=16 << 20),
        cost_estimate=cost(n * rows * dim, 6 << 20),
        name="place_rows",
    )(place, *parts)


def fwd_kernel(len_ref, qt_ref, k_ref, vt_ref, o_ref, m_ref, l_ref, acc_ref, qz_ref, sa_ref, sb_ref):
    qb = qt_ref.shape[1]
    seg_rows = k_ref.shape[0] // 2
    half = lax.broadcasted_iota(jnp.int32, (PAIR, qb), 0) // 64
    for h in range(2):
        qz_ref[h] = jnp.where(half == h, qt_ref[...], jnp.zeros((), BF))
    m_ref[...] = jnp.full(m_ref.shape, NEG, F32)
    l_ref[...] = jnp.zeros(l_ref.shape, F32)
    acc_ref[...] = jnp.zeros(acc_ref.shape, F32)
    first = len_ref[0] // FKB
    total = first + len_ref[1] // FKB

    def base(t):
        t = jnp.clip(t, 0, jnp.maximum(total - 1, 0))
        return pl.multiple_of(jnp.where(t < first, t * FKB, seg_rows + (t - first) * FKB), FKB)

    def scores(row, s_ref):
        kb = k_ref[pl.ds(row, FKB), :]
        for h in range(2):
            s_ref[h] = dot(kb, qz_ref[h])

    def absorb(row, s_ref, count=None):
        rows = pl.ds(row, FKB)
        for h in range(2):
            st = s_ref[h]
            if count is not None:
                st = jnp.where(lax.broadcasted_iota(jnp.int32, st.shape, 0) < count, st, NEG)
            m_old = m_ref[h]
            m_new = jnp.maximum(m_old, jnp.max(st, axis=0, keepdims=True))
            p = jnp.exp2((st - m_new) * LOG2E)
            alpha = jnp.exp2((m_old - m_new) * LOG2E)
            l_ref[h] = l_ref[h] * alpha + jnp.sum(p, axis=0, keepdims=True)
            pv = dot(vt_ref[h * 64:(h + 1) * 64, rows], p.astype(BF))
            acc_ref[h] = acc_ref[h] * alpha + pv
            m_ref[h] = m_new

    scores(base(0), sa_ref)

    @pl.loop(0, total // 2)
    def _(i):
        scores(base(2 * i + 1), sb_ref)
        absorb(base(2 * i), sa_ref)
        scores(base(2 * i + 2), sa_ref)
        absorb(base(2 * i + 1), sb_ref)

    @pl.when(total % 2 == 1)
    def _():
        absorb(base(total - 1), sa_ref)

    @pl.loop(0, 2)
    def _(s):
        full = len_ref[s] // FKB
        rest = len_ref[s] - full * FKB

        @pl.when(rest > 0)
        def _():
            row = pl.multiple_of(s * seg_rows + full * FKB, FKB)
            scores(row, sa_ref)
            absorb(row, sa_ref, rest)

    for h in range(2):
        o_ref[h, 0:64, :] = acc_ref[h]
        o_ref[h, 64:72, :] = jnp.concatenate([m_ref[h], l_ref[h], jnp.zeros((6, qb), F32)], axis=0)


def attention_forward(lens, qt, k, vt, pair0, pairs, at, nq):
    q_off = at // FQB
    rows = k.shape[0]
    off = pair0
    spec = pltpu.PrefetchScalarGridSpec(
        num_scalar_prefetch=1,
        grid=(pairs, nq // FQB),
        in_specs=[
            pl.BlockSpec((PAIR, FQB), lambda p, i, s: (p + off, i + q_off)),
            pl.BlockSpec((rows, PAIR), lambda p, i, s: (0, p + off)),
            pl.BlockSpec((PAIR, rows), lambda p, i, s: (p + off, 0)),
        ],
        out_specs=pl.BlockSpec((2, OROWS, FQB), lambda p, i, s: (p, 0, i)),
        scratch_shapes=[
            pltpu.VMEM((2, 1, FQB), F32), pltpu.VMEM((2, 1, FQB), F32), pltpu.VMEM((2, 64, FQB), F32),
            pltpu.VMEM((2, PAIR, FQB), BF), pltpu.VMEM((2, FKB, FQB), F32), pltpu.VMEM((2, FKB, FQB), F32),
        ])
    work = 2 * pairs * nq * rows
    return pl.pallas_call(
        fwd_kernel,
        out_shape=jax.ShapeDtypeStruct((2 * pairs, OROWS, nq), F32),
        grid_spec=spec,
        compiler_params=pltpu.CompilerParams(vmem_limit_bytes=60 << 20),
        cost_estimate=cost(work * 1024, 4 << 20, work),
        name="attn_fwd",
    )(lens, qt, k, vt)


def bwd_kernel(len_ref, qt_ref, dot_ref, lse_ref, dl_ref, k_ref, v_ref, kt_ref, dkv_ref, dqt_ref, qzt_ref, dozt_ref):
    nq = qt_ref.shape[1]
    seg_rows = k_ref.shape[0] // 2
    blocks = seg_rows // BKB
    half = lax.broadcasted_iota(jnp.int32, (PAIR, nq), 0) // 64
    zero = jnp.zeros((), BF)
    for h in range(2):
        qzt_ref[h] = jnp.where(half == h, qt_ref[...], zero)
        dozt_ref[h] = jnp.where(half == h, dot_ref[...], zero)
    dqt_ref[...] = jnp.zeros(dqt_ref.shape, F32)

    def step(seg, j, count):
        cols = pl.ds(pl.multiple_of(j * BKB, BKB), BKB)
        allc = pl.ds(pl.multiple_of(seg * seg_rows + j * BKB, BKB), BKB)
        kb, vb = k_ref[allc, :], v_ref[allc, :]
        for h in range(2):
            hs = slice(h * 64, (h + 1) * 64)
            ktb = kt_ref[hs, allc]
            dk = jnp.zeros((64, BKB), F32)
            dv = jnp.zeros((64, BKB), F32)
            for c in range(nq // BQB):
                qs = slice(c * BQB, (c + 1) * BQB)
                st = dot(kb, qzt_ref[h, :, qs])
                p = jnp.exp2((st - lse_ref[h, :, qs]) * LOG2E)
                if count is not None:
                    p = jnp.where(lax.broadcasted_iota(jnp.int32, st.shape, 0) < count, p, 0.0)
                dp = dot(vb, dozt_ref[h, :, qs])
                ds = (p * (dp - dl_ref[h, :, qs])).astype(BF)
                dv = dv + dot_nt(dot_ref[hs, qs], p.astype(BF))
                dk = dk + dot_nt(qt_ref[hs, qs], ds)
                dqt_ref[h, :, qs] += dot(ktb, ds)
            dkv_ref[seg, hs, cols] = dk.astype(BF)
            dkv_ref[seg, PAIR + h * 64:PAIR + (h + 1) * 64, cols] = dv.astype(BF)

    first = len_ref[0] // BKB

    @pl.loop(0, first + len_ref[1] // BKB)
    def _(t):
        seg = jnp.where(t < first, 0, 1)
        step(seg, t - seg * first, None)

    @pl.loop(0, 2)
    def _(seg):
        full = len_ref[seg] // BKB
        rest = len_ref[seg] - full * BKB

        @pl.when(rest > 0)
        def _():
            step(seg, full, rest)

        @pl.loop(full + jnp.where(rest > 0, 1, 0), blocks)
        def _(j):
            cols = pl.ds(pl.multiple_of(j * BKB, BKB), BKB)
            dkv_ref[seg, :, cols] = jnp.zeros((2 * PAIR, BKB), BF)


def attention_backward(lens, qt, dot_t, lse, delta, k, v, kt, pair0):
    nq = qt.shape[1]
    rows = k.shape[0]
    off = pair0
    across = pl.BlockSpec((PAIR, nq), lambda p, s: (off, 0))
    stat = pl.BlockSpec((2, 1, nq), lambda p, s: (off, 0, 0))
    keys = pl.BlockSpec((rows, PAIR), lambda p, s: (0, off))
    keys_t = pl.BlockSpec((PAIR, rows), lambda p, s: (off, 0))
    spec = pltpu.PrefetchScalarGridSpec(
        num_scalar_prefetch=1,
        grid=(1,),
        in_specs=[across, across, stat, stat, keys, keys, keys_t],
        out_specs=[pl.BlockSpec((2, 2 * PAIR, rows // 2), lambda p, s: (0, 0, 0)),
                   pl.BlockSpec((2, 64, nq), lambda p, s: (0, 0, 0))],
        scratch_shapes=[pltpu.VMEM((2, PAIR, nq), BF), pltpu.VMEM((2, PAIR, nq), BF)])
    work = 2 * nq * rows
    return pl.pallas_call(
        bwd_kernel,
        out_shape=[jax.ShapeDtypeStruct((2, 2 * PAIR, rows // 2), BF), jax.ShapeDtypeStruct((2, 64, nq), F32)],
        grid_spec=spec,
        compiler_params=pltpu.CompilerParams(vmem_limit_bytes=40 << 20),
        cost_estimate=cost(work * 2000, 8 << 20, work),
        name="attn_bwd",
    )(lens, qt, dot_t, lse, delta, k, v, kt)


def mlp_kernel(h_ref, g_ref, gain_ref, w1_ref, w3_ref, w2_ref,
               n2t_ref, gt_ref, dgate_ref, dup_ref, ut_ref, dh_ref, dhb_ref, gn_ref, n2_ref, acc_ref):
    step = pl.program_id(0)
    rows = h_ref.shape[0]
    chunk = 512

    @pl.when(step == 0)
    def _():
        for c in range(rows // chunk):
            rs = slice(c * chunk, (c + 1) * chunk)
            hid = h_ref[rs, :].astype(F32)
            n2 = (hid * inv_rms(hid) * gain_ref[...]).astype(BF)
            n2_ref[rs, :] = n2
            n2t_ref[:, rs] = n2.T
            gt_ref[rs, :] = g_ref[rs, :].astype(BF)
        acc_ref[...] = jnp.zeros(acc_ref.shape, F32)

    w1, w3, w2 = w1_ref[...], w3_ref[...], w2_ref[...]
    for c in range(rows // chunk):
        rs = slice(c * chunk, (c + 1) * chunk)
        n2 = n2_ref[rs, :]
        gate = dot(n2, w1)
        up = dot(n2, w3)
        ga = dot_nt(gt_ref[rs, :], w2)
        sig = 0.5 * jnp.tanh(0.5 * gate) + 0.5
        act = gate * sig
        ut_ref[:, rs] = (act * up).astype(BF).T
        dup = (ga * act).astype(BF)
        dgate = (ga * up * (sig + act * (1.0 - sig))).astype(BF)
        dup_ref[rs, :] = dup
        dgate_ref[rs, :] = dgate
        acc_ref[rs, :] += dot_nt(dgate, w1) + dot_nt(dup, w3)

    @pl.when(step == pl.num_programs(0) - 1)
    def _():
        total = jnp.zeros(gn_ref.shape, F32)
        for c in range(rows // chunk):
            rs = slice(c * chunk, (c + 1) * chunk)
            hid = h_ref[rs, :].astype(F32)
            inv = inv_rms(hid)
            unit = hid * inv
            grad = acc_ref[rs, :]
            total += jnp.sum(grad * unit, axis=0, keepdims=True)
            dh = g_ref[rs, :] + norm_back(unit, inv, gain_ref[...], grad)
            dh_ref[rs, :] = dh
            dhb_ref[rs, :] = dh.astype(BF)
        gn_ref[...] = total


def mlp(hidden, g_all, gain, w_gate, w_up, w_down):
    rows, dim = hidden.shape
    ff = w_gate.shape[1]
    fix = lambda *shape: pl.BlockSpec(shape, lambda i: (0,) * len(shape))
    wide = pl.BlockSpec((dim, FFB), lambda i: (0, i))
    tall = pl.BlockSpec((FFB, dim), lambda i: (i, 0))
    act = pl.BlockSpec((rows, FFB), lambda i: (0, i))
    act_t = pl.BlockSpec((FFB, rows), lambda i: (i, 0))
    return pl.pallas_call(
        mlp_kernel,
        grid=(ff // FFB,),
        in_specs=[fix(rows, dim), fix(rows, dim), fix(1, dim), wide, wide, tall],
        out_specs=[fix(dim, rows), fix(rows, dim), act, act, act_t, fix(rows, dim), fix(rows, dim), fix(1, dim)],
        out_shape=[jax.ShapeDtypeStruct((dim, rows), BF), jax.ShapeDtypeStruct((rows, dim), BF),
                   jax.ShapeDtypeStruct((rows, ff), BF), jax.ShapeDtypeStruct((rows, ff), BF),
                   jax.ShapeDtypeStruct((ff, rows), BF), jax.ShapeDtypeStruct((rows, dim), F32),
                   jax.ShapeDtypeStruct((rows, dim), BF), jax.ShapeDtypeStruct((1, dim), F32)],
        scratch_shapes=[pltpu.VMEM((rows, dim), BF), pltpu.VMEM((rows, dim), F32)],
        compiler_params=pltpu.CompilerParams(vmem_limit_bytes=56 << 20),
        cost_estimate=cost(10 * rows * dim * ff, 40 << 20, rows * ff),
        name="mlp",
    )(hidden, g_all, gain, w_gate, w_up, w_down)


def mlp_weights_kernel(n2t_ref, gt_ref, dgate_ref, dup_ref, ut_ref, g1_ref, g3_ref, g2_ref):
    g1_ref[...] = dot(n2t_ref[...], dgate_ref[...])
    g3_ref[...] = dot(n2t_ref[...], dup_ref[...])
    g2_ref[...] = dot(ut_ref[...], gt_ref[...])


def mlp_weights(n2t, g_top, d_gate, d_up, act_t):
    dim, rows = n2t.shape
    ff = d_gate.shape[1]
    fix = lambda *shape: pl.BlockSpec(shape, lambda i: (0,) * len(shape))
    act = pl.BlockSpec((rows, FFB), lambda i: (0, i))
    wide = pl.BlockSpec((dim, FFB), lambda i: (0, i))
    return pl.pallas_call(
        mlp_weights_kernel,
        grid=(ff // FFB,),
        in_specs=[fix(dim, rows), fix(rows, dim), act, act, pl.BlockSpec((FFB, rows), lambda i: (i, 0))],
        out_specs=[wide, wide, pl.BlockSpec((FFB, dim), lambda i: (i, 0))],
        out_shape=[jax.ShapeDtypeStruct((dim, ff), F32)] * 2 + [jax.ShapeDtypeStruct((ff, dim), F32)],
        compiler_params=pltpu.CompilerParams(vmem_limit_bytes=60 << 20),
        cost_estimate=cost(6 * rows * dim * ff, 50 << 20),
        name="mlp_weights",
    )(n2t, g_top, d_gate, d_up, act_t)


def memory_kernel(core_ref, a0_ref, a1_ref, a2_ref, b0_ref, b1_ref, b2_ref, wk_ref, wv_ref, o_ref):
    core = core_ref[0]
    total = None
    for who, refs in ((core, (a0_ref, a1_ref, a2_ref)), (1 - core, (b0_ref, b1_ref, b2_ref))):
        for i, ref in enumerate(refs):
            rows = pl.ds(pl.multiple_of((who * 3 + i) * PAIR, PAIR), PAIR)
            part = dot(ref[...].T, jnp.concatenate([wk_ref[rows, :], wv_ref[rows, :]], axis=0))
            total = part if total is None else total + part
    o_ref[...] = total


def memory_grad(core, mine, near, wkt, wvt):
    rows = mine[0].shape[-1]
    dim = wkt.shape[1]
    block = pl.BlockSpec((None, 2 * PAIR, MB), lambda i, s: (0, 0, i))
    block2 = pl.BlockSpec((2 * PAIR, MB), lambda i, s: (0, i))
    whole = pl.BlockSpec(wkt.shape, lambda i, s: (0, 0))
    return pl.pallas_call(
        memory_kernel,
        out_shape=jax.ShapeDtypeStruct((rows, dim), F32),
        grid_spec=pltpu.PrefetchScalarGridSpec(
            num_scalar_prefetch=1, grid=(rows // MB,),
            in_specs=[block] * 3 + [block2] * 3 + [whole, whole],
            out_specs=pl.BlockSpec((MB, dim), lambda i, s: (i, 0))),
        compiler_params=pltpu.CompilerParams(vmem_limit_bytes=32 << 20),
        cost_estimate=cost(4 * rows * dim * dim, 16 << 20),
        name="memory_grad",
    )(core, *mine, *near, wkt, wvt)


def half_index(i, core):
    return i + core - 2 * i * core


def out_proj_kernel(core_ref, mine_ref, near_ref, dh_ref, o_ref):
    for who, ref in enumerate((mine_ref, near_ref)):
        @pl.when(pl.program_id(0) == who)
        def _():
            o_ref[...] = dot(ref[...], dh_ref[...])


def out_proj_grad(core, mine, near, dh):
    width, rows = mine.shape
    dim = dh.shape[1]
    whole = pl.BlockSpec((width, rows), lambda i, s: (0, 0))
    return pl.pallas_call(
        out_proj_kernel,
        out_shape=jax.ShapeDtypeStruct((2 * width, dim), F32),
        grid_spec=pltpu.PrefetchScalarGridSpec(
            num_scalar_prefetch=1, grid=(2,),
            in_specs=[whole, whole, pl.BlockSpec((rows, dim), lambda i, s: (0, 0))],
            out_specs=pl.BlockSpec((width, dim), lambda i, s: (half_index(i, s[0]), 0))),
        compiler_params=pltpu.CompilerParams(vmem_limit_bytes=24 << 20),
        cost_estimate=cost(4 * rows * dim * width, 6 << 20),
        name="out_proj_grad",
    )(core, mine, near, dh)


def query_grad_kernel(place_ref, mine_ref, near_ref, n1_ref, wq_ref, x_ref, dh_ref, gain_ref,
                      gw_ref, gx_ref, gn_ref, acc_ref):
    for who, ref in enumerate((mine_ref, near_ref)):
        @pl.when(pl.program_id(0) == who)
        def _():
            dq = ref[...]
            gw_ref[...] = dot(dq, n1_ref[...])
            part = dot(dq.T, wq_ref[...])
            acc_ref[...] = part if who == 0 else acc_ref[...] + part

    @pl.when(pl.program_id(0) == 1)
    def _():
        rows = gx_ref.shape[0]
        total = jnp.zeros(gn_ref.shape, F32)
        for c in range(acc_ref.shape[0] // rows):
            rs = slice(c * rows, (c + 1) * rows)
            x = x_ref[rs, :].astype(F32)
            total += jnp.sum(acc_ref[rs, :] * (x * inv_rms(x)), axis=0, keepdims=True)
        gn_ref[...] = total
        own = pl.ds(pl.multiple_of(place_ref[0] * rows, rows), rows)
        x = x_ref[own, :].astype(F32)
        inv = inv_rms(x)
        gx_ref[...] = dh_ref[...] + norm_back(x * inv, inv, gain_ref[...], acc_ref[own, :])


def query_grad(place, mine, near, n1, wqt, x_all, d_hid, gain, rows):
    width, total = mine.shape
    dim = n1.shape[1]
    fix = lambda *shape: pl.BlockSpec(shape, lambda i, s: (0,) * len(shape))
    half = pl.BlockSpec((width, dim), lambda i, s: (half_index(i, s[4]), 0))
    return pl.pallas_call(
        query_grad_kernel,
        out_shape=[jax.ShapeDtypeStruct((2 * width, dim), F32), jax.ShapeDtypeStruct((rows, dim), F32),
                   jax.ShapeDtypeStruct((1, dim), F32)],
        grid_spec=pltpu.PrefetchScalarGridSpec(
            num_scalar_prefetch=1, grid=(2,),
            in_specs=[fix(width, total), fix(width, total), fix(total, dim), half, fix(total, dim),
                      pl.BlockSpec((rows, dim), lambda i, s: (s[0], 0)), fix(1, dim)],
            out_specs=[half, fix(rows, dim), fix(1, dim)],
            scratch_shapes=[pltpu.VMEM((total, dim), F32)]),
        compiler_params=pltpu.CompilerParams(vmem_limit_bytes=32 << 20),
        cost_estimate=cost(8 * total * dim * width, 10 << 20),
        name="query_grad",
    )(place, mine, near, n1, wqt, x_all, d_hid, gain)


def key_weights_kernel(core_ref, a0_ref, a1_ref, a2_ref, b0_ref, b1_ref, b2_ref, gk_ref, gv_ref):
    for at, ref in enumerate((a0_ref, a1_ref, a2_ref, b0_ref, b1_ref, b2_ref)):
        @pl.when(pl.program_id(0) == at)
        def _():
            gk_ref[...] = ref[:PAIR, :]
            gv_ref[...] = ref[PAIR:, :]


def key_weights(core, mine, near):
    pairs = len(mine)
    dim = mine[0].shape[1]
    out = pl.BlockSpec((PAIR, dim), lambda i, s: (half_index(i // pairs, s[0]) * pairs + i % pairs, 0))
    return pl.pallas_call(
        key_weights_kernel,
        out_shape=[jax.ShapeDtypeStruct((2 * pairs * PAIR, dim), F32)] * 2,
        grid_spec=pltpu.PrefetchScalarGridSpec(
            num_scalar_prefetch=1, grid=(2 * pairs,),
            in_specs=[pl.BlockSpec((2 * PAIR, dim), lambda i, s: (0, 0))] * (2 * pairs),
            out_specs=[out, out]),
        compiler_params=pltpu.CompilerParams(vmem_limit_bytes=24 << 20),
        cost_estimate=cost(4 * pairs * PAIR * dim, 10 << 20),
        name="key_weights",
    )(core, *mine, *near)


def inv_rms(tensor):
    return lax.rsqrt(jnp.mean(tensor * tensor, axis=-1, keepdims=True) + 1e-6)


def norm_back(unit, inv, gain, grad):
    scaled = grad * gain
    return inv * (scaled - unit * jnp.mean(scaled * unit, axis=-1, keepdims=True))


def mm(a, b, ca, cb, dtype=F32):
    out = lax.dot_general(a, b, (((ca,), (cb,)), ((), ())), preferred_element_type=F32)
    return out if dtype == F32 else out.astype(dtype)


def solution(mesh):
    n = mesh.shape['seq']
    near = [(i, i ^ 1) for i in range(n)]
    far = [(i, i ^ 2) for i in range(n)]
    row_spec = P(('data', 'seq'), None)
    weight_spec = P()
    part_vec = P('data')
    part_mat = P('data', None)
    part_cube = P('data', None, None)

    def to_near(a):
        return lax.ppermute(a, 'seq', near)

    def to_far(a):
        return lax.ppermute(a, 'seq', far)

    def device_work(dec_in, memory, mem_len, grad_out, norm_attn, wq, wk, wv, wo, norm_mlp, w_gate, w_up, w_down):
        rows, dim = dec_in.shape
        m_rows = memory.shape[0]
        heads, head = wq.shape[1], wq.shape[2]
        mine = heads // 2
        width = mine * head
        dev = lax.axis_index('seq')
        core = lax.rem(dev, 2)
        core1 = core.reshape(1).astype(jnp.int32)
        wqt, wkt, wvt = (w.transpose(1, 2, 0).reshape(heads * head, dim) for w in (wq, wk, wv))
        wo2 = wo.reshape(heads * head, dim)
        lens = jnp.stack([jnp.clip(mem_len[0] - i * m_rows, 0, m_rows) for i in (dev, dev ^ 1)]).astype(jnp.int32)
        place = jnp.stack([dev, dev ^ 1, dev ^ 2, dev ^ 3, core]).astype(jnp.int32)
        gain1 = norm_attn.astype(F32).reshape(1, dim)
        gain2 = norm_mlp.astype(F32).reshape(1, dim)

        def gather_parts(a):
            across = to_far(a)
            beside = to_near(a)
            return a, beside, across, to_near(across)

        x_parts = gather_parts(dec_in)
        mem_near = to_near(memory)
        g_parts = gather_parts(grad_out)

        first = project(core1, memory, wkt, wvt, 0, ())
        x_all_b, n1, _, qt_s = queries(place, x_parts, gain1, wqt)
        k, v, kt, vt = project(core1, mem_near, wkt, wvt, 1, first)

        pairs = mine // 2
        pieces = [(pair, 0, n * rows) for pair in range(pairs - 1)]
        pieces += [(pairs - 1, 0, n * rows // 2), (pairs - 1, n * rows // 2, n * rows // 2)]
        outs, lses = [], []
        parts = []
        for pair, at, count in pieces:
            part = attention_forward(lens, qt_s, k, vt, pair, 1, at, count)
            parts.append((part, to_far(part)))
        for a, b in parts:
            ma, mb = a[:, 64:65], b[:, 64:65]
            top = jnp.maximum(ma, mb)
            ea, eb = jnp.exp(ma - top), jnp.exp(mb - top)
            den = a[:, 65:66] * ea + b[:, 65:66] * eb
            outs.append((a[:, :64] * ea + b[:, :64] * eb) / den)
            lses.append(top + jnp.log(den))
        outs[-2:] = [jnp.concatenate(outs[-2:], axis=2)]
        lses[-2:] = [jnp.concatenate(lses[-2:], axis=2)]
        g_all = place_rows(place, g_parts)
        o_t = jnp.concatenate(outs, axis=0)
        lse = jnp.concatenate(lses, axis=0)
        o_t_b = o_t.astype(BF).reshape(width, n * rows)
        o_t_near = to_near(o_t_b)

        def half_rows(w, who):
            return lax.dynamic_slice(w, (who * width, 0), (width, dim))

        wo_m, wo_n = half_rows(wo2, core), half_rows(wo2, 1 - core)
        x_all = x_all_b.astype(F32)
        hidden = (x_all + mm(o_t_b, wo_m, 0, 0) + mm(o_t_near, wo_n, 0, 0)).astype(BF)

        n2t, g_top, d_gate, d_up, act_t, d_hid, d_hid_b, g_norm_mlp = mlp(hidden, g_all, gain2, w_gate, w_up, w_down)

        do_t_f = mm(wo_m, d_hid_b, 1, 1)
        delta = jnp.sum(do_t_f.reshape(mine, head, n * rows) * o_t, axis=1, keepdims=True)
        do_t = do_t_f.astype(BF)
        dkvs, dkvs_near, dqs, dws = [], [], [], []
        lens_now = lens
        for pair in range(pairs):
            dkv, dqt = attention_backward(lens_now, qt_s, do_t, lse, delta, k, v, kt, pair)
            dqs.append((dqt, to_far(dqt)))
            dw = mm(dkv[0], memory, 1, 0) + mm(dkv[1], mem_near, 1, 0)
            dws.append((dw, to_far(dw)))
            dkvs.append(dkv)
            dkvs_near.append(to_near(dkv[1]))
            lens_now, dw_last = lax.optimization_barrier((lens, dw))

        d_gate, _ = lax.optimization_barrier((d_gate, dw_last))
        g_gate, g_up, g_down = mlp_weights(n2t, g_top, d_gate, d_up, act_t)
        g_mem = memory_grad(core1, dkvs, dkvs_near, wkt, wvt)

        def as_weight(rows_by_dim):
            return rows_by_dim.reshape(heads, head, dim).transpose(2, 0, 1)

        g_wo = out_proj_grad(core1, o_t_b, o_t_near, d_hid_b).reshape(heads, head, dim)

        dqt_b = (jnp.concatenate([a + b for a, b in dqs], axis=0) * (head ** -0.5)).astype(BF).reshape(width, n * rows)
        dqt_near = to_near(dqt_b)
        g_wqt, g_dec, g_norm_attn = query_grad(place, dqt_b, dqt_near, n1, wqt, x_all_b, d_hid, gain1, rows)

        dw_mine, dw_near = [], []
        for a, b in dws:
            dw_mine.append(a + b)
            dw_near.append(to_near(dw_mine[-1]))
        g_wkt, g_wvt = key_weights(core1, dw_mine, dw_near)
        g_wq, g_wk, g_wv = as_weight(g_wqt), as_weight(g_wkt), as_weight(g_wvt)
        return (g_dec, g_mem, g_norm_attn.reshape(dim), g_wq, g_wk, g_wv, g_wo, g_norm_mlp.reshape(dim), g_gate, g_up, g_down)


    return jax.shard_map(device_work, mesh=mesh,
                         in_specs=(row_spec, row_spec, part_vec, row_spec) + (weight_spec,) * 9,
                         out_specs=(row_spec, row_spec, part_vec, part_cube, part_cube, part_cube, part_cube,
                                    part_vec, part_mat, part_mat, part_mat),
                         check_vma=False)
```

profile of v0, /device:TPU:5, one launch (start us, length us, event | category | flops | bytes accessed | tf_op | source)
XLA Modules:
  0.0 375.6 jit_solution(14287856219909195211)
XLA Ops:
  0.7 0.7 collective-permute-start.3
  1.4 1.2 collective-permute-start.10
  3.4 25.6 %collective-permute-done.1.x2_ref = bf16[256,768]{1,0:T(8,128)(2,1)S(1)} collective-permute-done((bf16[256,768]{1,0:T(8,128)(2,1)}, bf16[256,768]{1,0:T(8,128)(2,1)S(1)}, u32[]{:S(2)}, u32[]{:S(2)}) %collective-permute-start.1) | collective-permute-done | bytes 393248 | tf_op jit(solution)/shard_map/ppermute | solution.py:558
  29.1 0.9 collective-permute-start.2
  32.0 7.2 %kv_proj.2 = (bf16[4096,384]{1,0:T(8,128)(2,1)}, bf16[4096,384]{1,0:T(8,128)(2,1)}, bf16[384,4096]{1,0:T(8,128)(2,1)}, bf16[384,4096]{1,0:T(8,128)(2,1)}) custom-call(s32[1]{0:T(128)} %bitcast.4.core_ref, bf16[2048,768]{1,0:T(8,128)(2,1)} %m_ref.1, bf16[768,768]{1,0:T(8,128)(2,1)} %bitcast.96, bf16[768,768]{1,0:T(8,128)(2,1)} %bitcast.99), custom_call_target="tpu_custom_call" | custom-call | flops 2415919104 | bytes 12582912 | tf_op jit(solution)/shard_map/kv_proj/pallas_call | solution.py:55
  39.8 0.7 copy-done.22
  40.5 1.3 copy-done.3
  41.8 1.0 copy-done.23
  42.8 3.7 queries.1
  46.5 1.1 copy-done.18
  47.6 0.9 copy-done.25
  48.5 7.2 %kv_proj.3 = (bf16[4096,384]{1,0:T(8,128)(2,1)}, bf16[4096,384]{1,0:T(8,128)(2,1)}, bf16[384,4096]{1,0:T(8,128)(2,1)}, bf16[384,4096]{1,0:T(8,128)(2,1)}) custom-call(s32[1]{0:T(128)} %bitcast.4.core_ref, bf16[2048,768]{1,0:T(8,128)(2,1)} %collective-permute-done.3.m_ref, ...), custom_call_target="tpu_custom_call", output_to_operand_aliasing={{0}: (4, {}), {1}: (5, {}), {2}: (6, {}), {3}: (7, {})} | custom-call | flops 2415919104 | bytes 12582912 | tf_op jit(solution)/shard_map/kv_proj/pallas_call | solution.py:55
  55.7 9.8 %attn_fwd.6 = f32[2,72,512]{2,1,0:T(8,128)} custom-call(s32[2]{0:T(128)} %pad_add_fusion.len_ref, bf16[384,1024]{1,0:T(8,128)(2,1)} %copy-done.25, bf16[4096,384]{1,0:T(8,128)(2,1)} %get-tuple-element.52.k_ref, bf16[384,4096]{1,0:T(8,128)(2,1)} %get-tuple-element.53.vt_ref), custom_call_target="tpu_custom_call" | custom-call | flops 4294967296 | bytes 4194304 | tf_op jit(solution)/shard_map/attn_fwd/pallas_call | solution.py:212
  65.5 16.3 %attn_fwd.5 = f32[2,72,1024]{2,1,0:T(8,128)} custom-call(s32[2]{0:T(128)} %pad_add_fusion.len_ref, bf16[384,1024]{1,0:T(8,128)(2,1)} %copy-done.25, bf16[4096,384]{1,0:T(8,128)(2,1)} %get-tuple-element.52.k_ref, bf16[384,4096]{1,0:T(8,128)(2,1)} %get-tuple-element.53.vt_ref), custom_call_target="tpu_custom_call" | custom-call | flops 8589934592 | bytes 4194304 | tf_op jit(solution)/shard_map/attn_fwd/pallas_call | solution.py:212
  81.8 16.5 %attn_fwd.4 = f32[2,72,1024]{2,1,0:T(8,128)} custom-call(s32[2]{0:T(128)} %pad_add_fusion.len_ref, bf16[384,1024]{1,0:T(8,128)(2,1)} %copy-done.25, bf16[4096,384]{1,0:T(8,128)(2,1)} %get-tuple-element.52.k_ref, bf16[384,4096]{1,0:T(8,128)(2,1)} %get-tuple-element.53.vt_ref), custom_call_target="tpu_custom_call" | custom-call | flops 8589934592 | bytes 4194304 | tf_op jit(solution)/shard_map/attn_fwd/pallas_call | solution.py:212
  98.3 10.1 %attn_fwd.7 = f32[2,72,512]{2,1,0:T(8,128)} custom-call(s32[2]{0:T(128)} %pad_add_fusion.len_ref, bf16[384,1024]{1,0:T(8,128)(2,1)} %copy-done.25, bf16[4096,384]{1,0:T(8,128)(2,1)} %get-tuple-element.52.k_ref, bf16[384,4096]{1,0:T(8,128)(2,1)} %get-tuple-element.53.vt_ref), custom_call_target="tpu_custom_call" | custom-call | flops 4294967296 | bytes 4194304 | tf_op jit(solution)/shard_map/attn_fwd/pallas_call | solution.py:212
  108.4 1.5 collective-permute-start.4
  109.9 1.5 log_add_fusion.3
  111.4 5.8 %collective-permute-done.7 = f32[2,72,512]{2,1,0:T(8,128)S(1)} collective-permute-done((f32[2,72,512]{2,1,0:T(8,128)}, f32[2,72,512]{2,1,0:T(8,128)S(1)}, u32[]{:S(2)}, u32[]{:S(2)}) %collective-permute-start.7) | collective-permute-done | bytes 294944 | tf_op jit(solution)/shard_map/ppermute | solution.py:558
  117.2 1.5 log_add_fusion.2
  118.7 1.0 fusion.26
  119.7 1.1 fusion.24
  120.9 9.0 %collective-permute-done.4 = f32[2,72,1024]{2,1,0:T(8,128)S(1)} collective-permute-done((f32[2,72,1024]{2,1,0:T(8,128)}, f32[2,72,1024]{2,1,0:T(8,128)S(1)}, u32[]{:S(2)}, u32[]{:S(2)}) %collective-permute-start.4) | collective-permute-done | bytes 589856 | tf_op jit(solution)/shard_map/ppermute | solution.py:558
  129.9 1.0 log_add_fusion.1
  130.9 11.6 %collective-permute-done.5 = f32[2,72,1024]{2,1,0:T(8,128)S(1)} collective-permute-done((f32[2,72,1024]{2,1,0:T(8,128)S(1)}, f32[2,72,1024]{2,1,0:T(8,128)S(1)}, u32[]{:S(2)}, u32[]{:S(2)}) %collective-permute-start.5) | collective-permute-done | bytes 589856 | tf_op jit(solution)/shard_map/ppermute | solution.py:558
  144.2 0.9 collective-permute-start.8
  145.1 1.3 reshape.92.gain_ref
  146.4 1.1 copy-done.20
  147.5 2.5 place_rows.1.g_ref
  150.1 0.7 maximum_maximum_fusion.1.lse_ref
  150.8 1.0 fusion.21
  151.8 3.4 add_convert_fusion.h_ref
  155.2 39.3 %mlp.1 = (bf16[768,1024]{1,0:T(8,128)(2,1)}, bf16[1024,768]{1,0:T(8,128)(2,1)}, bf16[1024,3072]{1,0:T(8,128)(2,1)}, bf16[1024,3072]{1,0:T(8,128)(2,1)}, bf16[307...) custom-call(bf16[1024,768]{1,0:T(8,128)(2,1)} %add_convert_fusion.h_ref, ...), custom_call_target="tpu_custom_call" | custom-call | flops 24159191040 | bytes 41943040 | tf_op jit(solution)/shard_map/mlp/pallas_call | solution.py:361
  194.6 2.4 fusion.38
  197.4 1.5 copy-done.15
  198.9 1.9 copy-done.17
  200.8 25.1 %attn_bwd.3 = (bf16[2,256,2048]{2,1,0:T(8,128)(2,1)S(1)}, f32[2,64,1024]{2,1,0:T(8,128)S(1)}) custom-call(s32[2]{0:T(128)S(1)} %copy-done.27, bf16[384,1024]{1,0:T(8,128)(2,1)S(1)} %copy-done.26, bf16[384,1024]{1,0:T(8,128)(2,1)S(1)} %get-tuple-element.97.dot_ref, f32[6,1,1024]{2,1,0:T(1,128)S(1)} %copy-done.24, f32[6,1,1024]{2,1,0:T(1,128)S(1)} %broadcast_in_dim.3.dl_ref, ...), custom_call_target="tpu_custom_call" | custom-call | flops 16777216000 | bytes 8388608 | tf_op jit(solution)/shard_map/attn_bwd/pallas_call | solution.py:294
  225.9 1.0 fusion.5
  226.9 2.9 convolution_add_fusion.2
  229.9 1.2 slice_bitcast_fusion.2
  231.1 1.4 collective-permute-start.12
  232.4 25.3 %attn_bwd.4 = (bf16[2,256,2048]{2,1,0:T(8,128)(2,1)S(1)}, f32[2,64,1024]{2,1,0:T(8,128)S(1)}) custom-call(s32[2]{0:T(128)S(1)} %copy-done.27, bf16[384,1024]{1,0:T(8,128)(2,1)S(1)} %copy-done.26, bf16[384,1024]{1,0:T(8,128)(2,1)S(1)} %get-tuple-element.97.dot_ref, f32[6,1,1024]{2,1,0:T(1,128)S(1)} %copy-done.24, f32[6,1,1024]{2,1,0:T(1,128)S(1)} %broadcast_in_dim.3.dl_ref, ...), custom_call_target="tpu_custom_call" | custom-call | flops 16777216000 | bytes 8388608 | tf_op jit(solution)/shard_map/attn_bwd/pallas_call | solution.py:294
  257.8 1.0 fusion.3
  258.8 3.8 %convolution_add_fusion.1 = f32[256,768]{1,0:T(8,128)} fusion(f32[256,768]{1,0:T(8,128)S(1)} %fusion.3, bf16[2048,768]{1,0:T(8,128)(2,1)} %collective-permute-done.3.m_ref, bf16[2,256,2048]{2,1,0:T(8,128)(2,1)S(1)} %get-tuple-element.61.a1_ref), kind=kOutput, calls=%fused_computation.6 | convolution fusion | flops 805502976 | bytes 5767168 | tf_op jit(solution)/shard_map/dot_general | solution.py:540
  262.5 25.3 %attn_bwd.5 = (bf16[2,256,2048]{2,1,0:T(8,128)(2,1)S(1)}, f32[2,64,1024]{2,1,0:T(8,128)S(1)}) custom-call(s32[2]{0:T(128)S(1)} %copy-done.27, bf16[384,1024]{1,0:T(8,128)(2,1)S(1)} %copy-done.26, bf16[384,1024]{1,0:T(8,128)(2,1)S(1)} %get-tuple-element.97.dot_ref, f32[6,1,1024]{2,1,0:T(1,128)S(1)} %copy-done.24, f32[6,1,1024]{2,1,0:T(1,128)S(1)} %broadcast_in_dim.3.dl_ref, ...), custom_call_target="tpu_custom_call" | custom-call | flops 16777216000 | bytes 8388608 | tf_op jit(solution)/shard_map/attn_bwd/pallas_call | solution.py:294
  287.9 1.0 fusion.1
  288.9 2.9 convolution_add_fusion
  291.8 1.5 collective-permute-start.21
  293.3 1.1 slice_bitcast_fusion
  294.4 1.1 slice_bitcast_fusion.1
  295.7 1.2 collective-permute-start.16
  296.9 3.9 %collective-permute-done.14 = f32[2,64,1024]{2,1,0:T(8,128)S(1)} collective-permute-done((f32[2,64,1024]{2,1,0:T(8,128)S(1)}, f32[2,64,1024]{2,1,0:T(8,128)S(1)}, u32[]{:S(2)}, u32[]{:S(2)}) %collective-permute-start.14) | collective-permute-done | bytes 524320 | tf_op jit(solution)/shard_map/ppermute | solution.py:558
  300.8 2.5 collective-permute-start.17
  303.5 14.2 %collective-permute-done.21 = f32[256,768]{1,0:T(8,128)S(1)} collective-permute-done((f32[256,768]{1,0:T(8,128)S(1)}, f32[256,768]{1,0:T(8,128)S(1)}, u32[]{:S(2)}, u32[]{:S(2)}) %collective-permute-start.21) | collective-permute-done | bytes 786464 | tf_op jit(solution)/shard_map/ppermute | solution.py:558
  317.7 0.9 copy-done.39
  318.6 2.5 collective-permute-start.15
  321.1 20.9 %mlp_weights.1 = (f32[768,3072]{1,0:T(8,128)}, f32[768,3072]{1,0:T(8,128)}, f32[3072,768]{1,0:T(8,128)}) custom-call(bf16[768,1024]{1,0:T(8,128)(2,1)} %get-tuple-element.73.n2t_ref, bf16[1024,768]{1,0:T(8,128)(2,1)} %get-tuple-element.74.gt_ref, bf16[1024,3072]{1,0:T(8,128)(2,1)} %get-tuple-element.75.dgate_ref, ...), custom_call_target="tpu_custom_call" | custom-call | flops 14495514624 | bytes 52428800 | tf_op jit(solution)/shard_map/mlp_weights/pallas_call | solution.py:389
  342.5 2.5 add.96.a0_ref
  345.0 1.0 add.99.a2_ref
  346.1 2.5 add.97.a1_ref
  349.1 4.0 %out_proj_grad.1 = f32[768,768]{1,0:T(8,128)} custom-call(s32[1]{0:T(128)} %bitcast.4.core_ref, bf16[384,1024]{1,0:T(8,128)(2,1)S(1)} %bitcast.93, bf16[384,1024]{1,0:T(8,128)(2,1)} %collective-permute-done.8.near_ref, bf16[1024,768]{1,0:T(8,128)(2,1)S(1)} %copy-done.2), custom_call_target="tpu_custom_call" | custom-call | flops 1207959552 | bytes 6291456 | tf_op jit(solution)/shard_map/out_proj_grad/pallas_call | solution.py:446
  353.2 8.6 %memory_grad.1 = f32[2048,768]{1,0:T(8,128)} custom-call(s32[1]{0:T(128)} %bitcast.4.core_ref, bf16[2,256,2048]{2,1,0:T(8,128)(2,1)S(1)} %copy-done.6, bf16[2,256,2048]{2,1,0:T(8,128)(2,1)S(1)} %copy-done.8, bf16[2,256,2048]{2,1,0:T(8,128)(2,1)S(1)} %copy-done.10, bf16[256,2048]{1,0:T(8,128)(2,1)} %collective-permute-done.16.b0_ref, ...), custom_call_target="tpu_custom_call" | custom-call | flops 4831838208 | bytes 16777216 | tf_op jit(solution)/shard_map/memory_grad/pallas_call | solution.py:418
  361.9 7.1 %query_grad.1 = (f32[768,768]{1,0:T(8,128)}, f32[256,768]{1,0:T(8,128)}, f32[1,768]{1,0:T(1,128)S(1)}) custom-call(s32[5]{0:T(128)S(1)} %stack.32.place_ref, bf16[384,1024]{1,0:T(8,128)(2,1)S(1)} %bitcast.103, bf16[384,1024]{1,0:T(8,128)(2,1)} %collective-permute-done.15.near_ref, bf16[1024,768]{1,0:T(8,128)(2,1)S(1)} %copy-done.19, ...), custom_call_target="tpu_custom_call" | custom-call | flops 2415919104 | bytes 10485760 | tf_op jit(solution)/shard_map/query_grad/pallas_call | solution.py:489
  369.6 5.5 %key_weights.1 = (f32[768,768]{1,0:T(8,128)}, f32[768,768]{1,0:T(8,128)}) custom-call(s32[1]{0:T(128)} %bitcast.4.core_ref, f32[256,768]{1,0:T(8,128)} %add.96.a0_ref, f32[256,768]{1,0:T(8,128)} %add.97.a1_ref, f32[256,768]{1,0:T(8,128)} %add.99.a2_ref, f32[256,768]{1,0:T(8,128)} %collective-permute-done.22.b0_ref, ...), custom_call_target="tpu_custom_call" | custom-call | flops 1179648 | bytes 10485760 | tf_op jit(solution)/shard_map/key_weights/pallas_call | solution.py:517
  (146 shorter events, 7.5 us)
Async XLA Ops:
  0.6 150.1 %copy-start = (bf16[12,64,768]{2,1,0:T(8,128)(2,1)S(1)}, bf16[12,64,768]{2,1,0:T(8,128)(2,1)}, u32[]{:S(2)}) copy-start(bf16[12,64,768]{2,1,0:T(8,128)(2,1)} %param.21) | copy-start | bytes 3538948
  0.7 47.8 %collective-permute-start.3 = (bf16[2048,768]{1,0:T(8,128)(2,1)}, bf16[2048,768]{1,0:T(8,128)(2,1)}, u32[]{:S(2)}, u32[]{:S(2)}) collective-permute-start(bf16[2048,768]{1,0:T(8,128)(2,1)} %m_ref.1), channel_id=1, source_target_pairs={{0,1},{1,0},{2,3},{3,2},{4,5},{5,4},{6,7},{7,6}} | collective-permute-start | bytes 9437192 | tf_op jit(solution)/shard_map/ppermute | solution.py:555
  1.4 37.9 %collective-permute-start.10 = (f32[256,768]{1,0:T(8,128)}, f32[256,768]{1,0:T(8,128)}, u32[]{:S(2)}, u32[]{:S(2)}) collective-permute-start(f32[256,768]{1,0:T(8,128)} %x0_ref.3), channel_id=1, source_target_pairs={{0,2},{1,3},{2,0},{3,1},{4,6},{5,7},{6,4},{7,5}} | collective-permute-start | bytes 2359304 | tf_op jit(solution)/shard_map/ppermute | solution.py:558
  2.6 26.5 %collective-permute-start.1 = (bf16[256,768]{1,0:T(8,128)(2,1)}, bf16[256,768]{1,0:T(8,128)(2,1)S(1)}, u32[]{:S(2)}, u32[]{:S(2)}) collective-permute-start(bf16[256,768]{1,0:T(8,128)(2,1)} %x0_ref.2), channel_id=1, source_target_pairs={{0,2},{1,3},{2,0},{3,1},{4,6},{5,7},{6,4},{7,5}} | collective-permute-start | bytes 1179656 | tf_op jit(solution)/shard_map/ppermute | solution.py:558
  2.8 37.0 %collective-permute-start = (bf16[256,768]{1,0:T(8,128)(2,1)}, bf16[256,768]{1,0:T(8,128)(2,1)S(1)}, u32[]{:S(2)}, u32[]{:S(2)}) collective-permute-start(bf16[256,768]{1,0:T(8,128)(2,1)} %x0_ref.2), channel_id=1, source_target_pairs={{0,1},{1,0},{2,3},{3,2},{4,5},{5,4},{6,7},{7,6}} | collective-permute-start | bytes 1179656 | tf_op jit(solution)/shard_map/ppermute | solution.py:555
  29.1 10.7 %collective-permute-start.2 = (bf16[256,768]{1,0:T(8,128)(2,1)S(1)}, bf16[256,768]{1,0:T(8,128)(2,1)S(1)}, u32[]{:S(2)}, u32[]{:S(2)}) collective-permute-start(bf16[256,768]{1,0:T(8,128)(2,1)S(1)} %collective-permute-done.1.x2_ref), channel_id=1, source_target_pairs={{0,1},{1,0},{2,3},{3,2},{4,5},{5,4},{6,7},{7,6}} | collective-permute-start | bytes 1179656 | tf_op jit(solution)/shard_map/ppermute | solution.py:555
  30.0 116.4 %collective-permute-start.9 = (f32[256,768]{1,0:T(8,128)}, f32[256,768]{1,0:T(8,128)}, u32[]{:S(2)}, u32[]{:S(2)}) collective-permute-start(f32[256,768]{1,0:T(8,128)} %x0_ref.3), channel_id=1, source_target_pairs={{0,1},{1,0},{2,3},{3,2},{4,5},{5,4},{6,7},{7,6}} | collective-permute-start | bytes 2359304 | tf_op jit(solution)/shard_map/ppermute | solution.py:555
  32.0 8.5 %copy-start.21 = (bf16[256,768]{1,0:T(8,128)(2,1)S(1)}, bf16[256,768]{1,0:T(8,128)(2,1)}, u32[]{:S(2)}) copy-start(bf16[256,768]{1,0:T(8,128)(2,1)} %x0_ref.2) | copy-start | bytes 1179652
  39.3 107.1 %collective-permute-start.11 = (f32[256,768]{1,0:T(8,128)}, f32[256,768]{1,0:T(8,128)}, u32[]{:S(2)}, u32[]{:S(2)}) collective-permute-start(f32[256,768]{1,0:T(8,128)} %collective-permute-done.10.x2_ref), channel_id=1, source_target_pairs={{0,1},{1,0},{2,3},{3,2},{4,5},{5,4},{6,7},{7,6}} | collective-permute-start | bytes 2359304 | tf_op jit(solution)/shard_map/ppermute | solution.py:555
  81.8 16.5 %copy-start.43 = (f32[2,72,512]{2,1,0:T(8,128)S(1)}, f32[2,72,512]{2,1,0:T(8,128)}, u32[]{:S(2)}) copy-start(f32[2,72,512]{2,1,0:T(8,128)} %attn_fwd.6) | copy-start | bytes 884740
  98.3 11.6 %copy-start.41 = (f32[2,72,1024]{2,1,0:T(8,128)S(1)}, f32[2,72,1024]{2,1,0:T(8,128)}, u32[]{:S(2)}) copy-start(f32[2,72,1024]{2,1,0:T(8,128)} %attn_fwd.5) | copy-start | bytes 1769476
  98.3 11.6 %collective-permute-start.6 = (f32[2,72,512]{2,1,0:T(8,128)S(1)}, f32[2,72,512]{2,1,0:T(8,128)}, u32[]{:S(2)}, u32[]{:S(2)}) collective-permute-start(f32[2,72,512]{2,1,0:T(8,128)S(1)} %copy-done.43), channel_id=1, source_target_pairs={{0,2},{1,3},{2,0},{3,1},{4,6},{5,7},{6,4},{7,5}} | collective-permute-start | bytes 884744 | tf_op jit(solution)/shard_map/ppermute | solution.py:558
  108.4 34.7 %copy-start.42 = (f32[2,72,1024]{2,1,0:T(8,128)S(1)}, f32[2,72,1024]{2,1,0:T(8,128)}, u32[]{:S(2)}) copy-start(f32[2,72,1024]{2,1,0:T(8,128)} %attn_fwd.4) | copy-start | bytes 1769476
  108.4 8.8 %collective-permute-start.7 = (f32[2,72,512]{2,1,0:T(8,128)}, f32[2,72,512]{2,1,0:T(8,128)S(1)}, u32[]{:S(2)}, u32[]{:S(2)}) collective-permute-start(f32[2,72,512]{2,1,0:T(8,128)} %attn_fwd.7), channel_id=1, source_target_pairs={{0,2},{1,3},{2,0},{3,1},{4,6},{5,7},{6,4},{7,5}} | collective-permute-start | bytes 884744 | tf_op jit(solution)/shard_map/ppermute | solution.py:558
  108.4 21.4 %collective-permute-start.4 = (f32[2,72,1024]{2,1,0:T(8,128)}, f32[2,72,1024]{2,1,0:T(8,128)S(1)}, u32[]{:S(2)}, u32[]{:S(2)}) collective-permute-start(f32[2,72,1024]{2,1,0:T(8,128)} %attn_fwd.4), channel_id=1, source_target_pairs={{0,2},{1,3},{2,0},{3,1},{4,6},{5,7},{6,4},{7,5}} | collective-permute-start | bytes 1769480 | tf_op jit(solution)/shard_map/ppermute | solution.py:558
  109.9 32.6 %collective-permute-start.5 = (f32[2,72,1024]{2,1,0:T(8,128)S(1)}, f32[2,72,1024]{2,1,0:T(8,128)S(1)}, u32[]{:S(2)}, u32[]{:S(2)}) collective-permute-start(f32[2,72,1024]{2,1,0:T(8,128)S(1)} %copy-done.41), channel_id=1, source_target_pairs={{0,2},{1,3},{2,0},{3,1},{4,6},{5,7},{6,4},{7,5}} | collective-permute-start | bytes 1769480 | tf_op jit(solution)/shard_map/ppermute | solution.py:558
  119.7 23.7 %copy-start.32 = (f32[2,64,512]{2,1,0:T(8,128)}, f32[2,64,512]{2,1,0:T(8,128)S(1)}, u32[]{:S(2)}) copy-start(f32[2,64,512]{2,1,0:T(8,128)S(1)} %fusion.26) | copy-start | bytes 786436
  120.9 22.7 %copy-start.34 = (f32[2,64,512]{2,1,0:T(8,128)}, f32[2,64,512]{2,1,0:T(8,128)S(1)}, u32[]{:S(2)}) copy-start(f32[2,64,512]{2,1,0:T(8,128)S(1)} %fusion.24) | copy-start | bytes 786436
  144.2 7.6 %collective-permute-start.8 = (bf16[384,1024]{1,0:T(8,128)(2,1)S(1)}, bf16[384,1024]{1,0:T(8,128)(2,1)}, u32[]{:S(2)}, u32[]{:S(2)}) collective-permute-start(bf16[384,1024]{1,0:T(8,128)(2,1)S(1)} %bitcast.91), channel_id=1, source_target_pairs={{0,1},{1,0},{2,3},{3,2},{4,5},{5,4},{6,7},{7,6}} | collective-permute-start | bytes 2359304 | tf_op jit(solution)/shard_map/ppermute | solution.py:555
  147.5 2.5 copy-start.44
  147.5 2.5 copy-start.45
  147.5 2.5 copy-start.46
  155.2 41.8 %copy-start.31 = (f32[2,64,1024]{2,1,0:T(8,128)S(1)}, f32[2,64,1024]{2,1,0:T(8,128)}, u32[]{:S(2)}) copy-start(f32[2,64,1024]{2,1,0:T(8,128)} %copy-done.30) | copy-start | bytes 1572868
  155.2 41.8 %copy-start.33 = (f32[2,64,512]{2,1,0:T(8,128)S(1)}, f32[2,64,512]{2,1,0:T(8,128)}, u32[]{:S(2)}) copy-start(f32[2,64,512]{2,1,0:T(8,128)} %copy-done.32) | copy-start | bytes 786436
  155.2 41.8 %copy-start.35 = (f32[2,64,512]{2,1,0:T(8,128)S(1)}, f32[2,64,512]{2,1,0:T(8,128)}, u32[]{:S(2)}) copy-start(f32[2,64,512]{2,1,0:T(8,128)} %copy-done.34) | copy-start | bytes 786436
  194.5 2.5 copy-start.29
  194.6 2.9 copy-start.16
  194.6 2.9 copy-start.26
  197.0 2.0 copy-start.15
  197.0 2.0 copy-start.24
  197.0 2.0 copy-start.27
  198.9 1.9 copy-start.17
  200.8 25.1 %copy-start.48 = (bf16[2048,768]{1,0:T(8,128)(2,1)S(1)}, bf16[2048,768]{1,0:T(8,128)(2,1)}, u32[]{:S(2)}) copy-start(bf16[2048,768]{1,0:T(8,128)(2,1)} %m_ref.1) | copy-start | bytes 9437188
  225.9 4.0 %copy-start.5 = (bf16[2,256,2048]{2,1,0:T(8,128)(2,1)}, bf16[2,256,2048]{2,1,0:T(8,128)(2,1)S(1)}, u32[]{:S(2)}) copy-start(bf16[2,256,2048]{2,1,0:T(8,128)(2,1)S(1)} %get-tuple-element.58.a0_ref) | copy-start | bytes 6291460
  229.8 27.9 %copy-start.36 = (f32[256,768]{1,0:T(8,128)}, f32[256,768]{1,0:T(8,128)S(1)}, u32[]{:S(2)}) copy-start(f32[256,768]{1,0:T(8,128)S(1)} %convolution_add_fusion.2) | copy-start | bytes 2359300
  229.8 73.6 %collective-permute-start.19 = (f32[256,768]{1,0:T(8,128)S(1)}, f32[256,768]{1,0:T(8,128)}, u32[]{:S(2)}, u32[]{:S(2)}) collective-permute-start(f32[256,768]{1,0:T(8,128)S(1)} %convolution_add_fusion.2), channel_id=1, source_target_pairs={{0,2},{1,3},{2,0},{3,1},{4,6},{5,7},{6,4},{7,5}} | collective-permute-start | bytes 2359304 | tf_op jit(solution)/shard_map/ppermute | solution.py:558
  231.1 64.4 %collective-permute-start.12 = (f32[2,64,1024]{2,1,0:T(8,128)S(1)}, f32[2,64,1024]{2,1,0:T(8,128)S(1)}, u32[]{:S(2)}, u32[]{:S(2)}) collective-permute-start(f32[2,64,1024]{2,1,0:T(8,128)S(1)} %get-tuple-element.57), channel_id=1, source_target_pairs={{0,2},{1,3},{2,0},{3,1},{4,6},{5,7},{6,4},{7,5}} | collective-permute-start | bytes 1572872 | tf_op jit(solution)/shard_map/ppermute | solution.py:558
  257.7 36.7 %copy-start.7 = (bf16[2,256,2048]{2,1,0:T(8,128)(2,1)}, bf16[2,256,2048]{2,1,0:T(8,128)(2,1)S(1)}, u32[]{:S(2)}) copy-start(bf16[2,256,2048]{2,1,0:T(8,128)(2,1)S(1)} %get-tuple-element.61.a1_ref) | copy-start | bytes 6291460
  257.7 38.0 %collective-permute-start.13 = (f32[2,64,1024]{2,1,0:T(8,128)S(1)}, f32[2,64,1024]{2,1,0:T(8,128)S(1)}, u32[]{:S(2)}, u32[]{:S(2)}) collective-permute-start(f32[2,64,1024]{2,1,0:T(8,128)S(1)} %get-tuple-element.60), channel_id=1, source_target_pairs={{0,2},{1,3},{2,0},{3,1},{4,6},{5,7},{6,4},{7,5}} | collective-permute-start | bytes 1572872 | tf_op jit(solution)/shard_map/ppermute | solution.py:558
  287.9 5.4 %copy-start.9 = (bf16[2,256,2048]{2,1,0:T(8,128)(2,1)}, bf16[2,256,2048]{2,1,0:T(8,128)(2,1)S(1)}, u32[]{:S(2)}) copy-start(bf16[2,256,2048]{2,1,0:T(8,128)(2,1)S(1)} %get-tuple-element.67.a2_ref) | copy-start | bytes 6291460
  287.9 12.9 %collective-permute-start.14 = (f32[2,64,1024]{2,1,0:T(8,128)S(1)}, f32[2,64,1024]{2,1,0:T(8,128)S(1)}, u32[]{:S(2)}, u32[]{:S(2)}) collective-permute-start(f32[2,64,1024]{2,1,0:T(8,128)S(1)} %get-tuple-element.63), channel_id=1, source_target_pairs={{0,2},{1,3},{2,0},{3,1},{4,6},{5,7},{6,4},{7,5}} | collective-permute-start | bytes 1572872 | tf_op jit(solution)/shard_map/ppermute | solution.py:558
  291.8 3.7 copy-start.37
  291.8 25.8 %collective-permute-start.21 = (f32[256,768]{1,0:T(8,128)S(1)}, f32[256,768]{1,0:T(8,128)S(1)}, u32[]{:S(2)}, u32[]{:S(2)}) collective-permute-start(f32[256,768]{1,0:T(8,128)S(1)} %convolution_add_fusion), channel_id=1, source_target_pairs={{0,2},{1,3},{2,0},{3,1},{4,6},{5,7},{6,4},{7,5}} | collective-permute-start | bytes 2359304 | tf_op jit(solution)/shard_map/ppermute | solution.py:558
  295.5 50.6 %collective-permute-start.20 = (f32[256,768]{1,0:T(8,128)}, f32[256,768]{1,0:T(8,128)}, u32[]{:S(2)}, u32[]{:S(2)}) collective-permute-start(f32[256,768]{1,0:T(8,128)} %convolution_add_fusion.1), channel_id=1, source_target_pairs={{0,2},{1,3},{2,0},{3,1},{4,6},{5,7},{6,4},{7,5}} | collective-permute-start | bytes 2359304 | tf_op jit(solution)/shard_map/ppermute | solution.py:558
  295.7 52.8 %collective-permute-start.16 = (bf16[256,2048]{1,0:T(8,128)(2,1)}, bf16[256,2048]{1,0:T(8,128)(2,1)}, u32[]{:S(2)}, u32[]{:S(2)}) collective-permute-start(bf16[256,2048]{1,0:T(8,128)(2,1)} %slice_bitcast_fusion.2), channel_id=1, source_target_pairs={{0,1},{1,0},{2,3},{3,2},{4,5},{5,4},{6,7},{7,6}} | collective-permute-start | bytes 3145736 | tf_op jit(solution)/shard_map/ppermute | solution.py:555
  300.8 48.3 %collective-permute-start.17 = (bf16[256,2048]{1,0:T(8,128)(2,1)}, bf16[256,2048]{1,0:T(8,128)(2,1)}, u32[]{:S(2)}, u32[]{:S(2)}) collective-permute-start(bf16[256,2048]{1,0:T(8,128)(2,1)} %slice_bitcast_fusion.1), channel_id=1, source_target_pairs={{0,1},{1,0},{2,3},{3,2},{4,5},{5,4},{6,7},{7,6}} | collective-permute-start | bytes 3145736 | tf_op jit(solution)/shard_map/ppermute | solution.py:555
  303.5 49.7 %collective-permute-start.18 = (bf16[256,2048]{1,0:T(8,128)(2,1)}, bf16[256,2048]{1,0:T(8,128)(2,1)}, u32[]{:S(2)}, u32[]{:S(2)}) collective-permute-start(bf16[256,2048]{1,0:T(8,128)(2,1)} %slice_bitcast_fusion), channel_id=1, source_target_pairs={{0,1},{1,0},{2,3},{3,2},{4,5},{5,4},{6,7},{7,6}} | collective-permute-start | bytes 3145736 | tf_op jit(solution)/shard_map/ppermute | solution.py:555
  318.6 43.3 %collective-permute-start.15 = (bf16[384,1024]{1,0:T(8,128)(2,1)S(1)}, bf16[384,1024]{1,0:T(8,128)(2,1)}, u32[]{:S(2)}, u32[]{:S(2)}) collective-permute-start(bf16[384,1024]{1,0:T(8,128)(2,1)S(1)} %bitcast.102), channel_id=1, source_target_pairs={{0,1},{1,0},{2,3},{3,2},{4,5},{5,4},{6,7},{7,6}} | collective-permute-start | bytes 2359304 | tf_op jit(solution)/shard_map/ppermute | solution.py:555
  321.0 20.9 %copy-start.47 = (f32[1,768]{1,0:T(1,128)S(1)}, f32[1,768]{1,0:T(1,128)}, u32[]{:S(2)}) copy-start(f32[1,768]{1,0:T(1,128)} %get-tuple-element.72) | copy-start | bytes 9220
  342.5 2.5 copy-start.38
  342.5 2.5 copy-start.40
  345.0 4.1 %copy-start.2 = (bf16[1024,768]{1,0:T(8,128)(2,1)S(1)}, bf16[1024,768]{1,0:T(8,128)(2,1)}, u32[]{:S(2)}) copy-start(bf16[1024,768]{1,0:T(8,128)(2,1)} %get-tuple-element.54.dh_ref) | copy-start | bytes 4718596
  345.0 8.2 %copy-start.12 = (bf16[768,12,64]{0,2,1:T(8,128)(2,1)S(1)}, bf16[768,12,64]{0,2,1:T(8,128)(2,1)}, u32[]{:S(2)}) copy-start(bf16[768,12,64]{0,2,1:T(8,128)(2,1)} %param.20) | copy-start | bytes 3538948
  346.0 23.5 %collective-permute-start.22 = (f32[256,768]{1,0:T(8,128)}, f32[256,768]{1,0:T(8,128)}, u32[]{:S(2)}, u32[]{:S(2)}) collective-permute-start(f32[256,768]{1,0:T(8,128)} %add.96.a0_ref), channel_id=1, source_target_pairs={{0,1},{1,0},{2,3},{3,2},{4,5},{5,4},{6,7},{7,6}} | collective-permute-start | bytes 2359304 | tf_op jit(solution)/shard_map/ppermute | solution.py:555
  346.1 7.1 %copy-start.10 = (bf16[2,256,2048]{2,1,0:T(8,128)(2,1)S(1)}, bf16[2,256,2048]{2,1,0:T(8,128)(2,1)}, u32[]{:S(2)}) copy-start(bf16[2,256,2048]{2,1,0:T(8,128)(2,1)} %copy-done.9) | copy-start | bytes 6291460
  348.5 4.7 %copy-start.6 = (bf16[2,256,2048]{2,1,0:T(8,128)(2,1)S(1)}, bf16[2,256,2048]{2,1,0:T(8,128)(2,1)}, u32[]{:S(2)}) copy-start(bf16[2,256,2048]{2,1,0:T(8,128)(2,1)} %copy-done.5) | copy-start | bytes 6291460
  348.5 4.7 %copy-start.8 = (bf16[2,256,2048]{2,1,0:T(8,128)(2,1)S(1)}, bf16[2,256,2048]{2,1,0:T(8,128)(2,1)}, u32[]{:S(2)}) copy-start(bf16[2,256,2048]{2,1,0:T(8,128)(2,1)} %copy-done.7) | copy-start | bytes 6291460
  348.5 4.7 %copy-start.11 = (bf16[768,12,64]{0,2,1:T(8,128)(2,1)S(1)}, bf16[768,12,64]{0,2,1:T(8,128)(2,1)}, u32[]{:S(2)}) copy-start(bf16[768,12,64]{0,2,1:T(8,128)(2,1)} %param.19) | copy-start | bytes 3538948
  348.6 21.0 %collective-permute-start.24 = (f32[256,768]{1,0:T(8,128)}, f32[256,768]{1,0:T(8,128)}, u32[]{:S(2)}, u32[]{:S(2)}) collective-permute-start(f32[256,768]{1,0:T(8,128)} %add.99.a2_ref), channel_id=1, source_target_pairs={{0,1},{1,0},{2,3},{3,2},{4,5},{5,4},{6,7},{7,6}} | collective-permute-start | bytes 2359304 | tf_op jit(solution)/shard_map/ppermute | solution.py:555
  349.1 20.5 %collective-permute-start.23 = (f32[256,768]{1,0:T(8,128)}, f32[256,768]{1,0:T(8,128)}, u32[]{:S(2)}, u32[]{:S(2)}) collective-permute-start(f32[256,768]{1,0:T(8,128)} %add.97.a1_ref), channel_id=1, source_target_pairs={{0,1},{1,0},{2,3},{3,2},{4,5},{5,4},{6,7},{7,6}} | collective-permute-start | bytes 2359304 | tf_op jit(solution)/shard_map/ppermute | solution.py:555
  353.2 8.7 %copy-start.4 = (bf16[768,12,64]{0,2,1:T(8,128)(2,1)S(1)}, bf16[768,12,64]{0,2,1:T(8,128)(2,1)}, u32[]{:S(2)}) copy-start(bf16[768,12,64]{0,2,1:T(8,128)(2,1)} %param.18) | copy-start | bytes 3538948
  353.2 8.7 %copy-start.14 = (f32[1024,768]{1,0:T(8,128)S(1)}, f32[1024,768]{1,0:T(8,128)}, u32[]{:S(2)}) copy-start(f32[1024,768]{1,0:T(8,128)} %get-tuple-element.65.dh_ref) | copy-start | bytes 9437188
  353.2 8.7 %copy-start.19 = (bf16[1024,768]{1,0:T(8,128)(2,1)S(1)}, bf16[1024,768]{1,0:T(8,128)(2,1)}, u32[]{:S(2)}) copy-start(bf16[1024,768]{1,0:T(8,128)(2,1)} %copy-done.18) | copy-start | bytes 4718596
  369.0 6.1 %copy-start.1 = (bf16[12,64,768]{2,1,0:T(8,128)(2,1)S(1)}, bf16[12,64,768]{2,1,0:T(8,128)(2,1)}, u32[]{:S(2)}) copy-start(bf16[12,64,768]{2,1,0:T(8,128)(2,1)} %param.21) | copy-start | bytes 3538948
  (10 other events, 10.5 us)
where the time goes:
time: 381 us; the launch traced here: 376 us
  Pallas kernels  234 us (61%)
  waiting for transfers between devices  70.2 us (18%)
  matrix products  19.3 us (5%)
  local copies, waits for them, and re-layouts  16.8 us (4%)
  starting transfers between devices  16.2 us (4%)
  other arithmetic  16.2 us (4%)
    pallas_call x3, Pallas kernels, attention_backward(): pl.pallas_call(bwd_kernel, out_shape=[jax.ShapeDtypeStruct((2, 2 * PAIR,...  75.7 us
    ppermute x12, waiting for transfers between devices, to_far(): return lax.ppermute(a, 'seq', far)  70.1 us
    pallas_call x4, Pallas kernels, attention_forward(): pl.pallas_call(fwd_kernel, out_shape=jax.ShapeDtypeStruct((2 * pairs, ORO...  52.8 us
    pallas_call x1, Pallas kernels, mlp(): pl.pallas_call(mlp_kernel, grid=(ff // FFB,), in_specs=[fix(rows, dim), f...  39.3 us
    pallas_call x1, Pallas kernels, mlp_weights(): pl.pallas_call(mlp_weights_kernel, grid=(ff // FFB,), in_specs=[fix(dim,...  20.9 us
    dot_general x9, matrix products, mm(): lax.dot_general(a, b, (((ca,), (cb,)), ((), ())), preferred_element_type=...  19.3 us
    pallas_call x2, Pallas kernels, project(): pl.pallas_call(proj_kernel, out_shape=outs, grid_spec=pltpu.PrefetchScala...  14.4 us
    unnamed x106, local copies, waits for them, and re-layouts  11.4 us
  transfers between devices with their start and end apart: 25, of which 6 were waited for; matrix products, arithmetic and copies ran while one was open for 8% of the time, Pallas kernels for 44%

commit v1 on v0

--- a/solution.py
+++ b/solution.py
@@ -103,8 +103,8 @@
     )(place, *parts, gain, wqt)
 
 
-def place_kernel(place_ref, x0_ref, x1_ref, x2_ref, x3_ref, o_ref):
-    for part, src in enumerate((x0_ref, x1_ref, x2_ref, x3_ref)):
+def place_kernel(place_ref, x0_ref, x1_ref, o_ref):
+    for part, src in enumerate((x0_ref, x1_ref)):
         @pl.when(pl.program_id(0) == part)
         def _():
             o_ref[...] = src[...]
@@ -119,7 +119,7 @@
         grid_spec=pltpu.PrefetchScalarGridSpec(
             num_scalar_prefetch=1, grid=(n,),
             in_specs=[pl.BlockSpec((rows, dim), lambda i, s: (0, 0))] * n,
-            out_specs=pl.BlockSpec((rows, dim), lambda i, s: (s[i], 0))),
+            out_specs=pl.BlockSpec((rows, dim), lambda i, s: (s[2 * i], 0))),
         compiler_params=pltpu.CompilerParams(vmem_limit_bytes=16 << 20),
         cost_estimate=cost(n * rows * dim, 6 << 20),
         name="place_rows",
@@ -305,7 +305,7 @@
                n2t_ref, gt_ref, dgate_ref, dup_ref, ut_ref, dh_ref, dhb_ref, gn_ref, n2_ref, acc_ref):
     step = pl.program_id(0)
     rows = h_ref.shape[0]
-    chunk = 512
+    chunk = 256
 
     @pl.when(step == 0)
     def _():
@@ -374,28 +374,30 @@
     )(hidden, g_all, gain, w_gate, w_up, w_down)
 
 
-def mlp_weights_kernel(n2t_ref, gt_ref, dgate_ref, dup_ref, ut_ref, g1_ref, g3_ref, g2_ref):
-    g1_ref[...] = dot(n2t_ref[...], dgate_ref[...])
-    g3_ref[...] = dot(n2t_ref[...], dup_ref[...])
-    g2_ref[...] = dot(ut_ref[...], gt_ref[...])
-
-
-def mlp_weights(n2t, g_top, d_gate, d_up, act_t):
-    dim, rows = n2t.shape
-    ff = d_gate.shape[1]
+def mlp_weights_kernel(n2t_ref, gt_ref, dgate_ref, dup_ref, ut_ref, n2t2_ref, gt2_ref, dgate2_ref, dup2_ref, ut2_ref,
+                       g1_ref, g3_ref, g2_ref):
+    g1_ref[...] = dot(n2t_ref[...], dgate_ref[...]) + dot(n2t2_ref[...], dgate2_ref[...])
+    g3_ref[...] = dot(n2t_ref[...], dup_ref[...]) + dot(n2t2_ref[...], dup2_ref[...])
+    g2_ref[...] = dot(ut_ref[...], gt_ref[...]) + dot(ut2_ref[...], gt2_ref[...])
+
+
+def mlp_weights(factors, factors_near):
+    dim, rows = factors[0].shape
+    ff = factors[2].shape[1]
     fix = lambda *shape: pl.BlockSpec(shape, lambda i: (0,) * len(shape))
     act = pl.BlockSpec((rows, FFB), lambda i: (0, i))
     wide = pl.BlockSpec((dim, FFB), lambda i: (0, i))
+    ins = [fix(dim, rows), fix(rows, dim), act, act, pl.BlockSpec((FFB, rows), lambda i: (i, 0))]
     return pl.pallas_call(
         mlp_weights_kernel,
         grid=(ff // FFB,),
-        in_specs=[fix(dim, rows), fix(rows, dim), act, act, pl.BlockSpec((FFB, rows), lambda i: (i, 0))],
+        in_specs=ins + ins,
         out_specs=[wide, wide, pl.BlockSpec((FFB, dim), lambda i: (i, 0))],
         out_shape=[jax.ShapeDtypeStruct((dim, ff), F32)] * 2 + [jax.ShapeDtypeStruct((ff, dim), F32)],
         compiler_params=pltpu.CompilerParams(vmem_limit_bytes=60 << 20),
-        cost_estimate=cost(6 * rows * dim * ff, 50 << 20),
+        cost_estimate=cost(12 * rows * dim * ff, 50 << 20),
         name="mlp_weights",
-    )(n2t, g_top, d_gate, d_up, act_t)
+    )(*factors, *factors_near)
 
 
 def memory_kernel(core_ref, a0_ref, a1_ref, a2_ref, b0_ref, b1_ref, b2_ref, wk_ref, wv_ref, o_ref):
@@ -432,39 +434,51 @@
     return i + core - 2 * i * core
 
 
-def out_proj_kernel(core_ref, mine_ref, near_ref, dh_ref, o_ref):
-    for who, ref in enumerate((mine_ref, near_ref)):
-        @pl.when(pl.program_id(0) == who)
-        def _():
-            o_ref[...] = dot(ref[...], dh_ref[...])
+def out_proj_kernel(core_ref, mine_ref, near0_ref, near1_ref, dh_ref, o_ref):
+    half = near0_ref.shape[1]
+
+    @pl.when(pl.program_id(0) == 0)
+    def _():
+        o_ref[...] = dot(mine_ref[...], dh_ref[...])
+
+    @pl.when(pl.program_id(0) == 1)
+    def _():
+        o_ref[...] = dot(near0_ref[...], dh_ref[:half, :]) + dot(near1_ref[...], dh_ref[half:, :])
 
 
 def out_proj_grad(core, mine, near, dh):
     width, rows = mine.shape
     dim = dh.shape[1]
     whole = pl.BlockSpec((width, rows), lambda i, s: (0, 0))
+    part = pl.BlockSpec((width, rows // 2), lambda i, s: (0, 0))
     return pl.pallas_call(
         out_proj_kernel,
         out_shape=jax.ShapeDtypeStruct((2 * width, dim), F32),
         grid_spec=pltpu.PrefetchScalarGridSpec(
             num_scalar_prefetch=1, grid=(2,),
-            in_specs=[whole, whole, pl.BlockSpec((rows, dim), lambda i, s: (0, 0))],
+            in_specs=[whole, part, part, pl.BlockSpec((rows, dim), lambda i, s: (0, 0))],
             out_specs=pl.BlockSpec((width, dim), lambda i, s: (half_index(i, s[0]), 0))),
         compiler_params=pltpu.CompilerParams(vmem_limit_bytes=24 << 20),
         cost_estimate=cost(4 * rows * dim * width, 6 << 20),
         name="out_proj_grad",
-    )(core, mine, near, dh)
+    )(core, mine, *near, dh)
 
 
 def query_grad_kernel(place_ref, mine_ref, near_ref, n1_ref, wq_ref, x_ref, dh_ref, gain_ref,
                       gw_ref, gx_ref, gn_ref, acc_ref):
-    for who, ref in enumerate((mine_ref, near_ref)):
-        @pl.when(pl.program_id(0) == who)
-        def _():
-            dq = ref[...]
-            gw_ref[...] = dot(dq, n1_ref[...])
-            part = dot(dq.T, wq_ref[...])
-            acc_ref[...] = part if who == 0 else acc_ref[...] + part
+    half = acc_ref.shape[0] // 2
+
+    @pl.when(pl.program_id(0) == 0)
+    def _():
+        gw_ref[...] = dot(mine_ref[...], n1_ref[...])
+        acc_ref[...] = dot(mine_ref[...].T, wq_ref[...])
+
+    @pl.when(pl.program_id(0) == 1)
+    def _():
+        first, second = near_ref[:, half:], near_ref[:, :half]
+        gw_ref[...] = dot(first, n1_ref[:half, :]) + dot(second, n1_ref[half:, :])
+        acc_ref[:half, :] += dot(first.T, wq_ref[...])
+        acc_ref[half:, :] += dot(second.T, wq_ref[...])
 
     @pl.when(pl.program_id(0) == 1)
     def _():
@@ -569,7 +583,8 @@
         wqt, wkt, wvt = (w.transpose(1, 2, 0).reshape(heads * head, dim) for w in (wq, wk, wv))
         wo2 = wo.reshape(heads * head, dim)
         lens = jnp.stack([jnp.clip(mem_len[0] - i * m_rows, 0, m_rows) for i in (dev, dev ^ 1)]).astype(jnp.int32)
-        place = jnp.stack([dev, dev ^ 1, dev ^ 2, dev ^ 3, core]).astype(jnp.int32)
+        chip = dev // 2
+        place = jnp.stack([chip, 2 + chip, 1 - chip, 3 - chip, core]).astype(jnp.int32)
         gain1 = norm_attn.astype(F32).reshape(1, dim)
         gain2 = norm_mlp.astype(F32).reshape(1, dim)
 
@@ -580,7 +595,7 @@
 
         x_parts = gather_parts(dec_in)
         mem_near = to_near(memory)
-        g_parts = gather_parts(grad_out)
+        g_parts = (grad_out, to_far(grad_out))
 
         first = project(core1, memory, wkt, wvt, 0, ())
         x_all_b, n1, _, qt_s = queries(place, x_parts, gain1, wqt)
@@ -603,20 +618,27 @@
             lses.append(top + jnp.log(den))
         outs[-2:] = [jnp.concatenate(outs[-2:], axis=2)]
         lses[-2:] = [jnp.concatenate(lses[-2:], axis=2)]
-        g_all = place_rows(place, g_parts)
+        g_half = place_rows(place, g_parts)
         o_t = jnp.concatenate(outs, axis=0)
         lse = jnp.concatenate(lses, axis=0)
         o_t_b = o_t.astype(BF).reshape(width, n * rows)
-        o_t_near = to_near(o_t_b)
+        half = n * rows // 2
+        o_t_first, o_t_second = o_t_b[:, :half], o_t_b[:, half:]
+        o_near_first = to_near(o_t_second)
 
         def half_rows(w, who):
             return lax.dynamic_slice(w, (who * width, 0), (width, dim))
 
         wo_m, wo_n = half_rows(wo2, core), half_rows(wo2, 1 - core)
-        x_all = x_all_b.astype(F32)
-        hidden = (x_all + mm(o_t_b, wo_m, 0, 0) + mm(o_t_near, wo_n, 0, 0)).astype(BF)
-
-        n2t, g_top, d_gate, d_up, act_t, d_hid, d_hid_b, g_norm_mlp = mlp(hidden, g_all, gain2, w_gate, w_up, w_down)
+        hidden = (x_all_b[:half].astype(F32) + mm(o_t_first, wo_m, 0, 0) + mm(o_near_first, wo_n, 0, 0)).astype(BF)
+
+        n2t, g_top, d_gate, d_up, act_t, d_hid, d_hid_half, g_norm_half = mlp(
+            hidden, g_half, gain2, w_gate, w_up, w_down)
+        d_hid_b = jnp.concatenate([d_hid_half, to_near(d_hid_half)], axis=0)
+        factors = (n2t, g_top, d_gate, d_up, act_t)
+        factors_near = tuple(to_near(a) for a in factors)
+        o_near_second = to_near(o_t_first)
+        g_norm_mlp = g_norm_half + to_near(g_norm_half)
 
         do_t_f = mm(wo_m, d_hid_b, 1, 1)
         delta = jnp.sum(do_t_f.reshape(mine, head, n * rows) * o_t, axis=1, keepdims=True)
@@ -632,14 +654,15 @@
             dkvs_near.append(to_near(dkv[1]))
             lens_now, dw_last = lax.optimization_barrier((lens, dw))
 
-        d_gate, _ = lax.optimization_barrier((d_gate, dw_last))
-        g_gate, g_up, g_down = mlp_weights(n2t, g_top, d_gate, d_up, act_t)
+        act_t, _ = lax.optimization_barrier((act_t, dw_last))
+        factors = (n2t, g_top, d_gate, d_up, act_t)
+        g_gate, g_up, g_down = mlp_weights(factors, factors_near)
         g_mem = memory_grad(core1, dkvs, dkvs_near, wkt, wvt)
 
         def as_weight(rows_by_dim):
             return rows_by_dim.reshape(heads, head, dim).transpose(2, 0, 1)
 
-        g_wo = out_proj_grad(core1, o_t_b, o_t_near, d_hid_b).reshape(heads, head, dim)
+        g_wo = out_proj_grad(core1, o_t_b, (o_near_first, o_near_second), d_hid_b).reshape(heads, head, dim)
 
         dqt_b = (jnp.concatenate([a + b for a, b in dqs], axis=0) * (head ** -0.5)).astype(BF).reshape(width, n * rows)
         dqt_near = to_near(dqt_b)

time: 381 us -> 385 us (1.010)
  waiting for transfers between devices: 70.2 us -> 104 us
  Pallas kernels: 234 us -> 210 us
  other arithmetic: 16.2 us -> 8.08 us
    ppermute x12, waiting for transfers between devices: 70.1 us -> 89.1 us  [to_far(): return lax.ppermute(a, 'seq', far)]
    pallas_call x1, Pallas kernels: 39.3 us -> 21.7 us  [mlp(): pl.pallas_call(mlp_kernel, grid=(ff // FFB,), in_specs=[fix(rows, dim), f...]
    ppermute x13 -> x19, waiting for transfers between devices: 0.03 us -> 14.5 us  [to_near(): return lax.ppermute(a, 'seq', near)]
    add x3, other arithmetic: 5.97 us -> 0.29 us  [device_work(): dw_mine.append(a + b)]
    unnamed x106 -> x99, local copies, waits for them, and re-layouts: 11.4 us -> 13.3 us
    ppermute x13 -> x19, starting transfers between devices: 10.2 us -> 10.6 us  [to_near(): return lax.ppermute(a, 'seq', near)]
  transfers between devices with their start and end apart: 25 -> 31, of which waited for: 6 -> 11; matrix products, arithmetic and copies ran while one was open for 8% -> 9% of each run, Pallas kernels for 44% -> 44%
where the time goes in v1:
time: 385 us; the launch traced here: 380 us
  Pallas kernels  210 us (55%)
  waiting for transfers between devices  104 us (27%)
  matrix products  21.2 us (6%)
  starting transfers between devices  17.9 us (5%)
  local copies, waits for them, and re-layouts  16.5 us (4%)
  other arithmetic  8.08 us (2%)
    ppermute x12, waiting for transfers between devices, to_far(): return lax.ppermute(a, 'seq', far)  89.1 us
    pallas_call x3, Pallas kernels, attention_backward(): pl.pallas_call(bwd_kernel, out_shape=[jax.ShapeDtypeStruct((2, 2 * PAIR,...  75.6 us
    pallas_call x4, Pallas kernels, attention_forward(): pl.pallas_call(fwd_kernel, out_shape=jax.ShapeDtypeStruct((2 * pairs, ORO...  52.9 us
    pallas_call x1, Pallas kernels, mlp(): pl.pallas_call(mlp_kernel, grid=(ff // FFB,), in_specs=[fix(rows, dim), f...  21.7 us
    pallas_call x1, Pallas kernels, mlp_weights(): pl.pallas_call(mlp_weights_kernel, grid=(ff // FFB,), in_specs=ins + ins,...  21.4 us
    dot_general x9, matrix products, mm(): lax.dot_general(a, b, (((ca,), (cb,)), ((), ())), preferred_element_type=...  21.2 us
    pallas_call x2, Pallas kernels, project(): pl.pallas_call(proj_kernel, out_shape=outs, grid_spec=pltpu.PrefetchScala...  14.5 us
    ppermute x19, waiting for transfers between devices, to_near(): return lax.ppermute(a, 'seq', near)  14.5 us
  transfers between devices with their start and end apart: 31, of which 11 were waited for; matrix products, arithmetic and copies ran while one was open for 9% of the time, Pallas kernels for 44%

profile of v1, /device:TPU:5, one launch (start us, length us, event | category | flops | bytes accessed | tf_op | source)
XLA Modules:
  0.0 379.7 jit_solution(9840486562500887678)
XLA Ops:
  0.7 0.7 collective-permute-start.3
  1.4 1.2 collective-permute-start.1
  2.9 9.3 %collective-permute-done.1.x2_ref = bf16[256,768]{1,0:T(8,128)(2,1)S(1)} collective-permute-done((bf16[256,768]{1,0:T(8,128)(2,1)}, bf16[256,768]{1,0:T(8,128)(2,1)S(1)}, u32[]{:S(2)}, u32[]{:S(2)}) %collective-permute-start.1) | collective-permute-done | bytes 393248 | tf_op jit(solution)/shard_map/ppermute | solution.py:572
  12.2 0.9 collective-permute-start.2
  13.1 1.2 collective-permute-start.9
  15.0 0.7 reshape.90.gain_ref
  16.3 7.3 %kv_proj.2 = (bf16[4096,384]{1,0:T(8,128)(2,1)}, bf16[4096,384]{1,0:T(8,128)(2,1)}, bf16[384,4096]{1,0:T(8,128)(2,1)}, bf16[384,4096]{1,0:T(8,128)(2,1)}) custom-call(s32[1]{0:T(128)} %bitcast.4.core_ref, bf16[2048,768]{1,0:T(8,128)(2,1)} %m_ref.1, bf16[768,768]{1,0:T(8,128)(2,1)} %bitcast.93, bf16[768,768]{1,0:T(8,128)(2,1)} %bitcast.96), custom_call_target="tpu_custom_call" | custom-call | flops 2415919104 | bytes 12582912 | tf_op jit(solution)/shard_map/kv_proj/pallas_call | solution.py:55
  23.6 3.6 queries.1
  27.3 1.1 copy-done.19
  28.4 1.1 copy-done.23
  29.6 0.9 copy-done.25
  30.4 7.2 %kv_proj.3 = (bf16[4096,384]{1,0:T(8,128)(2,1)}, bf16[4096,384]{1,0:T(8,128)(2,1)}, bf16[384,4096]{1,0:T(8,128)(2,1)}, bf16[384,4096]{1,0:T(8,128)(2,1)}) custom-call(s32[1]{0:T(128)} %bitcast.4.core_ref, bf16[2048,768]{1,0:T(8,128)(2,1)} %collective-permute-done.3.m_ref, ...), custom_call_target="tpu_custom_call", output_to_operand_aliasing={{0}: (4, {}), {1}: (5, {}), {2}: (6, {}), {3}: (7, {})} | custom-call | flops 2415919104 | bytes 12582912 | tf_op jit(solution)/shard_map/kv_proj/pallas_call | solution.py:55
  37.6 9.9 %attn_fwd.6 = f32[2,72,512]{2,1,0:T(8,128)} custom-call(s32[2]{0:T(128)} %pad_add_fusion.len_ref, bf16[384,1024]{1,0:T(8,128)(2,1)} %copy-done.25, bf16[4096,384]{1,0:T(8,128)(2,1)} %get-tuple-element.52.k_ref, bf16[384,4096]{1,0:T(8,128)(2,1)} %get-tuple-element.53.vt_ref), custom_call_target="tpu_custom_call" | custom-call | flops 4294967296 | bytes 4194304 | tf_op jit(solution)/shard_map/attn_fwd/pallas_call | solution.py:212
  47.5 16.5 %attn_fwd.5 = f32[2,72,1024]{2,1,0:T(8,128)} custom-call(s32[2]{0:T(128)} %pad_add_fusion.len_ref, bf16[384,1024]{1,0:T(8,128)(2,1)} %copy-done.25, bf16[4096,384]{1,0:T(8,128)(2,1)} %get-tuple-element.52.k_ref, bf16[384,4096]{1,0:T(8,128)(2,1)} %get-tuple-element.53.vt_ref), custom_call_target="tpu_custom_call" | custom-call | flops 8589934592 | bytes 4194304 | tf_op jit(solution)/shard_map/attn_fwd/pallas_call | solution.py:212
  63.9 16.6 %attn_fwd.4 = f32[2,72,1024]{2,1,0:T(8,128)} custom-call(s32[2]{0:T(128)} %pad_add_fusion.len_ref, bf16[384,1024]{1,0:T(8,128)(2,1)} %copy-done.25, bf16[4096,384]{1,0:T(8,128)(2,1)} %get-tuple-element.52.k_ref, bf16[384,4096]{1,0:T(8,128)(2,1)} %get-tuple-element.53.vt_ref), custom_call_target="tpu_custom_call" | custom-call | flops 8589934592 | bytes 4194304 | tf_op jit(solution)/shard_map/attn_fwd/pallas_call | solution.py:212
  80.6 10.0 %attn_fwd.7 = f32[2,72,512]{2,1,0:T(8,128)} custom-call(s32[2]{0:T(128)} %pad_add_fusion.len_ref, bf16[384,1024]{1,0:T(8,128)(2,1)} %copy-done.25, bf16[4096,384]{1,0:T(8,128)(2,1)} %get-tuple-element.52.k_ref, bf16[384,4096]{1,0:T(8,128)(2,1)} %get-tuple-element.53.vt_ref), custom_call_target="tpu_custom_call" | custom-call | flops 4294967296 | bytes 4194304 | tf_op jit(solution)/shard_map/attn_fwd/pallas_call | solution.py:212
  90.6 1.5 collective-permute-start.4
  92.7 6.3 %collective-permute-done.7 = f32[2,72,512]{2,1,0:T(8,128)S(1)} collective-permute-done((f32[2,72,512]{2,1,0:T(8,128)}, f32[2,72,512]{2,1,0:T(8,128)S(1)}, u32[]{:S(2)}, u32[]{:S(2)}) %collective-permute-start.7) | collective-permute-done | bytes 294944 | tf_op jit(solution)/shard_map/ppermute | solution.py:572
  99.1 1.5 log_add_fusion.2
  100.6 1.1 fusion.24
  101.7 10.0 %collective-permute-done.4 = f32[2,72,1024]{2,1,0:T(8,128)S(1)} collective-permute-done((f32[2,72,1024]{2,1,0:T(8,128)S(1)}, f32[2,72,1024]{2,1,0:T(8,128)S(1)}, u32[]{:S(2)}, u32[]{:S(2)}) %collective-permute-start.4) | collective-permute-done | bytes 589856 | tf_op jit(solution)/shard_map/ppermute | solution.py:572
  111.8 12.6 %collective-permute-done.5 = f32[2,72,1024]{2,1,0:T(8,128)S(1)} collective-permute-done((f32[2,72,1024]{2,1,0:T(8,128)S(1)}, f32[2,72,1024]{2,1,0:T(8,128)S(1)}, u32[]{:S(2)}, u32[]{:S(2)}) %collective-permute-start.5) | collective-permute-done | bytes 589856 | tf_op jit(solution)/shard_map/ppermute | solution.py:572
  124.4 0.6 log_add_fusion
  125.4 0.8 fusion.39
  126.2 1.2 collective-permute-start.8
  127.4 1.3 reshape.92.gain_ref
  128.7 1.8 place_rows.1.g_ref
  131.7 1.5 add_convert_fusion.h_ref
  133.2 21.7 %mlp.1 = (bf16[768,512]{1,0:T(8,128)(2,1)}, bf16[512,768]{1,0:T(8,128)(2,1)}, bf16[512,3072]{1,0:T(8,128)(2,1)}, bf16[512,3072]{1,0:T(8,128)(2,1)}, bf16[3072,51...) custom-call(bf16[512,768]{1,0:T(8,128)(2,1)} %add_convert_fusion.h_ref, ...), custom_call_target="tpu_custom_call" | custom-call | flops 12079595520 | bytes 41943040 | tf_op jit(solution)/shard_map/mlp/pallas_call | solution.py:361
  155.6 1.3 constant_dynamic-update-slice_fusion.1
  157.6 0.8 fusion.40
  159.8 1.1 copy-done.4
  160.9 25.4 %attn_bwd.3 = (bf16[2,256,2048]{2,1,0:T(8,128)(2,1)S(1)}, f32[2,64,1024]{2,1,0:T(8,128)S(1)}) custom-call(s32[2]{0:T(128)S(1)} %copy-done.27, bf16[384,1024]{1,0:T(8,128)(2,1)S(1)} %copy-done.26, bf16[384,1024]{1,0:T(8,128)(2,1)S(1)} %get-tuple-element.99.dot_ref, f32[6,1,1024]{2,1,0:T(1,128)S(1)} %maximum_maximum_fusion.1.lse_ref, ...), custom_call_target="tpu_custom_call" | custom-call | flops 16777216000 | bytes 8388608 | tf_op jit(solution)/shard_map/attn_bwd/pallas_call | solution.py:294
  186.3 2.9 fusion.5
  189.4 3.8 convolution_add_fusion.2
  193.1 25.0 %attn_bwd.4 = (bf16[2,256,2048]{2,1,0:T(8,128)(2,1)S(1)}, f32[2,64,1024]{2,1,0:T(8,128)S(1)}) custom-call(s32[2]{0:T(128)S(1)} %copy-done.27, bf16[384,1024]{1,0:T(8,128)(2,1)S(1)} %copy-done.26, bf16[384,1024]{1,0:T(8,128)(2,1)S(1)} %get-tuple-element.99.dot_ref, f32[6,1,1024]{2,1,0:T(1,128)S(1)} %maximum_maximum_fusion.1.lse_ref, ...), custom_call_target="tpu_custom_call" | custom-call | flops 16777216000 | bytes 8388608 | tf_op jit(solution)/shard_map/attn_bwd/pallas_call | solution.py:294
  218.2 2.9 fusion.3
  221.1 2.9 convolution_add_fusion.1
  224.0 25.2 %attn_bwd.5 = (bf16[2,256,2048]{2,1,0:T(8,128)(2,1)S(1)}, f32[2,64,1024]{2,1,0:T(8,128)S(1)}) custom-call(s32[2]{0:T(128)S(1)} %copy-done.27, bf16[384,1024]{1,0:T(8,128)(2,1)S(1)} %copy-done.26, bf16[384,1024]{1,0:T(8,128)(2,1)S(1)} %get-tuple-element.99.dot_ref, f32[6,1,1024]{2,1,0:T(1,128)S(1)} %maximum_maximum_fusion.1.lse_ref, ...), custom_call_target="tpu_custom_call" | custom-call | flops 16777216000 | bytes 8388608 | tf_op jit(solution)/shard_map/attn_bwd/pallas_call | solution.py:294
  249.2 2.9 fusion.1
  252.1 3.0 convolution_add_fusion
  255.0 1.5 collective-permute-start.18
  256.6 0.7 collective-permute-start.15
  257.2 1.7 collective-permute-start.20
  259.0 3.5 collective-permute-done.13
  262.5 1.5 collective-permute-start.16
  264.1 15.3 %collective-permute-done.18 = f32[256,768]{1,0:T(8,128)S(1)} collective-permute-done((f32[256,768]{1,0:T(8,128)S(1)}, f32[256,768]{1,0:T(8,128)S(1)}, u32[]{:S(2)}, u32[]{:S(2)}) %collective-permute-start.18) | collective-permute-done | bytes 786464 | tf_op jit(solution)/shard_map/ppermute | solution.py:572
  279.4 1.5 collective-permute-start.17
  280.9 32.2 %collective-permute-done.20 = f32[256,768]{1,0:T(8,128)S(1)} collective-permute-done((f32[256,768]{1,0:T(8,128)S(1)}, f32[256,768]{1,0:T(8,128)S(1)}, u32[]{:S(2)}, u32[]{:S(2)}) %collective-permute-start.20) | collective-permute-done | bytes 786464 | tf_op jit(solution)/shard_map/ppermute | solution.py:572
  313.1 1.0 collective-permute-start.28
  314.6 1.1 add.101
  316.7 12.9 %collective-permute-done.14.near_ref = bf16[384,1024]{1,0:T(8,128)(2,1)S(1)} collective-permute-done((bf16[384,1024]{1,0:T(8,128)(2,1)S(1)}, bf16[384,1024]{1,0:T(8,128)(2,1)S(1)}, u32[]{:S(2)}, u32[]{:S(2)}) %collective-permute-start.14) | collective-permute-done | bytes 786464 | tf_op jit(solution)/shard_map/ppermute | solution.py:569
  330.1 0.7 collective-permute-done.21.b0_ref
  330.8 0.9 copy-done.12
  332.7 0.9 copy-done.14
  334.0 0.9 copy-done.16
  335.2 2.6 out_proj_grad.1
  337.8 7.5 %memory_grad.1 = f32[2048,768]{1,0:T(8,128)} custom-call(s32[1]{0:T(128)} %bitcast.4.core_ref, bf16[2,256,2048]{2,1,0:T(8,128)(2,1)S(1)} %get-tuple-element.58.a0_ref, bf16[2,256,2048]{2,1,0:T(8,128)(2,1)S(1)} %get-tuple-element.61.a1_ref, bf16[2,256,2048]{2,1,0:T(8,128)(2,1)S(1)} %get-tuple-element.67.a2_ref, ...), custom_call_target="tpu_custom_call" | custom-call | flops 4831838208 | bytes 16777216 | tf_op jit(solution)/shard_map/memory_grad/pallas_call | solution.py:420
  345.3 5.6 %query_grad.1 = (f32[768,768]{1,0:T(8,128)}, f32[256,768]{1,0:T(8,128)}, f32[1,768]{1,0:T(1,128)S(1)}) custom-call(s32[5]{0:T(128)S(1)} %stack.32.place_ref, bf16[384,1024]{1,0:T(8,128)(2,1)S(1)} %bitcast.102, bf16[384,1024]{1,0:T(8,128)(2,1)S(1)} %collective-permute-done.14.near_ref, bf16[1024,768]{1,0:T(8,128)(2,1)S(1)} %copy-done.24, ...), custom_call_target="tpu_custom_call" | custom-call | flops 2415919104 | bytes 10485760 | tf_op jit(solution)/shard_map/query_grad/pallas_call | solution.py:503
  351.5 1.1 copy-done.13
  352.6 1.1 copy-done.15
  353.8 1.1 copy-done.17
  354.9 3.1 key_weights.1
  358.1 21.4 %mlp_weights.1 = (f32[768,3072]{1,0:T(8,128)}, f32[768,3072]{1,0:T(8,128)}, f32[3072,768]{1,0:T(8,128)}) custom-call(bf16[768,512]{1,0:T(8,128)(2,1)} %get-tuple-element.73.n2t_ref, bf16[512,768]{1,0:T(8,128)(2,1)} %get-tuple-element.74.gt_ref, bf16[512,3072]{1,0:T(8,128)(2,1)} %get-tuple-element.75.dgate_ref, bf16[512,3072]{1,0:T(8,128)(2,1)} %get-tuple-element.76.dup_ref, ...), custom_call_target="tpu_custom_call" | custom-call | flops 14495514624 | bytes 52428800 | tf_op jit(solution)/shard_map/mlp_weights/pallas_call | solution.py:391
  (153 shorter events, 10.7 us)
Async XLA Ops:
  0.6 129.9 %copy-start = (bf16[12,64,768]{2,1,0:T(8,128)(2,1)S(1)}, bf16[12,64,768]{2,1,0:T(8,128)(2,1)}, u32[]{:S(2)}) copy-start(bf16[12,64,768]{2,1,0:T(8,128)(2,1)} %param.21) | copy-start | bytes 3538948
  0.7 29.8 %collective-permute-start.3 = (bf16[2048,768]{1,0:T(8,128)(2,1)}, bf16[2048,768]{1,0:T(8,128)(2,1)}, u32[]{:S(2)}, u32[]{:S(2)}) collective-permute-start(bf16[2048,768]{1,0:T(8,128)(2,1)} %m_ref.1), channel_id=1, source_target_pairs={{0,1},{1,0},{2,3},{3,2},{4,5},{5,4},{6,7},{7,6}} | collective-permute-start | bytes 9437192 | tf_op jit(solution)/shard_map/ppermute | solution.py:569
  1.4 10.8 %collective-permute-start.1 = (bf16[256,768]{1,0:T(8,128)(2,1)}, bf16[256,768]{1,0:T(8,128)(2,1)S(1)}, u32[]{:S(2)}, u32[]{:S(2)}) collective-permute-start(bf16[256,768]{1,0:T(8,128)(2,1)} %x0_ref.2), channel_id=1, source_target_pairs={{0,2},{1,3},{2,0},{3,1},{4,6},{5,7},{6,4},{7,5}} | collective-permute-start | bytes 1179656 | tf_op jit(solution)/shard_map/ppermute | solution.py:572
  2.6 21.0 %collective-permute-start = (bf16[256,768]{1,0:T(8,128)(2,1)}, bf16[256,768]{1,0:T(8,128)(2,1)S(1)}, u32[]{:S(2)}, u32[]{:S(2)}) collective-permute-start(bf16[256,768]{1,0:T(8,128)(2,1)} %x0_ref.2), channel_id=1, source_target_pairs={{0,1},{1,0},{2,3},{3,2},{4,5},{5,4},{6,7},{7,6}} | collective-permute-start | bytes 1179656 | tf_op jit(solution)/shard_map/ppermute | solution.py:569
  12.2 11.4 %collective-permute-start.2 = (bf16[256,768]{1,0:T(8,128)(2,1)S(1)}, bf16[256,768]{1,0:T(8,128)(2,1)S(1)}, u32[]{:S(2)}, u32[]{:S(2)}) collective-permute-start(bf16[256,768]{1,0:T(8,128)(2,1)S(1)} %collective-permute-done.1.x2_ref), channel_id=1, source_target_pairs={{0,1},{1,0},{2,3},{3,2},{4,5},{5,4},{6,7},{7,6}} | collective-permute-start | bytes 1179656 | tf_op jit(solution)/shard_map/ppermute | solution.py:569
  13.1 115.6 %collective-permute-start.9 = (f32[256,768]{1,0:T(8,128)}, f32[256,768]{1,0:T(8,128)}, u32[]{:S(2)}, u32[]{:S(2)}) collective-permute-start(f32[256,768]{1,0:T(8,128)} %x0_ref.3), channel_id=1, source_target_pairs={{0,2},{1,3},{2,0},{3,1},{4,6},{5,7},{6,4},{7,5}} | collective-permute-start | bytes 2359304 | tf_op jit(solution)/shard_map/ppermute | solution.py:572
  16.3 7.3 %copy-start.10 = (bf16[768,12,64]{0,2,1:T(8,128)(2,1)S(1)}, bf16[768,12,64]{0,2,1:T(8,128)(2,1)}, u32[]{:S(2)}) copy-start(bf16[768,12,64]{0,2,1:T(8,128)(2,1)} %param.18) | copy-start | bytes 3538948
  16.3 7.3 %copy-start.22 = (bf16[256,768]{1,0:T(8,128)(2,1)S(1)}, bf16[256,768]{1,0:T(8,128)(2,1)}, u32[]{:S(2)}) copy-start(bf16[256,768]{1,0:T(8,128)(2,1)} %x0_ref.2) | copy-start | bytes 1179652
  63.9 16.6 %copy-start.40 = (f32[2,72,512]{2,1,0:T(8,128)S(1)}, f32[2,72,512]{2,1,0:T(8,128)}, u32[]{:S(2)}) copy-start(f32[2,72,512]{2,1,0:T(8,128)} %attn_fwd.6) | copy-start | bytes 884740
  80.5 10.1 %copy-start.39 = (f32[2,72,1024]{2,1,0:T(8,128)S(1)}, f32[2,72,1024]{2,1,0:T(8,128)}, u32[]{:S(2)}) copy-start(f32[2,72,1024]{2,1,0:T(8,128)} %attn_fwd.4) | copy-start | bytes 1769476
  80.5 11.5 %copy-start.38 = (f32[2,72,1024]{2,1,0:T(8,128)S(1)}, f32[2,72,1024]{2,1,0:T(8,128)}, u32[]{:S(2)}) copy-start(f32[2,72,1024]{2,1,0:T(8,128)} %attn_fwd.5) | copy-start | bytes 1769476
  80.5 11.6 %collective-permute-start.6 = (f32[2,72,512]{2,1,0:T(8,128)S(1)}, f32[2,72,512]{2,1,0:T(8,128)S(1)}, u32[]{:S(2)}, u32[]{:S(2)}) collective-permute-start(f32[2,72,512]{2,1,0:T(8,128)S(1)} %copy-done.40), channel_id=1, source_target_pairs={{0,2},{1,3},{2,0},{3,1},{4,6},{5,7},{6,4},{7,5}} | collective-permute-start | bytes 884744 | tf_op jit(solution)/shard_map/ppermute | solution.py:572
  90.6 8.5 %collective-permute-start.7 = (f32[2,72,512]{2,1,0:T(8,128)}, f32[2,72,512]{2,1,0:T(8,128)S(1)}, u32[]{:S(2)}, u32[]{:S(2)}) collective-permute-start(f32[2,72,512]{2,1,0:T(8,128)} %attn_fwd.7), channel_id=1, source_target_pairs={{0,2},{1,3},{2,0},{3,1},{4,6},{5,7},{6,4},{7,5}} | collective-permute-start | bytes 884744 | tf_op jit(solution)/shard_map/ppermute | solution.py:572
  90.6 21.1 %collective-permute-start.4 = (f32[2,72,1024]{2,1,0:T(8,128)S(1)}, f32[2,72,1024]{2,1,0:T(8,128)S(1)}, u32[]{:S(2)}, u32[]{:S(2)}) collective-permute-start(f32[2,72,1024]{2,1,0:T(8,128)S(1)} %copy-done.39), channel_id=1, source_target_pairs={{0,2},{1,3},{2,0},{3,1},{4,6},{5,7},{6,4},{7,5}} | collective-permute-start | bytes 1769480 | tf_op jit(solution)/shard_map/ppermute | solution.py:572
  92.1 32.3 %collective-permute-start.5 = (f32[2,72,1024]{2,1,0:T(8,128)S(1)}, f32[2,72,1024]{2,1,0:T(8,128)S(1)}, u32[]{:S(2)}, u32[]{:S(2)}) collective-permute-start(f32[2,72,1024]{2,1,0:T(8,128)S(1)} %copy-done.38), channel_id=1, source_target_pairs={{0,2},{1,3},{2,0},{3,1},{4,6},{5,7},{6,4},{7,5}} | collective-permute-start | bytes 1769480 | tf_op jit(solution)/shard_map/ppermute | solution.py:572
  100.6 24.6 %copy-start.33 = (f32[2,64,512]{2,1,0:T(8,128)}, f32[2,64,512]{2,1,0:T(8,128)S(1)}, u32[]{:S(2)}) copy-start(f32[2,64,512]{2,1,0:T(8,128)S(1)} %fusion.26) | copy-start | bytes 786436
  101.7 23.7 %copy-start.35 = (f32[2,64,512]{2,1,0:T(8,128)}, f32[2,64,512]{2,1,0:T(8,128)S(1)}, u32[]{:S(2)}) copy-start(f32[2,64,512]{2,1,0:T(8,128)S(1)} %fusion.24) | copy-start | bytes 786436
  125.3 3.4 copy-start.18
  126.2 4.9 %collective-permute-start.8 = (bf16[384,512]{1,0:T(8,128)(2,1)S(1)}, bf16[384,512]{1,0:T(8,128)(2,1)S(1)}, u32[]{:S(2)}, u32[]{:S(2)}) collective-permute-start(bf16[384,512]{1,0:T(8,128)(2,1)S(1)} %get-tuple-element.98), channel_id=1, source_target_pairs={{0,1},{1,0},{2,3},{3,2},{4,5},{5,4},{6,7},{7,6}} | collective-permute-start | bytes 1179656 | tf_op jit(solution)/shard_map/ppermute | solution.py:569
  128.7 3.0 copy-start.20
  130.5 1.1 copy-start.9
  131.7 23.3 %copy-start.7 = (bf16[384,512]{1,0:T(8,128)(2,1)}, bf16[384,512]{1,0:T(8,128)(2,1)S(1)}, u32[]{:S(2)}) copy-start(bf16[384,512]{1,0:T(8,128)(2,1)S(1)} %collective-permute-done.8.near0_ref) | copy-start | bytes 1179652
  133.2 22.3 %copy-start.41 = (f32[2,1,1024]{2,1,0:T(1,128)S(1)}, f32[2,1,1024]{2,1,0:T(1,128)}, u32[]{:S(2)}) copy-start(f32[2,1,1024]{2,1,0:T(1,128)} %get-tuple-element.85) | copy-start | bytes 24580
  133.2 22.3 %copy-start.42 = (f32[2,1,512]{2,1,0:T(1,128)S(1)}, f32[2,1,512]{2,1,0:T(1,128)}, u32[]{:S(2)}) copy-start(f32[2,1,512]{2,1,0:T(1,128)} %get-tuple-element.89) | copy-start | bytes 12292
  133.2 22.3 %copy-start.43 = (f32[2,1,512]{2,1,0:T(1,128)S(1)}, f32[2,1,512]{2,1,0:T(1,128)}, u32[]{:S(2)}) copy-start(f32[2,1,512]{2,1,0:T(1,128)} %get-tuple-element.93) | copy-start | bytes 12292
  133.2 25.2 %copy-start.32 = (f32[2,64,1024]{2,1,0:T(8,128)S(1)}, f32[2,64,1024]{2,1,0:T(8,128)}, u32[]{:S(2)}) copy-start(f32[2,64,1024]{2,1,0:T(8,128)} %copy-done.31) | copy-start | bytes 1572868
  133.2 25.2 %copy-start.34 = (f32[2,64,512]{2,1,0:T(8,128)S(1)}, f32[2,64,512]{2,1,0:T(8,128)}, u32[]{:S(2)}) copy-start(f32[2,64,512]{2,1,0:T(8,128)} %copy-done.33) | copy-start | bytes 786436
  133.2 25.2 %copy-start.36 = (f32[2,64,512]{2,1,0:T(8,128)S(1)}, f32[2,64,512]{2,1,0:T(8,128)}, u32[]{:S(2)}) copy-start(f32[2,64,512]{2,1,0:T(8,128)} %copy-done.35) | copy-start | bytes 786436
  155.0 2.5 collective-permute-start.10
  155.0 100.0 %collective-permute-start.24 = (bf16[384,512]{1,0:T(8,128)(2,1)}, bf16[384,512]{1,0:T(8,128)(2,1)S(1)}, u32[]{:S(2)}, u32[]{:S(2)}) collective-permute-start(bf16[384,512]{1,0:T(8,128)(2,1)} %get-tuple-element.97), channel_id=1, source_target_pairs={{0,1},{1,0},{2,3},{3,2},{4,5},{5,4},{6,7},{7,6}} | collective-permute-start | bytes 1179656 | tf_op jit(solution)/shard_map/ppermute | solution.py:569
  155.5 101.0 %collective-permute-start.25 = (f32[1,768]{1,0:T(1,128)}, f32[1,768]{1,0:T(1,128)S(1)}, u32[]{:S(2)}, u32[]{:S(2)}) collective-permute-start(f32[1,768]{1,0:T(1,128)} %get-tuple-element.72), channel_id=1, source_target_pairs={{0,1},{1,0},{2,3},{3,2},{4,5},{5,4},{6,7},{7,6}} | collective-permute-start | bytes 9224 | tf_op jit(solution)/shard_map/ppermute | solution.py:569
  155.6 3.4 copy-start.6
  157.5 2.1 copy-start.5
  157.6 2.2 copy-start.26
  158.4 2.5 copy-start.4
  158.4 2.5 copy-start.27
  189.3 67.2 %collective-permute-start.11 = (f32[2,64,1024]{2,1,0:T(8,128)S(1)}, f32[2,64,1024]{2,1,0:T(8,128)S(1)}, u32[]{:S(2)}, u32[]{:S(2)}) collective-permute-start(f32[2,64,1024]{2,1,0:T(8,128)S(1)} %get-tuple-element.57), channel_id=1, source_target_pairs={{0,2},{1,3},{2,0},{3,1},{4,6},{5,7},{6,4},{7,5}} | collective-permute-start | bytes 1572872 | tf_op jit(solution)/shard_map/ppermute | solution.py:572
  218.1 39.1 %collective-permute-start.12 = (f32[2,64,1024]{2,1,0:T(8,128)S(1)}, f32[2,64,1024]{2,1,0:T(8,128)}, u32[]{:S(2)}, u32[]{:S(2)}) collective-permute-start(f32[2,64,1024]{2,1,0:T(8,128)S(1)} %get-tuple-element.60), channel_id=1, source_target_pairs={{0,2},{1,3},{2,0},{3,1},{4,6},{5,7},{6,4},{7,5}} | collective-permute-start | bytes 1572872 | tf_op jit(solution)/shard_map/ppermute | solution.py:572
  249.1 13.4 %collective-permute-start.13 = (f32[2,64,1024]{2,1,0:T(8,128)S(1)}, f32[2,64,1024]{2,1,0:T(8,128)S(1)}, u32[]{:S(2)}, u32[]{:S(2)}) collective-permute-start(f32[2,64,1024]{2,1,0:T(8,128)S(1)} %get-tuple-element.63), channel_id=1, source_target_pairs={{0,2},{1,3},{2,0},{3,1},{4,6},{5,7},{6,4},{7,5}} | collective-permute-start | bytes 1572872 | tf_op jit(solution)/shard_map/ppermute | solution.py:572
  252.0 3.0 copy-start.37
  255.0 24.3 %collective-permute-start.18 = (f32[256,768]{1,0:T(8,128)S(1)}, f32[256,768]{1,0:T(8,128)S(1)}, u32[]{:S(2)}, u32[]{:S(2)}) collective-permute-start(f32[256,768]{1,0:T(8,128)S(1)} %copy-done.37), channel_id=1, source_target_pairs={{0,2},{1,3},{2,0},{3,1},{4,6},{5,7},{6,4},{7,5}} | collective-permute-start | bytes 2359304 | tf_op jit(solution)/shard_map/ppermute | solution.py:572
  256.5 57.5 %collective-permute-start.19 = (f32[256,768]{1,0:T(8,128)S(1)}, f32[256,768]{1,0:T(8,128)S(1)}, u32[]{:S(2)}, u32[]{:S(2)}) collective-permute-start(f32[256,768]{1,0:T(8,128)S(1)} %convolution_add_fusion.1), channel_id=1, source_target_pairs={{0,2},{1,3},{2,0},{3,1},{4,6},{5,7},{6,4},{7,5}} | collective-permute-start | bytes 2359304 | tf_op jit(solution)/shard_map/ppermute | solution.py:572
  256.6 57.5 %collective-permute-start.15 = (bf16[256,2048]{1,0:T(8,128)(2,1)S(1)}, bf16[256,2048]{1,0:T(8,128)(2,1)S(1)}, u32[]{:S(2)}, u32[]{:S(2)}) collective-permute-start(bf16[256,2048]{1,0:T(8,128)(2,1)S(1)} %slice_bitcast_fusion.2), channel_id=1, source_target_pairs={{0,1},{1,0},{2,3},{3,2},{4,5},{5,4},{6,7},{7,6}} | collective-permute-start | bytes 3145736 | tf_op jit(solution)/shard_map/ppermute | solution.py:569
  257.2 55.8 %collective-permute-start.20 = (f32[256,768]{1,0:T(8,128)S(1)}, f32[256,768]{1,0:T(8,128)S(1)}, u32[]{:S(2)}, u32[]{:S(2)}) collective-permute-start(f32[256,768]{1,0:T(8,128)S(1)} %convolution_add_fusion), channel_id=1, source_target_pairs={{0,2},{1,3},{2,0},{3,1},{4,6},{5,7},{6,4},{7,5}} | collective-permute-start | bytes 2359304 | tf_op jit(solution)/shard_map/ppermute | solution.py:572
  262.5 53.4 %collective-permute-start.16 = (bf16[256,2048]{1,0:T(8,128)(2,1)S(1)}, bf16[256,2048]{1,0:T(8,128)(2,1)S(1)}, u32[]{:S(2)}, u32[]{:S(2)}) collective-permute-start(bf16[256,2048]{1,0:T(8,128)(2,1)S(1)} %slice_bitcast_fusion.1), channel_id=1, source_target_pairs={{0,1},{1,0},{2,3},{3,2},{4,5},{5,4},{6,7},{7,6}} | collective-permute-start | bytes 3145736 | tf_op jit(solution)/shard_map/ppermute | solution.py:569
  279.4 36.8 %collective-permute-start.17 = (bf16[256,2048]{1,0:T(8,128)(2,1)S(1)}, bf16[256,2048]{1,0:T(8,128)(2,1)S(1)}, u32[]{:S(2)}, u32[]{:S(2)}) collective-permute-start(bf16[256,2048]{1,0:T(8,128)(2,1)S(1)} %slice_bitcast_fusion), channel_id=1, source_target_pairs={{0,1},{1,0},{2,3},{3,2},{4,5},{5,4},{6,7},{7,6}} | collective-permute-start | bytes 3145736 | tf_op jit(solution)/shard_map/ppermute | solution.py:569
  313.1 45.0 %collective-permute-start.28 = (bf16[512,3072]{1,0:T(8,128)(2,1)}, bf16[512,3072]{1,0:T(8,128)(2,1)}, u32[]{:S(2)}, u32[]{:S(2)}) collective-permute-start(bf16[512,3072]{1,0:T(8,128)(2,1)} %get-tuple-element.75.dgate_ref), channel_id=1, source_target_pairs={{0,1},{1,0},{2,3},{3,2},{4,5},{5,4},{6,7},{7,6}} | collective-permute-start | bytes 9437192 | tf_op jit(solution)/shard_map/ppermute | solution.py:569
  314.0 44.0 %collective-permute-start.29 = (bf16[512,3072]{1,0:T(8,128)(2,1)}, bf16[512,3072]{1,0:T(8,128)(2,1)}, u32[]{:S(2)}, u32[]{:S(2)}) collective-permute-start(bf16[512,3072]{1,0:T(8,128)(2,1)} %get-tuple-element.76.dup_ref), channel_id=1, source_target_pairs={{0,1},{1,0},{2,3},{3,2},{4,5},{5,4},{6,7},{7,6}} | collective-permute-start | bytes 9437192 | tf_op jit(solution)/shard_map/ppermute | solution.py:569
  314.1 44.0 %collective-permute-start.30 = (bf16[3072,512]{1,0:T(8,128)(2,1)}, bf16[3072,512]{1,0:T(8,128)(2,1)}, u32[]{:S(2)}, u32[]{:S(2)}) collective-permute-start(bf16[3072,512]{1,0:T(8,128)(2,1)} %get-tuple-element.77.ut_ref), channel_id=1, source_target_pairs={{0,1},{1,0},{2,3},{3,2},{4,5},{5,4},{6,7},{7,6}} | collective-permute-start | bytes 9437192 | tf_op jit(solution)/shard_map/ppermute | solution.py:569
  315.9 13.7 %collective-permute-start.14 = (bf16[384,1024]{1,0:T(8,128)(2,1)S(1)}, bf16[384,1024]{1,0:T(8,128)(2,1)S(1)}, u32[]{:S(2)}, u32[]{:S(2)}) collective-permute-start(bf16[384,1024]{1,0:T(8,128)(2,1)S(1)} %bitcast.101), channel_id=1, source_target_pairs={{0,1},{1,0},{2,3},{3,2},{4,5},{5,4},{6,7},{7,6}} | collective-permute-start | bytes 2359304 | tf_op jit(solution)/shard_map/ppermute | solution.py:569
  316.1 15.9 %copy-start.44 = (f32[1,768]{1,0:T(1,128)S(1)}, f32[1,768]{1,0:T(1,128)}, u32[]{:S(2)}) copy-start(f32[1,768]{1,0:T(1,128)} %get-tuple-element.72) | copy-start | bytes 9220
  316.1 19.1 %copy-start.8 = (bf16[384,512]{1,0:T(8,128)(2,1)S(1)}, bf16[384,512]{1,0:T(8,128)(2,1)}, u32[]{:S(2)}) copy-start(bf16[384,512]{1,0:T(8,128)(2,1)} %copy-done.7) | copy-start | bytes 1179652
  316.1 14.7 %collective-permute-start.21 = (f32[256,768]{1,0:T(8,128)S(1)}, f32[256,768]{1,0:T(8,128)S(1)}, u32[]{:S(2)}, u32[]{:S(2)}) collective-permute-start(f32[256,768]{1,0:T(8,128)S(1)} %add.104.a0_ref), channel_id=1, source_target_pairs={{0,1},{1,0},{2,3},{3,2},{4,5},{5,4},{6,7},{7,6}} | collective-permute-start | bytes 2359304 | tf_op jit(solution)/shard_map/ppermute | solution.py:569
  329.7 3.0 collective-permute-start.23
  331.7 2.3 collective-permute-start.22
  333.5 24.5 %collective-permute-start.26 = (bf16[768,512]{1,0:T(8,128)(2,1)}, bf16[768,512]{1,0:T(8,128)(2,1)}, u32[]{:S(2)}, u32[]{:S(2)}) collective-permute-start(bf16[768,512]{1,0:T(8,128)(2,1)} %get-tuple-element.73.n2t_ref), channel_id=1, source_target_pairs={{0,1},{1,0},{2,3},{3,2},{4,5},{5,4},{6,7},{7,6}} | collective-permute-start | bytes 2359304 | tf_op jit(solution)/shard_map/ppermute | solution.py:569
  334.8 3.0 copy-start.2
  334.8 3.0 copy-start.3
  334.8 23.2 %collective-permute-start.27 = (bf16[512,768]{1,0:T(8,128)(2,1)}, bf16[512,768]{1,0:T(8,128)(2,1)}, u32[]{:S(2)}, u32[]{:S(2)}) collective-permute-start(bf16[512,768]{1,0:T(8,128)(2,1)} %get-tuple-element.74.gt_ref), channel_id=1, source_target_pairs={{0,1},{1,0},{2,3},{3,2},{4,5},{5,4},{6,7},{7,6}} | collective-permute-start | bytes 2359304 | tf_op jit(solution)/shard_map/ppermute | solution.py:569
  337.8 7.5 %copy-start.11 = (bf16[768,12,64]{0,2,1:T(8,128)(2,1)S(1)}, bf16[768,12,64]{0,2,1:T(8,128)(2,1)}, u32[]{:S(2)}) copy-start(bf16[768,12,64]{0,2,1:T(8,128)(2,1)} %param.18) | copy-start | bytes 3538948
  337.8 7.5 %copy-start.21 = (bf16[1024,768]{1,0:T(8,128)(2,1)S(1)}, bf16[1024,768]{1,0:T(8,128)(2,1)}, u32[]{:S(2)}) copy-start(bf16[1024,768]{1,0:T(8,128)(2,1)} %copy-done.19) | copy-start | bytes 4718596
  337.8 7.5 %copy-start.24 = (bf16[1024,768]{1,0:T(8,128)(2,1)S(1)}, bf16[1024,768]{1,0:T(8,128)(2,1)}, u32[]{:S(2)}) copy-start(bf16[1024,768]{1,0:T(8,128)(2,1)} %copy-done.23) | copy-start | bytes 4718596
  337.8 7.5 %copy-start.28 = (f32[512,768]{1,0:T(8,128)S(1)}, f32[512,768]{1,0:T(8,128)}, u32[]{:S(2)}) copy-start(f32[512,768]{1,0:T(8,128)} %get-tuple-element.65.dh_ref) | copy-start | bytes 4718596
  358.1 21.4 %copy-start.1 = (bf16[12,64,768]{2,1,0:T(8,128)(2,1)S(1)}, bf16[12,64,768]{2,1,0:T(8,128)(2,1)}, u32[]{:S(2)}) copy-start(bf16[12,64,768]{2,1,0:T(8,128)(2,1)} %param.21) | copy-start | bytes 3538948
  (12 other events, 12.3 us)

commit v2 on v1

--- a/solution.py
+++ b/solution.py
@@ -35,12 +35,10 @@
 def proj_kernel(core_ref, m_ref, wk_ref, wv_ref, *refs):
     k_ref, v_ref, kt_ref, vt_ref = refs[-4:]
     m = m_ref[...]
-    k = dot_nt(m, wk_ref[...]).astype(BF)
-    v = dot_nt(m, wv_ref[...]).astype(BF)
-    k_ref[...] = k
-    v_ref[...] = v
-    kt_ref[...] = k.T
-    vt_ref[...] = v.T
+    k_ref[...] = dot_nt(m, wk_ref[...]).astype(BF)
+    v_ref[...] = dot_nt(m, wv_ref[...]).astype(BF)
+    kt_ref[...] = dot_nt(wk_ref[...], m).astype(BF)
+    vt_ref[...] = dot_nt(wv_ref[...], m).astype(BF)
 
 
 def project(core, mem, wkt, wvt, seg, before):
@@ -234,24 +232,30 @@
         cols = pl.ds(pl.multiple_of(j * BKB, BKB), BKB)
         allc = pl.ds(pl.multiple_of(seg * seg_rows + j * BKB, BKB), BKB)
         kb, vb = k_ref[allc, :], v_ref[allc, :]
-        for h in range(2):
+        chunks = [(h, slice(c * BQB, (c + 1) * BQB)) for h in range(2) for c in range(nq // BQB)]
+
+        def products(h, qs):
+            return dot(kb, qzt_ref[h, :, qs]), dot(vb, dozt_ref[h, :, qs])
+
+        ahead = products(*chunks[0])
+        for i, (h, qs) in enumerate(chunks):
+            st, dp = ahead
+            if i + 1 < len(chunks):
+                ahead = products(*chunks[i + 1])
             hs = slice(h * 64, (h + 1) * 64)
-            ktb = kt_ref[hs, allc]
-            dk = jnp.zeros((64, BKB), F32)
-            dv = jnp.zeros((64, BKB), F32)
-            for c in range(nq // BQB):
-                qs = slice(c * BQB, (c + 1) * BQB)
-                st = dot(kb, qzt_ref[h, :, qs])
-                p = jnp.exp2((st - lse_ref[h, :, qs]) * LOG2E)
-                if count is not None:
-                    p = jnp.where(lax.broadcasted_iota(jnp.int32, st.shape, 0) < count, p, 0.0)
-                dp = dot(vb, dozt_ref[h, :, qs])
-                ds = (p * (dp - dl_ref[h, :, qs])).astype(BF)
-                dv = dv + dot_nt(dot_ref[hs, qs], p.astype(BF))
-                dk = dk + dot_nt(qt_ref[hs, qs], ds)
-                dqt_ref[h, :, qs] += dot(ktb, ds)
-            dkv_ref[seg, hs, cols] = dk.astype(BF)
-            dkv_ref[seg, PAIR + h * 64:PAIR + (h + 1) * 64, cols] = dv.astype(BF)
+            if qs.start == 0:
+                dk = jnp.zeros((64, BKB), F32)
+                dv = jnp.zeros((64, BKB), F32)
+            p = jnp.exp2((st - lse_ref[h, :, qs]) * LOG2E)
+            if count is not None:
+                p = jnp.where(lax.broadcasted_iota(jnp.int32, st.shape, 0) < count, p, 0.0)
+            ds = (p * (dp - dl_ref[h, :, qs])).astype(BF)
+            dv = dv + dot_nt(dot_ref[hs, qs], p.astype(BF))
+            dk = dk + dot_nt(qt_ref[hs, qs], ds)
+            dqt_ref[h, :, qs] += dot(kt_ref[hs, allc], ds)
+            if qs.stop == nq:
+                dkv_ref[seg, hs, cols] = dk.astype(BF)
+                dkv_ref[seg, PAIR + h * 64:PAIR + (h + 1) * 64, cols] = dv.astype(BF)
 
     first = len_ref[0] // BKB
 
@@ -301,6 +305,92 @@
     )(lens, qt, dot_t, lse, delta, k, v, kt)
 
 
+def pair_weights_kernel(dkv_ref, m0_ref, m1_ref, o_ref):
+    step = pl.program_id(0)
+    half = pl.num_programs(0) // 2
+
+    @pl.when(step == 0)
+    def _():
+        o_ref[...] = dot(dkv_ref[...], m0_ref[...])
+
+    @pl.when((step > 0) & (step < half))
+    def _():
+        o_ref[...] += dot(dkv_ref[...], m0_ref[...])
+
+    @pl.when(step >= half)
+    def _():
+        o_ref[...] += dot(dkv_ref[...], m1_ref[...])
+
+
+def pair_weights(dkv, mem, mem_near):
+    _, width, rows = dkv.shape
+    dim = mem.shape[1]
+    block = 1024
+    half = rows // block
+    return pl.pallas_call(
+        pair_weights_kernel,
+        grid=(2 * half,),
+        in_specs=[pl.BlockSpec((None, width, block), lambda i: (i // half, 0, i % half)),
+                  pl.BlockSpec((block, dim), lambda i: (jnp.minimum(i, half - 1), 0)),
+                  pl.BlockSpec((block, dim), lambda i: (jnp.maximum(i - half, 0), 0))],
+        out_specs=pl.BlockSpec((width, dim), lambda i: (0, 0)),
+        out_shape=jax.ShapeDtypeStruct((width, dim), F32),
+        compiler_params=pltpu.CompilerParams(vmem_limit_bytes=24 << 20),
+        cost_estimate=cost(4 * rows * dim * width, 8 << 20),
+        name="pair_weights",
+    )(dkv, mem, mem_near)
+
+
+def combine_kernel(a_ref, b_ref, o_ref, ob_ref, lse_ref):
+    for h in range(2):
+        ma, mb = a_ref[h, 64:65, :], b_ref[h, 64:65, :]
+        top = jnp.maximum(ma, mb)
+        ea, eb = jnp.exp(ma - top), jnp.exp(mb - top)
+        den = a_ref[h, 65:66, :] * ea + b_ref[h, 65:66, :] * eb
+        o = (a_ref[h, :64, :] * ea + b_ref[h, :64, :] * eb) / den
+        o_ref[h] = o
+        ob_ref[h * 64:(h + 1) * 64, :] = o.astype(BF)
+        lse_ref[h] = top + jnp.log(den)
+
+
+def combine(a, b):
+    _, rows, nq = a.shape
+    fix = lambda *shape: pl.BlockSpec(shape, lambda i: (0,) * len(shape))
+    return pl.pallas_call(
+        combine_kernel,
+        grid=(1,),
+        in_specs=[fix(2, rows, nq)] * 2,
+        out_specs=[fix(2, 64, nq), fix(PAIR, nq), fix(2, 1, nq)],
+        out_shape=[jax.ShapeDtypeStruct((2, 64, nq), F32), jax.ShapeDtypeStruct((PAIR, nq), BF),
+                   jax.ShapeDtypeStruct((2, 1, nq), F32)],
+        compiler_params=pltpu.CompilerParams(vmem_limit_bytes=16 << 20),
+        cost_estimate=cost(500 * nq, 2 << 20),
+        name="combine",
+    )(a, b)
+
+
+def sum_queries_kernel(a0_ref, a1_ref, a2_ref, b0_ref, b1_ref, b2_ref, o_ref):
+    for i, (a, b) in enumerate(((a0_ref, b0_ref), (a1_ref, b1_ref), (a2_ref, b2_ref))):
+        for h in range(2):
+            at = i * PAIR + h * 64
+            o_ref[at:at + 64, :] = ((a[h] + b[h]) * 0.125).astype(BF)
+
+
+def sum_queries(mine, far):
+    nq = mine[0].shape[2]
+    part = pl.BlockSpec((2, 64, nq // 2), lambda i: (0, 0, i))
+    return pl.pallas_call(
+        sum_queries_kernel,
+        grid=(2,),
+        in_specs=[part] * 6,
+        out_specs=pl.BlockSpec((3 * PAIR, nq // 2), lambda i: (0, i)),
+        out_shape=jax.ShapeDtypeStruct((3 * PAIR, nq), BF),
+        compiler_params=pltpu.CompilerParams(vmem_limit_bytes=16 << 20),
+        cost_estimate=cost(1000 * nq, 4 << 20),
+        name="sum_queries",
+    )(*mine, *far)
+
+
 def mlp_kernel(h_ref, g_ref, gain_ref, w1_ref, w3_ref, w2_ref,
                n2t_ref, gt_ref, dgate_ref, dup_ref, ut_ref, dh_ref, dhb_ref, gn_ref, n2_ref, acc_ref):
     step = pl.program_id(0)
@@ -516,29 +606,32 @@
     )(place, mine, near, n1, wqt, x_all, d_hid, gain)
 
 
-def key_weights_kernel(core_ref, a0_ref, a1_ref, a2_ref, b0_ref, b1_ref, b2_ref, gk_ref, gv_ref):
-    for at, ref in enumerate((a0_ref, a1_ref, a2_ref, b0_ref, b1_ref, b2_ref)):
+def key_weights_kernel(core_ref, *refs):
+    gk_ref, gv_ref = refs[-2:]
+    count = (len(refs) - 2) // 2
+    for at in range(count):
         @pl.when(pl.program_id(0) == at)
         def _():
-            gk_ref[...] = ref[:PAIR, :]
-            gv_ref[...] = ref[PAIR:, :]
-
-
-def key_weights(core, mine, near):
-    pairs = len(mine)
-    dim = mine[0].shape[1]
+            a, b = refs[at], refs[count + at]
+            gk_ref[...] = a[:PAIR, :] + b[:PAIR, :]
+            gv_ref[...] = a[PAIR:, :] + b[PAIR:, :]
+
+
+def key_weights(core, parts, others):
+    pairs = len(parts) // 2
+    dim = parts[0].shape[1]
     out = pl.BlockSpec((PAIR, dim), lambda i, s: (half_index(i // pairs, s[0]) * pairs + i % pairs, 0))
     return pl.pallas_call(
         key_weights_kernel,
         out_shape=[jax.ShapeDtypeStruct((2 * pairs * PAIR, dim), F32)] * 2,
         grid_spec=pltpu.PrefetchScalarGridSpec(
             num_scalar_prefetch=1, grid=(2 * pairs,),
-            in_specs=[pl.BlockSpec((2 * PAIR, dim), lambda i, s: (0, 0))] * (2 * pairs),
+            in_specs=[pl.BlockSpec((2 * PAIR, dim), lambda i, s: (0, 0))] * (4 * pairs),
             out_specs=[out, out]),
         compiler_params=pltpu.CompilerParams(vmem_limit_bytes=24 << 20),
         cost_estimate=cost(4 * pairs * PAIR * dim, 10 << 20),
         name="key_weights",
-    )(core, *mine, *near)
+    )(core, *parts, *others)
 
 
 def inv_rms(tensor):
@@ -609,19 +702,18 @@
         for pair, at, count in pieces:
             part = attention_forward(lens, qt_s, k, vt, pair, 1, at, count)
             parts.append((part, to_far(part)))
+        outs_b = []
         for a, b in parts:
-            ma, mb = a[:, 64:65], b[:, 64:65]
-            top = jnp.maximum(ma, mb)
-            ea, eb = jnp.exp(ma - top), jnp.exp(mb - top)
-            den = a[:, 65:66] * ea + b[:, 65:66] * eb
-            outs.append((a[:, :64] * ea + b[:, :64] * eb) / den)
-            lses.append(top + jnp.log(den))
-        outs[-2:] = [jnp.concatenate(outs[-2:], axis=2)]
-        lses[-2:] = [jnp.concatenate(lses[-2:], axis=2)]
+            o_piece, ob_piece, lse_piece = combine(a, b)
+            outs.append(o_piece)
+            outs_b.append(ob_piece)
+            lses.append(lse_piece)
+        for pieces_of, axis in ((outs, 2), (outs_b, 1), (lses, 2)):
+            pieces_of[-2:] = [jnp.concatenate(pieces_of[-2:], axis=axis)]
         g_half = place_rows(place, g_parts)
         o_t = jnp.concatenate(outs, axis=0)
         lse = jnp.concatenate(lses, axis=0)
-        o_t_b = o_t.astype(BF).reshape(width, n * rows)
+        o_t_b = jnp.concatenate(outs_b, axis=0)
         half = n * rows // 2
         o_t_first, o_t_second = o_t_b[:, :half], o_t_b[:, half:]
         o_near_first = to_near(o_t_second)
@@ -648,7 +740,7 @@
         for pair in range(pairs):
             dkv, dqt = attention_backward(lens_now, qt_s, do_t, lse, delta, k, v, kt, pair)
             dqs.append((dqt, to_far(dqt)))
-            dw = mm(dkv[0], memory, 1, 0) + mm(dkv[1], mem_near, 1, 0)
+            dw = pair_weights(dkv, memory, mem_near)
             dws.append((dw, to_far(dw)))
             dkvs.append(dkv)
             dkvs_near.append(to_near(dkv[1]))
@@ -664,15 +756,15 @@
 
         g_wo = out_proj_grad(core1, o_t_b, (o_near_first, o_near_second), d_hid_b).reshape(heads, head, dim)
 
-        dqt_b = (jnp.concatenate([a + b for a, b in dqs], axis=0) * (head ** -0.5)).astype(BF).reshape(width, n * rows)
+        dqt_b = sum_queries([a for a, _ in dqs], [b for _, b in dqs])
         dqt_near = to_near(dqt_b)
         g_wqt, g_dec, g_norm_attn = query_grad(place, dqt_b, dqt_near, n1, wqt, x_all_b, d_hid, gain1, rows)
 
-        dw_mine, dw_near = [], []
+        mine_near = []
         for a, b in dws:
-            dw_mine.append(a + b)
-            dw_near.append(to_near(dw_mine[-1]))
-        g_wkt, g_wvt = key_weights(core1, dw_mine, dw_near)
+            mine_near.append((to_near(a), to_near(b)))
+        g_wkt, g_wvt = key_weights(core1, [a for a, _ in dws] + [a for a, _ in mine_near],
+                                   [b for _, b in dws] + [b for _, b in mine_near])
         g_wq, g_wk, g_wv = as_weight(g_wqt), as_weight(g_wkt), as_weight(g_wvt)
         return (g_dec, g_mem, g_norm_attn.reshape(dim), g_wq, g_wk, g_wv, g_wo, g_norm_mlp.reshape(dim), g_gate, g_up, g_down)
 

time: 385 us -> 389 us (1.010)
  matrix products: 21.2 us -> 2.89 us
  Pallas kernels: 210 us -> 224 us
  local copies, waits for them, and re-layouts: 16.5 us -> 24.9 us
  other arithmetic: 8.08 us -> 2.33 us
    dot_general x9 -> x3, matrix products: 21.2 us -> 2.89 us  [mm(): lax.dot_general(a, b, (((ca,), (cb,)), ((), ())), preferred_element_type=...]
    pallas_call x0 -> x8, Pallas kernels: none -> 17.5 us  [the longest x3 14.5 us: pair_weights(): pl.pallas_call(pair_weights_kernel, grid=(2 * half,), in_specs=[pl.BlockS...]
    pallas_call x3, Pallas kernels: 75.6 us -> 65.7 us  [attention_backward(): pl.pallas_call(bwd_kernel, out_shape=[jax.ShapeDtypeStruct((2, 2 * PAIR,...]
    unnamed x99 -> x137, local copies, waits for them, and re-layouts: 13.3 us -> 21.8 us
    add x10 -> x0, other arithmetic: 4.32 us -> none  [the longest x4 2.78 us: device_work(): lses.append(top + jnp.log(den))]
    ppermute x19 -> x22, starting transfers between devices: 10.6 us -> 14 us  [to_near(): return lax.ppermute(a, 'seq', near)]
    ppermute x19 -> x22, waiting for transfers between devices: 14.5 us -> 15.2 us  [to_near(): return lax.ppermute(a, 'seq', near)]
  transfers between devices with their start and end apart: 31 -> 34, of which waited for: 11 -> 11; matrix products, arithmetic and copies ran while one was open for 9% -> 2% of each run, Pallas kernels for 44% -> 34%
where the time goes in v2:
time: 389 us; the launch traced here: 383 us
  Pallas kernels  224 us (58%)
  waiting for transfers between devices  106 us (27%)
  local copies, waits for them, and re-layouts  24.9 us (6%)
  starting transfers between devices  21.7 us (6%)
    ppermute x12, waiting for transfers between devices, to_far(): return lax.ppermute(a, 'seq', far)  90.3 us
    pallas_call x3, Pallas kernels, attention_backward(): pl.pallas_call(bwd_kernel, out_shape=[jax.ShapeDtypeStruct((2, 2 * PAIR,...  65.7 us
    pallas_call x4, Pallas kernels, attention_forward(): pl.pallas_call(fwd_kernel, out_shape=jax.ShapeDtypeStruct((2 * pairs, ORO...  52.8 us
    unnamed x137, local copies, waits for them, and re-layouts  21.8 us
    pallas_call x1, Pallas kernels, mlp(): pl.pallas_call(mlp_kernel, grid=(ff // FFB,), in_specs=[fix(rows, dim), f...  21.8 us
    pallas_call x1, Pallas kernels, mlp_weights(): pl.pallas_call(mlp_weights_kernel, grid=(ff // FFB,), in_specs=ins + ins,...  21.4 us
    pallas_call x2, Pallas kernels, project(): pl.pallas_call(proj_kernel, out_shape=outs, grid_spec=pltpu.PrefetchScala...  17.7 us
    ppermute x22, waiting for transfers between devices, to_near(): return lax.ppermute(a, 'seq', near)  15.2 us
  transfers between devices with their start and end apart: 34, of which 11 were waited for; matrix products, arithmetic and copies ran while one was open for 2% of the time, Pallas kernels for 34%

profile of v2, /device:TPU:5, one launch (start us, length us, event | category | flops | bytes accessed | tf_op | source)
XLA Modules:
  0.0 383.4 jit_solution(10521096433057849637)
XLA Ops:
  1.4 1.2 collective-permute-start.1
  2.9 9.3 %collective-permute-done.1.x2_ref = bf16[256,768]{1,0:T(8,128)(2,1)S(1)} collective-permute-done((bf16[256,768]{1,0:T(8,128)(2,1)}, bf16[256,768]{1,0:T(8,128)(2,1)S(1)}, u32[]{:S(2)}, u32[]{:S(2)}) %collective-permute-start.1) | collective-permute-done | bytes 393248 | tf_op jit(solution)/shard_map/ppermute | solution.py:665
  12.2 0.9 collective-permute-start.2
  15.2 8.8 %kv_proj.2 = (bf16[4096,384]{1,0:T(8,128)(2,1)}, bf16[4096,384]{1,0:T(8,128)(2,1)}, bf16[384,4096]{1,0:T(8,128)(2,1)}, bf16[384,4096]{1,0:T(8,128)(2,1)}) custom-call(s32[1]{0:T(128)} %bitcast.4.core_ref, bf16[2048,768]{1,0:T(8,128)(2,1)} %m0_ref.5, bf16[768,768]{1,0:T(8,128)(2,1)} %bitcast.42, bf16[768,768]{1,0:T(8,128)(2,1)} %bitcast.45), custom_call_target="tpu_custom_call" | custom-call | flops 2415919104 | bytes 12582912 | tf_op jit(solution)/shard_map/kv_proj/pallas_call | solution.py:53
  24.0 3.6 queries.1
  27.7 1.1 copy-done.44
  28.8 1.1 copy-done.60
  30.0 0.9 copy-done.62
  30.8 8.9 %kv_proj.3 = (bf16[4096,384]{1,0:T(8,128)(2,1)}, bf16[4096,384]{1,0:T(8,128)(2,1)}, bf16[384,4096]{1,0:T(8,128)(2,1)}, bf16[384,4096]{1,0:T(8,128)(2,1)}) custom-call(s32[1]{0:T(128)} %bitcast.4.core_ref, bf16[2048,768]{1,0:T(8,128)(2,1)} %collective-permute-done.3.m_ref.m1_ref, ...), custom_call_target="tpu_custom_call", output_to_operand_aliasing={{0}: (4, {}), {1}: (5, {}), {2}: (6, {}), {3}: (7, {})} | custom-call | flops 2415919104 | bytes 12582912 | tf_op jit(solution)/shard_map/kv_proj/pallas_call | solution.py:53
  39.8 9.8 %attn_fwd.6.a_ref = f32[2,72,512]{2,1,0:T(8,128)} custom-call(s32[2]{0:T(128)} %pad_add_fusion.len_ref, bf16[384,1024]{1,0:T(8,128)(2,1)} %copy-done.62, bf16[4096,384]{1,0:T(8,128)(2,1)} %get-tuple-element.64.k_ref, bf16[384,4096]{1,0:T(8,128)(2,1)} %get-tuple-element.65.vt_ref), custom_call_target="tpu_custom_call" | custom-call | flops 4294967296 | bytes 4194304 | tf_op jit(solution)/shard_map/attn_fwd/pallas_call | solution.py:210
  49.6 16.5 %attn_fwd.5.a_ref = f32[2,72,1024]{2,1,0:T(8,128)} custom-call(s32[2]{0:T(128)} %pad_add_fusion.len_ref, bf16[384,1024]{1,0:T(8,128)(2,1)} %copy-done.62, bf16[4096,384]{1,0:T(8,128)(2,1)} %get-tuple-element.64.k_ref, bf16[384,4096]{1,0:T(8,128)(2,1)} %get-tuple-element.65.vt_ref), custom_call_target="tpu_custom_call" | custom-call | flops 8589934592 | bytes 4194304 | tf_op jit(solution)/shard_map/attn_fwd/pallas_call | solution.py:210
  66.1 16.6 %attn_fwd.4.a_ref = f32[2,72,1024]{2,1,0:T(8,128)} custom-call(s32[2]{0:T(128)} %pad_add_fusion.len_ref, bf16[384,1024]{1,0:T(8,128)(2,1)} %copy-done.62, bf16[4096,384]{1,0:T(8,128)(2,1)} %get-tuple-element.64.k_ref, bf16[384,4096]{1,0:T(8,128)(2,1)} %get-tuple-element.65.vt_ref), custom_call_target="tpu_custom_call" | custom-call | flops 8589934592 | bytes 4194304 | tf_op jit(solution)/shard_map/attn_fwd/pallas_call | solution.py:210
  82.7 1.5 collective-permute-start.4
  84.2 9.9 %attn_fwd.7.a_ref = f32[2,72,512]{2,1,0:T(8,128)} custom-call(s32[2]{0:T(128)} %pad_add_fusion.len_ref, bf16[384,1024]{1,0:T(8,128)(2,1)} %copy-done.62, bf16[4096,384]{1,0:T(8,128)(2,1)} %get-tuple-element.64.k_ref, bf16[384,4096]{1,0:T(8,128)(2,1)} %get-tuple-element.65.vt_ref), custom_call_target="tpu_custom_call" | custom-call | flops 4294967296 | bytes 4194304 | tf_op jit(solution)/shard_map/attn_fwd/pallas_call | solution.py:210
  94.1 1.5 collective-permute-start.9
  95.6 27.2 %collective-permute-done.7.b_ref = f32[2,72,512]{2,1,0:T(8,128)S(1)} collective-permute-done((f32[2,72,512]{2,1,0:T(8,128)}, f32[2,72,512]{2,1,0:T(8,128)S(1)}, u32[]{:S(2)}, u32[]{:S(2)}) %collective-permute-start.7) | collective-permute-done | bytes 294944 | tf_op jit(solution)/shard_map/ppermute | solution.py:665
  122.8 1.0 copy-done.49
  124.5 1.3 combine.4
  127.6 0.8 fusion.13
  128.4 1.4 collective-permute-start.8
  129.7 1.3 reshape.84.gain_ref
  131.0 8.8 %collective-permute-done.9.x1_ref = f32[256,768]{1,0:T(8,128)} collective-permute-done((f32[256,768]{1,0:T(8,128)S(1)}, f32[256,768]{1,0:T(8,128)}, u32[]{:S(2)}, u32[]{:S(2)}) %collective-permute-start.9) | collective-permute-done | bytes 786464 | tf_op jit(solution)/shard_map/ppermute | solution.py:665
  139.8 1.8 place_rows.1.g_ref
  142.8 0.8 copy-done.45
  143.6 1.5 add_convert_fusion.h_ref
  145.1 21.8 %mlp.1 = (bf16[768,512]{1,0:T(8,128)(2,1)}, bf16[512,768]{1,0:T(8,128)(2,1)}, bf16[512,3072]{1,0:T(8,128)(2,1)}, bf16[512,3072]{1,0:T(8,128)(2,1)}, bf16[3072,51...) custom-call(bf16[512,768]{1,0:T(8,128)(2,1)} %add_convert_fusion.h_ref, ...), custom_call_target="tpu_custom_call" | custom-call | flops 12079595520 | bytes 41943040 | tf_op jit(solution)/shard_map/mlp/pallas_call | solution.py:451
  166.9 0.9 collective-permute-start.10
  168.3 1.3 constant_dynamic-update-slice_fusion.1
  170.0 0.8 fusion.14
  171.7 1.0 copy-done.12
  172.6 0.9 copy-done.11
  173.6 22.4 %attn_bwd.3 = (bf16[2,256,2048]{2,1,0:T(8,128)(2,1)S(1)}, f32[2,64,1024]{2,1,0:T(8,128)}) custom-call(s32[2]{0:T(128)S(1)} %copy-done.65, bf16[384,1024]{1,0:T(8,128)(2,1)S(1)} %copy-done.63, bf16[384,1024]{1,0:T(8,128)(2,1)S(1)} %get-tuple-element.107.dot_ref, f32[6,1,1024]{2,1,0:T(1,128)S(1)} %maximum_maximum_fusion.1.lse_ref, ...), custom_call_target="tpu_custom_call" | custom-call | flops 16777216000 | bytes 8388608 | tf_op jit(solution)/shard_map/attn_bwd/pallas_call | solution.py:298
  195.9 4.8 %pair_weights.3.refs_0_ = f32[256,768]{1,0:T(8,128)S(1)} custom-call(bf16[2,256,2048]{2,1,0:T(8,128)(2,1)S(1)} %get-tuple-element.82.dkv_ref.a0_ref, bf16[2048,768]{1,0:T(8,128)(2,1)S(1)} %copy-done.2, bf16[2048,768]{1,0:T(8,128)(2,1)} %collective-permute-done.3.m_ref.m1_ref), custom_call_target="tpu_custom_call" | custom-call | flops 1610612736 | bytes 8388608 | tf_op jit(solution)/shard_map/pair_weights/pallas_call | solution.py:330
  201.2 1.7 collective-permute-start.11
  203.0 21.2 %attn_bwd.4 = (bf16[2,256,2048]{2,1,0:T(8,128)(2,1)S(1)}, f32[2,64,1024]{2,1,0:T(8,128)S(1)}) custom-call(s32[2]{0:T(128)S(1)} %copy-done.65, bf16[384,1024]{1,0:T(8,128)(2,1)S(1)} %copy-done.64, bf16[384,1024]{1,0:T(8,128)(2,1)S(1)} %get-tuple-element.107.dot_ref, f32[6,1,1024]{2,1,0:T(1,128)S(1)} %maximum_maximum_fusion.1.lse_ref, ...), custom_call_target="tpu_custom_call" | custom-call | flops 16777216000 | bytes 8388608 | tf_op jit(solution)/shard_map/attn_bwd/pallas_call | solution.py:298
  225.0 4.8 %pair_weights.4.refs_1_ = f32[256,768]{1,0:T(8,128)S(1)} custom-call(bf16[2,256,2048]{2,1,0:T(8,128)(2,1)S(1)} %get-tuple-element.85.dkv_ref.a1_ref, bf16[2048,768]{1,0:T(8,128)(2,1)S(1)} %copy-done.2, bf16[2048,768]{1,0:T(8,128)(2,1)} %collective-permute-done.3.m_ref.m1_ref), custom_call_target="tpu_custom_call" | custom-call | flops 1610612736 | bytes 8388608 | tf_op jit(solution)/shard_map/pair_weights/pallas_call | solution.py:330
  229.9 22.1 %attn_bwd.5 = (bf16[2,256,2048]{2,1,0:T(8,128)(2,1)S(1)}, f32[2,64,1024]{2,1,0:T(8,128)}) custom-call(s32[2]{0:T(128)S(1)} %copy-done.65, bf16[384,1024]{1,0:T(8,128)(2,1)S(1)} %copy-done.64, bf16[384,1024]{1,0:T(8,128)(2,1)S(1)} %copy-done.34, f32[6,1,1024]{2,1,0:T(1,128)S(1)} %maximum_maximum_fusion.1.lse_ref, f32[6,1,1024]{2,1,0:T(1,128)S(1)} %broadcast_in_dim.3.dl_ref, ...), custom_call_target="tpu_custom_call" | custom-call | flops 16777216000 | bytes 8388608 | tf_op jit(solution)/shard_map/attn_bwd/pallas_call | solution.py:298
  252.0 1.5 collective-permute-start.13
  253.5 4.8 %pair_weights.5.refs_2_ = f32[256,768]{1,0:T(8,128)S(1)} custom-call(bf16[2,256,2048]{2,1,0:T(8,128)(2,1)S(1)} %get-tuple-element.91.a2_ref.dkv_ref, bf16[2048,768]{1,0:T(8,128)(2,1)S(1)} %copy-done.2, bf16[2048,768]{1,0:T(8,128)(2,1)} %collective-permute-done.3.m_ref.m1_ref), custom_call_target="tpu_custom_call" | custom-call | flops 1610612736 | bytes 8388608 | tf_op jit(solution)/shard_map/pair_weights/pallas_call | solution.py:330
  258.4 7.0 %collective-permute-done.12.b1_ref = f32[2,64,1024]{2,1,0:T(8,128)S(1)} collective-permute-done((f32[2,64,1024]{2,1,0:T(8,128)}, f32[2,64,1024]{2,1,0:T(8,128)S(1)}, u32[]{:S(2)}, u32[]{:S(2)}) %collective-permute-start.12) | collective-permute-done | bytes 524320 | tf_op jit(solution)/shard_map/ppermute | solution.py:665
  265.4 1.9 collective-permute-start.20
  267.3 9.4 %collective-permute-done.13.b2_ref = f32[2,64,1024]{2,1,0:T(8,128)S(1)} collective-permute-done((f32[2,64,1024]{2,1,0:T(8,128)}, f32[2,64,1024]{2,1,0:T(8,128)S(1)}, u32[]{:S(2)}, u32[]{:S(2)}) %collective-permute-start.13) | collective-permute-done | bytes 524320 | tf_op jit(solution)/shard_map/ppermute | solution.py:665
  277.0 1.6 collective-permute-start.19
  278.7 14.8 %collective-permute-done.23.refs_8_ = f32[256,768]{1,0:T(8,128)S(1)} collective-permute-done((f32[256,768]{1,0:T(8,128)S(1)}, f32[256,768]{1,0:T(8,128)S(1)}, u32[]{:S(2)}, u32[]{:S(2)}) %collective-permute-start.23) | collective-permute-done | bytes 786464 | tf_op jit(solution)/shard_map/ppermute | solution.py:665
  293.5 1.9 collective-permute-start.16
  295.5 1.0 copy-done.21
  296.5 13.8 %collective-permute-done.22.refs_7_ = f32[256,768]{1,0:T(8,128)S(1)} collective-permute-done((f32[256,768]{1,0:T(8,128)S(1)}, f32[256,768]{1,0:T(8,128)S(1)}, u32[]{:S(2)}, u32[]{:S(2)}) %collective-permute-start.22) | collective-permute-done | bytes 786464 | tf_op jit(solution)/shard_map/ppermute | solution.py:665
  310.4 1.1 collective-permute-start.31
  312.1 1.5 sum_queries.1.mine_ref
  314.1 13.0 %collective-permute-done.14.near_ref = bf16[384,1024]{1,0:T(8,128)(2,1)S(1)} collective-permute-done((bf16[384,1024]{1,0:T(8,128)(2,1)S(1)}, bf16[384,1024]{1,0:T(8,128)(2,1)S(1)}, u32[]{:S(2)}, u32[]{:S(2)}) %collective-permute-start.14) | collective-permute-done | bytes 786464 | tf_op jit(solution)/shard_map/ppermute | solution.py:662
  328.3 0.9 copy-done.27
  330.3 1.2 collective-permute-done.25.refs_10_
  331.5 0.9 copy-done.31
  332.7 3.8 out_proj_grad.1
  336.6 7.5 %memory_grad.1 = f32[2048,768]{1,0:T(8,128)} custom-call(s32[1]{0:T(128)} %bitcast.4.core_ref, bf16[2,256,2048]{2,1,0:T(8,128)(2,1)S(1)} %get-tuple-element.82.dkv_ref.a0_ref, bf16[2,256,2048]{2,1,0:T(8,128)(2,1)S(1)} %get-tuple-element.85.dkv_ref.a1_ref, bf16[2,256,2048]{2,1,0:T(8,128)(2,1)S(1)} %get-tuple-element.91.a2_ref.dkv_ref, ...), custom_call_target="tpu_custom_call" | custom-call | flops 4831838208 | bytes 16777216 | tf_op jit(solution)/shard_map/memory_grad/pallas_call | solution.py:510
  344.1 5.6 %query_grad.1 = (f32[768,768]{1,0:T(8,128)}, f32[256,768]{1,0:T(8,128)}, f32[1,768]{1,0:T(1,128)S(1)}) custom-call(s32[5]{0:T(128)S(1)} %stack.32.place_ref, bf16[384,1024]{1,0:T(8,128)(2,1)S(1)} %sum_queries.1.mine_ref, bf16[384,1024]{1,0:T(8,128)(2,1)S(1)} %collective-permute-done.14.near_ref, bf16[1024,768]{1,0:T(8,128)(2,1)S(1)} %copy-done.61, ...), custom_call_target="tpu_custom_call" | custom-call | flops 2415919104 | bytes 10485760 | tf_op jit(solution)/shard_map/query_grad/pallas_call | solution.py:593
  350.3 1.1 copy-done.22
  351.4 1.1 copy-done.24
  352.6 1.1 copy-done.26
  353.7 1.1 copy-done.28
  354.8 1.1 copy-done.30
  356.0 1.1 copy-done.32
  357.1 4.6 %key_weights.1 = (f32[768,768]{1,0:T(8,128)}, f32[768,768]{1,0:T(8,128)}) custom-call(s32[1]{0:T(128)} %bitcast.4.core_ref, f32[256,768]{1,0:T(8,128)S(1)} %copy-done.6, f32[256,768]{1,0:T(8,128)S(1)} %copy-done.8, f32[256,768]{1,0:T(8,128)S(1)} %copy-done.10, f32[256,768]{1,0:T(8,128)} %collective-permute-done.18.refs_3_, f32[256,768]{1,0:T(8,128)S(1)} %copy-done.26, ...), custom_call_target="tpu_custom_call" | custom-call | flops 1179648 | bytes 10485760 | tf_op jit(solution)/shard_map/key_weights/pallas_call | solution.py:624
  361.8 21.4 %mlp_weights.1 = (f32[768,3072]{1,0:T(8,128)}, f32[768,3072]{1,0:T(8,128)}, f32[3072,768]{1,0:T(8,128)}) custom-call(bf16[768,512]{1,0:T(8,128)(2,1)} %get-tuple-element.97.n2t_ref, bf16[512,768]{1,0:T(8,128)(2,1)} %get-tuple-element.98.gt_ref, bf16[512,3072]{1,0:T(8,128)(2,1)} %get-tuple-element.99.dgate_ref, bf16[512,3072]{1,0:T(8,128)(2,1)} %get-tuple-element.100.dup_ref, ...), custom_call_target="tpu_custom_call" | custom-call | flops 14495514624 | bytes 52428800 | tf_op jit(solution)/shard_map/mlp_weights/pallas_call | solution.py:481
  (184 shorter events, 14.2 us)
Async XLA Ops:
  0.6 141.0 %copy-start = (bf16[12,64,768]{2,1,0:T(8,128)(2,1)S(1)}, bf16[12,64,768]{2,1,0:T(8,128)(2,1)}, u32[]{:S(2)}) copy-start(bf16[12,64,768]{2,1,0:T(8,128)(2,1)} %param.21) | copy-start | bytes 3538948
  0.7 30.2 %collective-permute-start.3 = (bf16[2048,768]{1,0:T(8,128)(2,1)}, bf16[2048,768]{1,0:T(8,128)(2,1)}, u32[]{:S(2)}, u32[]{:S(2)}) collective-permute-start(bf16[2048,768]{1,0:T(8,128)(2,1)} %m0_ref.5), channel_id=1, source_target_pairs={{0,1},{1,0},{2,3},{3,2},{4,5},{5,4},{6,7},{7,6}} | collective-permute-start | bytes 9437192 | tf_op jit(solution)/shard_map/ppermute | solution.py:662
  1.4 10.8 %collective-permute-start.1 = (bf16[256,768]{1,0:T(8,128)(2,1)}, bf16[256,768]{1,0:T(8,128)(2,1)S(1)}, u32[]{:S(2)}, u32[]{:S(2)}) collective-permute-start(bf16[256,768]{1,0:T(8,128)(2,1)} %x0_ref.2), channel_id=1, source_target_pairs={{0,2},{1,3},{2,0},{3,1},{4,6},{5,7},{6,4},{7,5}} | collective-permute-start | bytes 1179656 | tf_op jit(solution)/shard_map/ppermute | solution.py:665
  2.6 21.4 %collective-permute-start = (bf16[256,768]{1,0:T(8,128)(2,1)}, bf16[256,768]{1,0:T(8,128)(2,1)S(1)}, u32[]{:S(2)}, u32[]{:S(2)}) collective-permute-start(bf16[256,768]{1,0:T(8,128)(2,1)} %x0_ref.2), channel_id=1, source_target_pairs={{0,1},{1,0},{2,3},{3,2},{4,5},{5,4},{6,7},{7,6}} | collective-permute-start | bytes 1179656 | tf_op jit(solution)/shard_map/ppermute | solution.py:662
  12.2 11.8 %collective-permute-start.2 = (bf16[256,768]{1,0:T(8,128)(2,1)S(1)}, bf16[256,768]{1,0:T(8,128)(2,1)S(1)}, u32[]{:S(2)}, u32[]{:S(2)}) collective-permute-start(bf16[256,768]{1,0:T(8,128)(2,1)S(1)} %collective-permute-done.1.x2_ref), channel_id=1, source_target_pairs={{0,1},{1,0},{2,3},{3,2},{4,5},{5,4},{6,7},{7,6}} | collective-permute-start | bytes 1179656 | tf_op jit(solution)/shard_map/ppermute | solution.py:662
  15.2 8.8 %copy-start.17 = (bf16[768,12,64]{0,2,1:T(8,128)(2,1)S(1)}, bf16[768,12,64]{0,2,1:T(8,128)(2,1)}, u32[]{:S(2)}) copy-start(bf16[768,12,64]{0,2,1:T(8,128)(2,1)} %param.18) | copy-start | bytes 3538948
  15.2 8.9 %copy-start.47 = (bf16[256,768]{1,0:T(8,128)(2,1)S(1)}, bf16[256,768]{1,0:T(8,128)(2,1)}, u32[]{:S(2)}) copy-start(bf16[256,768]{1,0:T(8,128)(2,1)} %x0_ref.2) | copy-start | bytes 1179652
  66.1 16.6 %copy-start.48 = (f32[2,72,512]{2,1,0:T(8,128)S(1)}, f32[2,72,512]{2,1,0:T(8,128)}, u32[]{:S(2)}) copy-start(f32[2,72,512]{2,1,0:T(8,128)} %attn_fwd.6.a_ref) | copy-start | bytes 884740
  66.1 18.1 %copy-start.36 = (f32[2,72,1024]{2,1,0:T(8,128)S(1)}, f32[2,72,1024]{2,1,0:T(8,128)}, u32[]{:S(2)}) copy-start(f32[2,72,1024]{2,1,0:T(8,128)} %attn_fwd.5.a_ref) | copy-start | bytes 1769476
  82.7 11.4 %copy-start.35 = (f32[256,768]{1,0:T(8,128)S(1)}, f32[256,768]{1,0:T(8,128)}, u32[]{:S(2)}) copy-start(f32[256,768]{1,0:T(8,128)} %x0_ref.3) | copy-start | bytes 2359300
  82.7 12.9 %collective-permute-start.6 = (f32[2,72,512]{2,1,0:T(8,128)S(1)}, f32[2,72,512]{2,1,0:T(8,128)S(1)}, u32[]{:S(2)}, u32[]{:S(2)}) collective-permute-start(f32[2,72,512]{2,1,0:T(8,128)S(1)} %copy-done.48), channel_id=1, source_target_pairs={{0,2},{1,3},{2,0},{3,1},{4,6},{5,7},{6,4},{7,5}} | collective-permute-start | bytes 884744 | tf_op jit(solution)/shard_map/ppermute | solution.py:665
  82.7 41.8 %collective-permute-start.4 = (f32[2,72,1024]{2,1,0:T(8,128)}, f32[2,72,1024]{2,1,0:T(8,128)}, u32[]{:S(2)}, u32[]{:S(2)}) collective-permute-start(f32[2,72,1024]{2,1,0:T(8,128)} %attn_fwd.4.a_ref), channel_id=1, source_target_pairs={{0,2},{1,3},{2,0},{3,1},{4,6},{5,7},{6,4},{7,5}} | collective-permute-start | bytes 1769480 | tf_op jit(solution)/shard_map/ppermute | solution.py:665
  84.1 42.4 %collective-permute-start.5 = (f32[2,72,1024]{2,1,0:T(8,128)S(1)}, f32[2,72,1024]{2,1,0:T(8,128)S(1)}, u32[]{:S(2)}, u32[]{:S(2)}) collective-permute-start(f32[2,72,1024]{2,1,0:T(8,128)S(1)} %copy-done.36), channel_id=1, source_target_pairs={{0,2},{1,3},{2,0},{3,1},{4,6},{5,7},{6,4},{7,5}} | collective-permute-start | bytes 1769480 | tf_op jit(solution)/shard_map/ppermute | solution.py:665
  94.1 30.4 %copy-start.37 = (f32[2,72,1024]{2,1,0:T(8,128)S(1)}, f32[2,72,1024]{2,1,0:T(8,128)}, u32[]{:S(2)}) copy-start(f32[2,72,1024]{2,1,0:T(8,128)} %attn_fwd.4.a_ref) | copy-start | bytes 1769476
  94.1 28.8 %collective-permute-start.7 = (f32[2,72,512]{2,1,0:T(8,128)}, f32[2,72,512]{2,1,0:T(8,128)S(1)}, u32[]{:S(2)}, u32[]{:S(2)}) collective-permute-start(f32[2,72,512]{2,1,0:T(8,128)} %attn_fwd.7.a_ref), channel_id=1, source_target_pairs={{0,2},{1,3},{2,0},{3,1},{4,6},{5,7},{6,4},{7,5}} | collective-permute-start | bytes 884744 | tf_op jit(solution)/shard_map/ppermute | solution.py:665
  94.1 45.7 %collective-permute-start.9 = (f32[256,768]{1,0:T(8,128)S(1)}, f32[256,768]{1,0:T(8,128)}, u32[]{:S(2)}, u32[]{:S(2)}) collective-permute-start(f32[256,768]{1,0:T(8,128)S(1)} %copy-done.35), channel_id=1, source_target_pairs={{0,2},{1,3},{2,0},{3,1},{4,6},{5,7},{6,4},{7,5}} | collective-permute-start | bytes 2359304 | tf_op jit(solution)/shard_map/ppermute | solution.py:665
  95.6 28.3 %copy-start.56 = (f32[2,1,512]{2,1,0:T(1,128)}, f32[2,1,512]{2,1,0:T(1,128)S(1)}, u32[]{:S(2)}) copy-start(f32[2,1,512]{2,1,0:T(1,128)S(1)} %get-tuple-element.73) | copy-start | bytes 12292
  95.6 32.0 %copy-start.50 = (f32[2,64,512]{2,1,0:T(8,128)}, f32[2,64,512]{2,1,0:T(8,128)S(1)}, u32[]{:S(2)}) copy-start(f32[2,64,512]{2,1,0:T(8,128)S(1)} %get-tuple-element.77) | copy-start | bytes 786436
  128.4 13.9 %collective-permute-start.8 = (bf16[384,512]{1,0:T(8,128)(2,1)S(1)}, bf16[384,512]{1,0:T(8,128)(2,1)S(1)}, u32[]{:S(2)}, u32[]{:S(2)}) collective-permute-start(bf16[384,512]{1,0:T(8,128)(2,1)S(1)} %get-tuple-element.106), channel_id=1, source_target_pairs={{0,1},{1,0},{2,3},{3,2},{4,5},{5,4},{6,7},{7,6}} | collective-permute-start | bytes 1179656 | tf_op jit(solution)/shard_map/ppermute | solution.py:662
  145.1 22.7 %copy-start.55 = (f32[2,1,1024]{2,1,0:T(1,128)S(1)}, f32[2,1,1024]{2,1,0:T(1,128)}, u32[]{:S(2)}) copy-start(f32[2,1,1024]{2,1,0:T(1,128)} %copy-done.54) | copy-start | bytes 24580
  145.1 22.7 %copy-start.57 = (f32[2,1,512]{2,1,0:T(1,128)S(1)}, f32[2,1,512]{2,1,0:T(1,128)}, u32[]{:S(2)}) copy-start(f32[2,1,512]{2,1,0:T(1,128)} %copy-done.56) | copy-start | bytes 12292
  145.1 22.7 %copy-start.59 = (f32[2,1,512]{2,1,0:T(1,128)S(1)}, f32[2,1,512]{2,1,0:T(1,128)}, u32[]{:S(2)}) copy-start(f32[2,1,512]{2,1,0:T(1,128)} %copy-done.58) | copy-start | bytes 12292
  145.1 25.7 %copy-start.53 = (f32[2,64,512]{2,1,0:T(8,128)S(1)}, f32[2,64,512]{2,1,0:T(8,128)}, u32[]{:S(2)}) copy-start(f32[2,64,512]{2,1,0:T(8,128)} %copy-done.52) | copy-start | bytes 786436
  145.1 26.5 %copy-start.63 = (bf16[384,1024]{1,0:T(8,128)(2,1)S(1)}, bf16[384,1024]{1,0:T(8,128)(2,1)}, u32[]{:S(2)}) copy-start(bf16[384,1024]{1,0:T(8,128)(2,1)} %copy-done.62) | copy-start | bytes 2359300
  166.9 3.0 collective-permute-start.10
  167.8 84.3 %collective-permute-start.27 = (bf16[384,512]{1,0:T(8,128)(2,1)}, bf16[384,512]{1,0:T(8,128)(2,1)}, u32[]{:S(2)}, u32[]{:S(2)}) collective-permute-start(bf16[384,512]{1,0:T(8,128)(2,1)} %get-tuple-element.105), channel_id=1, source_target_pairs={{0,1},{1,0},{2,3},{3,2},{4,5},{5,4},{6,7},{7,6}} | collective-permute-start | bytes 1179656 | tf_op jit(solution)/shard_map/ppermute | solution.py:662
  167.8 84.2 %collective-permute-start.28 = (f32[1,768]{1,0:T(1,128)}, f32[1,768]{1,0:T(1,128)S(1)}, u32[]{:S(2)}, u32[]{:S(2)}) collective-permute-start(f32[1,768]{1,0:T(1,128)} %get-tuple-element.96), channel_id=1, source_target_pairs={{0,1},{1,0},{2,3},{3,2},{4,5},{5,4},{6,7},{7,6}} | collective-permute-start | bytes 9224 | tf_op jit(solution)/shard_map/ppermute | solution.py:662
  170.8 32.2 %copy-start.33 = (bf16[384,1024]{1,0:T(8,128)(2,1)}, bf16[384,1024]{1,0:T(8,128)(2,1)S(1)}, u32[]{:S(2)}) copy-start(bf16[384,1024]{1,0:T(8,128)(2,1)S(1)} %get-tuple-element.107.dot_ref) | copy-start | bytes 2359300
  173.5 22.4 %copy-start.2 = (bf16[2048,768]{1,0:T(8,128)(2,1)S(1)}, bf16[2048,768]{1,0:T(8,128)(2,1)}, u32[]{:S(2)}) copy-start(bf16[2048,768]{1,0:T(8,128)(2,1)} %m0_ref.5) | copy-start | bytes 9437188
  195.9 7.0 %copy-start.64 = (bf16[384,1024]{1,0:T(8,128)(2,1)S(1)}, bf16[384,1024]{1,0:T(8,128)(2,1)}, u32[]{:S(2)}) copy-start(bf16[384,1024]{1,0:T(8,128)(2,1)} %copy-done.62) | copy-start | bytes 2359300
  200.8 23.4 %copy-start.5 = (f32[256,768]{1,0:T(8,128)}, f32[256,768]{1,0:T(8,128)S(1)}, u32[]{:S(2)}) copy-start(f32[256,768]{1,0:T(8,128)S(1)} %pair_weights.3.refs_0_) | copy-start | bytes 2359300
  200.8 76.2 %collective-permute-start.21 = (f32[256,768]{1,0:T(8,128)S(1)}, f32[256,768]{1,0:T(8,128)}, u32[]{:S(2)}, u32[]{:S(2)}) collective-permute-start(f32[256,768]{1,0:T(8,128)S(1)} %pair_weights.3.refs_0_), channel_id=1, source_target_pairs={{0,2},{1,3},{2,0},{3,1},{4,6},{5,7},{6,4},{7,5}} | collective-permute-start | bytes 2359304 | tf_op jit(solution)/shard_map/ppermute | solution.py:665
  200.8 77.8 %collective-permute-start.18 = (f32[256,768]{1,0:T(8,128)S(1)}, f32[256,768]{1,0:T(8,128)}, u32[]{:S(2)}, u32[]{:S(2)}) collective-permute-start(f32[256,768]{1,0:T(8,128)S(1)} %pair_weights.3.refs_0_), channel_id=1, source_target_pairs={{0,1},{1,0},{2,3},{3,2},{4,5},{5,4},{6,7},{7,6}} | collective-permute-start | bytes 2359304 | tf_op jit(solution)/shard_map/ppermute | solution.py:662
  201.2 57.1 %collective-permute-start.11 = (f32[2,64,1024]{2,1,0:T(8,128)}, f32[2,64,1024]{2,1,0:T(8,128)}, u32[]{:S(2)}, u32[]{:S(2)}) collective-permute-start(f32[2,64,1024]{2,1,0:T(8,128)} %get-tuple-element.81.a0_ref), channel_id=1, source_target_pairs={{0,2},{1,3},{2,0},{3,1},{4,6},{5,7},{6,4},{7,5}} | collective-permute-start | bytes 1572872 | tf_op jit(solution)/shard_map/ppermute | solution.py:665
  229.9 47.1 %copy-start.7 = (f32[256,768]{1,0:T(8,128)}, f32[256,768]{1,0:T(8,128)S(1)}, u32[]{:S(2)}) copy-start(f32[256,768]{1,0:T(8,128)S(1)} %pair_weights.4.refs_1_) | copy-start | bytes 2359300
  252.0 13.4 %collective-permute-start.12 = (f32[2,64,1024]{2,1,0:T(8,128)}, f32[2,64,1024]{2,1,0:T(8,128)S(1)}, u32[]{:S(2)}, u32[]{:S(2)}) collective-permute-start(f32[2,64,1024]{2,1,0:T(8,128)} %copy-done.38), channel_id=1, source_target_pairs={{0,2},{1,3},{2,0},{3,1},{4,6},{5,7},{6,4},{7,5}} | collective-permute-start | bytes 1572872 | tf_op jit(solution)/shard_map/ppermute | solution.py:665
  252.0 24.6 %collective-permute-start.13 = (f32[2,64,1024]{2,1,0:T(8,128)}, f32[2,64,1024]{2,1,0:T(8,128)S(1)}, u32[]{:S(2)}, u32[]{:S(2)}) collective-permute-start(f32[2,64,1024]{2,1,0:T(8,128)} %get-tuple-element.87.a2_ref), channel_id=1, source_target_pairs={{0,2},{1,3},{2,0},{3,1},{4,6},{5,7},{6,4},{7,5}} | collective-permute-start | bytes 1572872 | tf_op jit(solution)/shard_map/ppermute | solution.py:665
  258.3 20.4 %copy-start.9 = (f32[256,768]{1,0:T(8,128)}, f32[256,768]{1,0:T(8,128)S(1)}, u32[]{:S(2)}) copy-start(f32[256,768]{1,0:T(8,128)S(1)} %pair_weights.5.refs_2_) | copy-start | bytes 2359300
  258.3 35.2 %collective-permute-start.23 = (f32[256,768]{1,0:T(8,128)S(1)}, f32[256,768]{1,0:T(8,128)S(1)}, u32[]{:S(2)}, u32[]{:S(2)}) collective-permute-start(f32[256,768]{1,0:T(8,128)S(1)} %pair_weights.5.refs_2_), channel_id=1, source_target_pairs={{0,2},{1,3},{2,0},{3,1},{4,6},{5,7},{6,4},{7,5}} | collective-permute-start | bytes 2359304 | tf_op jit(solution)/shard_map/ppermute | solution.py:665
  265.4 30.0 %collective-permute-start.20 = (f32[256,768]{1,0:T(8,128)S(1)}, f32[256,768]{1,0:T(8,128)S(1)}, u32[]{:S(2)}, u32[]{:S(2)}) collective-permute-start(f32[256,768]{1,0:T(8,128)S(1)} %pair_weights.5.refs_2_), channel_id=1, source_target_pairs={{0,1},{1,0},{2,3},{3,2},{4,5},{5,4},{6,7},{7,6}} | collective-permute-start | bytes 2359304 | tf_op jit(solution)/shard_map/ppermute | solution.py:662
  276.7 33.7 %collective-permute-start.22 = (f32[256,768]{1,0:T(8,128)S(1)}, f32[256,768]{1,0:T(8,128)S(1)}, u32[]{:S(2)}, u32[]{:S(2)}) collective-permute-start(f32[256,768]{1,0:T(8,128)S(1)} %pair_weights.4.refs_1_), channel_id=1, source_target_pairs={{0,2},{1,3},{2,0},{3,1},{4,6},{5,7},{6,4},{7,5}} | collective-permute-start | bytes 2359304 | tf_op jit(solution)/shard_map/ppermute | solution.py:665
  277.0 34.6 %collective-permute-start.19 = (f32[256,768]{1,0:T(8,128)S(1)}, f32[256,768]{1,0:T(8,128)S(1)}, u32[]{:S(2)}, u32[]{:S(2)}) collective-permute-start(f32[256,768]{1,0:T(8,128)S(1)} %pair_weights.4.refs_1_), channel_id=1, source_target_pairs={{0,1},{1,0},{2,3},{3,2},{4,5},{5,4},{6,7},{7,6}} | collective-permute-start | bytes 2359304 | tf_op jit(solution)/shard_map/ppermute | solution.py:662
  278.6 33.0 %collective-permute-start.15 = (bf16[256,2048]{1,0:T(8,128)(2,1)S(1)}, bf16[256,2048]{1,0:T(8,128)(2,1)S(1)}, u32[]{:S(2)}, u32[]{:S(2)}) collective-permute-start(bf16[256,2048]{1,0:T(8,128)(2,1)S(1)} %slice_bitcast_fusion.2), channel_id=1, source_target_pairs={{0,1},{1,0},{2,3},{3,2},{4,5},{5,4},{6,7},{7,6}} | collective-permute-start | bytes 3145736 | tf_op jit(solution)/shard_map/ppermute | solution.py:662
  278.7 33.3 %copy-start.39 = (f32[2,64,1024]{2,1,0:T(8,128)S(1)}, f32[2,64,1024]{2,1,0:T(8,128)}, u32[]{:S(2)}) copy-start(f32[2,64,1024]{2,1,0:T(8,128)} %copy-done.38) | copy-start | bytes 1572868
  293.5 33.6 %copy-start.19 = (f32[256,768]{1,0:T(8,128)}, f32[256,768]{1,0:T(8,128)S(1)}, u32[]{:S(2)}) copy-start(f32[256,768]{1,0:T(8,128)S(1)} %collective-permute-done.23.refs_8_) | copy-start | bytes 2359300
  293.5 20.0 %collective-permute-start.16 = (bf16[256,2048]{1,0:T(8,128)(2,1)S(1)}, bf16[256,2048]{1,0:T(8,128)(2,1)S(1)}, u32[]{:S(2)}, u32[]{:S(2)}) collective-permute-start(bf16[256,2048]{1,0:T(8,128)(2,1)S(1)} %slice_bitcast_fusion.1), channel_id=1, source_target_pairs={{0,1},{1,0},{2,3},{3,2},{4,5},{5,4},{6,7},{7,6}} | collective-permute-start | bytes 3145736 | tf_op jit(solution)/shard_map/ppermute | solution.py:662
  296.5 17.2 %collective-permute-start.17 = (bf16[256,2048]{1,0:T(8,128)(2,1)S(1)}, bf16[256,2048]{1,0:T(8,128)(2,1)S(1)}, u32[]{:S(2)}, u32[]{:S(2)}) collective-permute-start(bf16[256,2048]{1,0:T(8,128)(2,1)S(1)} %slice_bitcast_fusion), channel_id=1, source_target_pairs={{0,1},{1,0},{2,3},{3,2},{4,5},{5,4},{6,7},{7,6}} | collective-permute-start | bytes 3145736 | tf_op jit(solution)/shard_map/ppermute | solution.py:662
  310.4 17.9 %copy-start.23 = (f32[256,768]{1,0:T(8,128)}, f32[256,768]{1,0:T(8,128)S(1)}, u32[]{:S(2)}) copy-start(f32[256,768]{1,0:T(8,128)S(1)} %collective-permute-done.22.refs_7_) | copy-start | bytes 2359300
  310.4 51.3 %collective-permute-start.31 = (bf16[512,3072]{1,0:T(8,128)(2,1)}, bf16[512,3072]{1,0:T(8,128)(2,1)}, u32[]{:S(2)}, u32[]{:S(2)}) collective-permute-start(bf16[512,3072]{1,0:T(8,128)(2,1)} %get-tuple-element.99.dgate_ref), channel_id=1, source_target_pairs={{0,1},{1,0},{2,3},{3,2},{4,5},{5,4},{6,7},{7,6}} | collective-permute-start | bytes 9437192 | tf_op jit(solution)/shard_map/ppermute | solution.py:662
  311.5 50.2 %collective-permute-start.32 = (bf16[512,3072]{1,0:T(8,128)(2,1)}, bf16[512,3072]{1,0:T(8,128)(2,1)}, u32[]{:S(2)}, u32[]{:S(2)}) collective-permute-start(bf16[512,3072]{1,0:T(8,128)(2,1)} %get-tuple-element.100.dup_ref), channel_id=1, source_target_pairs={{0,1},{1,0},{2,3},{3,2},{4,5},{5,4},{6,7},{7,6}} | collective-permute-start | bytes 9437192 | tf_op jit(solution)/shard_map/ppermute | solution.py:662
  311.6 18.0 %copy-start.67 = (f32[1,768]{1,0:T(1,128)S(1)}, f32[1,768]{1,0:T(1,128)}, u32[]{:S(2)}) copy-start(f32[1,768]{1,0:T(1,128)} %get-tuple-element.96) | copy-start | bytes 9220
  311.6 21.2 %copy-start.15 = (bf16[384,512]{1,0:T(8,128)(2,1)S(1)}, bf16[384,512]{1,0:T(8,128)(2,1)}, u32[]{:S(2)}) copy-start(bf16[384,512]{1,0:T(8,128)(2,1)} %copy-done.14) | copy-start | bytes 1179652
  311.6 50.2 %collective-permute-start.33 = (bf16[3072,512]{1,0:T(8,128)(2,1)}, bf16[3072,512]{1,0:T(8,128)(2,1)}, u32[]{:S(2)}, u32[]{:S(2)}) collective-permute-start(bf16[3072,512]{1,0:T(8,128)(2,1)} %get-tuple-element.101.ut_ref), channel_id=1, source_target_pairs={{0,1},{1,0},{2,3},{3,2},{4,5},{5,4},{6,7},{7,6}} | collective-permute-start | bytes 9437192 | tf_op jit(solution)/shard_map/ppermute | solution.py:662
  313.6 13.6 %collective-permute-start.14 = (bf16[384,1024]{1,0:T(8,128)(2,1)S(1)}, bf16[384,1024]{1,0:T(8,128)(2,1)S(1)}, u32[]{:S(2)}, u32[]{:S(2)}) collective-permute-start(bf16[384,1024]{1,0:T(8,128)(2,1)S(1)} %sum_queries.1.mine_ref), channel_id=1, source_target_pairs={{0,1},{1,0},{2,3},{3,2},{4,5},{5,4},{6,7},{7,6}} | collective-permute-start | bytes 2359304 | tf_op jit(solution)/shard_map/ppermute | solution.py:662
  313.7 14.6 %collective-permute-start.24 = (f32[256,768]{1,0:T(8,128)}, f32[256,768]{1,0:T(8,128)S(1)}, u32[]{:S(2)}, u32[]{:S(2)}) collective-permute-start(f32[256,768]{1,0:T(8,128)} %collective-permute-done.21.refs_6_), channel_id=1, source_target_pairs={{0,1},{1,0},{2,3},{3,2},{4,5},{5,4},{6,7},{7,6}} | collective-permute-start | bytes 2359304 | tf_op jit(solution)/shard_map/ppermute | solution.py:662
  327.1 3.0 collective-permute-start.26
  329.2 2.3 collective-permute-start.25
  330.2 31.5 %collective-permute-start.29 = (bf16[768,512]{1,0:T(8,128)(2,1)}, bf16[768,512]{1,0:T(8,128)(2,1)}, u32[]{:S(2)}, u32[]{:S(2)}) collective-permute-start(bf16[768,512]{1,0:T(8,128)(2,1)} %get-tuple-element.97.n2t_ref), channel_id=1, source_target_pairs={{0,1},{1,0},{2,3},{3,2},{4,5},{5,4},{6,7},{7,6}} | collective-permute-start | bytes 2359304 | tf_op jit(solution)/shard_map/ppermute | solution.py:662
  332.4 29.4 %collective-permute-start.30 = (bf16[512,768]{1,0:T(8,128)(2,1)}, bf16[512,768]{1,0:T(8,128)(2,1)}, u32[]{:S(2)}, u32[]{:S(2)}) collective-permute-start(bf16[512,768]{1,0:T(8,128)(2,1)} %get-tuple-element.98.gt_ref), channel_id=1, source_target_pairs={{0,1},{1,0},{2,3},{3,2},{4,5},{5,4},{6,7},{7,6}} | collective-permute-start | bytes 2359304 | tf_op jit(solution)/shard_map/ppermute | solution.py:662
  336.5 7.5 %copy-start.18 = (bf16[768,12,64]{0,2,1:T(8,128)(2,1)S(1)}, bf16[768,12,64]{0,2,1:T(8,128)(2,1)}, u32[]{:S(2)}) copy-start(bf16[768,12,64]{0,2,1:T(8,128)(2,1)} %param.18) | copy-start | bytes 3538948
  336.5 7.5 %copy-start.46 = (bf16[1024,768]{1,0:T(8,128)(2,1)S(1)}, bf16[1024,768]{1,0:T(8,128)(2,1)}, u32[]{:S(2)}) copy-start(bf16[1024,768]{1,0:T(8,128)(2,1)} %copy-done.44) | copy-start | bytes 4718596
  336.5 7.5 %copy-start.61 = (bf16[1024,768]{1,0:T(8,128)(2,1)S(1)}, bf16[1024,768]{1,0:T(8,128)(2,1)}, u32[]{:S(2)}) copy-start(bf16[1024,768]{1,0:T(8,128)(2,1)} %copy-done.60) | copy-start | bytes 4718596
  336.6 7.5 %copy-start.66 = (f32[512,768]{1,0:T(8,128)S(1)}, f32[512,768]{1,0:T(8,128)}, u32[]{:S(2)}) copy-start(f32[512,768]{1,0:T(8,128)} %get-tuple-element.89.dh_ref) | copy-start | bytes 4718596
  361.7 21.4 %copy-start.1 = (bf16[12,64,768]{2,1,0:T(8,128)(2,1)S(1)}, bf16[12,64,768]{2,1,0:T(8,128)(2,1)}, u32[]{:S(2)}) copy-start(bf16[12,64,768]{2,1,0:T(8,128)(2,1)} %param.21) | copy-start | bytes 3538948
  (38 other events, 86.6 us)

commit v3 on v2

--- a/solution.py
+++ b/solution.py
@@ -14,9 +14,11 @@
 FQB = 512
 BKB = 512
 BQB = 256
+WKB = 1024
 PAIR = 128
 OROWS = 72
 FFB = 512
+WFB = 1024
 MB = 512
 
 
@@ -32,37 +34,41 @@
     return pl.CostEstimate(flops=int(flops), bytes_accessed=int(bytes_accessed), transcendentals=int(exps))
 
 
-def proj_kernel(core_ref, m_ref, wk_ref, wv_ref, *refs):
-    k_ref, v_ref, kt_ref, vt_ref = refs[-4:]
-    m = m_ref[...]
-    k_ref[...] = dot_nt(m, wk_ref[...]).astype(BF)
-    v_ref[...] = dot_nt(m, wv_ref[...]).astype(BF)
-    kt_ref[...] = dot_nt(wk_ref[...], m).astype(BF)
-    vt_ref[...] = dot_nt(wv_ref[...], m).astype(BF)
-
-
-def project(core, mem, wkt, wvt, seg, before):
+def proj_kernel(core_ref, m0_ref, m1_ref, wk_ref, wv_ref, k_ref, v_ref, kt_ref, vt_ref):
+    step = pl.program_id(0)
+    half = pl.num_programs(0) // 2
+    for seg, m_ref in enumerate((m0_ref, m1_ref)):
+        @pl.when((step >= half) == (seg == 1))
+        def _():
+            m = m_ref[...]
+            k = dot_nt(m, wk_ref[...]).astype(BF)
+            v = dot_nt(m, wv_ref[...]).astype(BF)
+            k_ref[...] = k
+            v_ref[...] = v
+            kt_ref[...] = k.T
+            vt_ref[...] = v.T
+
+
+def project(core, mem, mem_near, wkt, wvt):
     rows, dim = mem.shape
     width = wkt.shape[0] // 2
-    steps = rows // MB
-    base = seg * steps
+    half = rows // MB
     weights = pl.BlockSpec((width, dim), lambda i, s: (s[0], 0))
-    down = pl.BlockSpec((MB, width), lambda i, s: (base + i, 0))
-    across = pl.BlockSpec((width, MB), lambda i, s: (0, base + i))
+    down = pl.BlockSpec((MB, width), lambda i, s: (i, 0))
+    across = pl.BlockSpec((width, MB), lambda i, s: (0, i))
     outs = [jax.ShapeDtypeStruct((2 * rows, width), BF)] * 2 + [jax.ShapeDtypeStruct((width, 2 * rows), BF)] * 2
     return pl.pallas_call(
         proj_kernel,
         out_shape=outs,
         grid_spec=pltpu.PrefetchScalarGridSpec(
-            num_scalar_prefetch=1, grid=(steps,),
-            in_specs=[pl.BlockSpec((MB, dim), lambda i, s: (i, 0)), weights, weights]
-                     + [pl.BlockSpec(memory_space=pl.ANY)] * len(before),
+            num_scalar_prefetch=1, grid=(2 * half,),
+            in_specs=[pl.BlockSpec((MB, dim), lambda i, s: (jnp.minimum(i, half - 1), 0)),
+                      pl.BlockSpec((MB, dim), lambda i, s: (jnp.maximum(i - half, 0), 0)), weights, weights],
             out_specs=[down, down, across, across]),
-        input_output_aliases={4 + i: i for i in range(len(before))},
-        compiler_params=pltpu.CompilerParams(vmem_limit_bytes=60 << 20),
-        cost_estimate=cost(4 * rows * dim * width, 12 << 20),
+        compiler_params=pltpu.CompilerParams(vmem_limit_bytes=24 << 20),
+        cost_estimate=cost(8 * rows * dim * width, 24 << 20),
         name="kv_proj",
-    )(core, mem, wkt, wvt, *before)
+    )(core, mem, mem_near, wkt, wvt)
 
 
 def query_kernel(place_ref, x0_ref, x1_ref, x2_ref, x3_ref, gain_ref, wq_ref, x_ref, n_ref, q_ref, qt_ref):
@@ -211,13 +217,17 @@
         fwd_kernel,
         out_shape=jax.ShapeDtypeStruct((2 * pairs, OROWS, nq), F32),
         grid_spec=spec,
-        compiler_params=pltpu.CompilerParams(vmem_limit_bytes=60 << 20),
+        compiler_params=pltpu.CompilerParams(vmem_limit_bytes=24 << 20),
         cost_estimate=cost(work * 1024, 4 << 20, work),
         name="attn_fwd",
     )(lens, qt, k, vt)
 
 
-def bwd_kernel(len_ref, qt_ref, dot_ref, lse_ref, dl_ref, k_ref, v_ref, kt_ref, dkv_ref, dqt_ref, qzt_ref, dozt_ref):
+def bwd_kernel(len_ref, qt_ref, dot_ref, lse_ref, dl_ref, k_ref, v_ref, kt_ref, m0_ref, m1_ref,
+               dkv0_ref, dkv1_ref, dqt_ref, dw_ref, qzt_ref, dozt_ref, dkv_ref, m_ref, sems):
+    copies = [pltpu.make_async_copy(src, m_ref.at[i], sems.at[i]) for i, src in enumerate((m0_ref, m1_ref))]
+    for copy in copies:
+        copy.start()
     nq = qt_ref.shape[1]
     seg_rows = k_ref.shape[0] // 2
     blocks = seg_rows // BKB
@@ -278,8 +288,20 @@
             cols = pl.ds(pl.multiple_of(j * BKB, BKB), BKB)
             dkv_ref[seg, :, cols] = jnp.zeros((2 * PAIR, BKB), BF)
 
-
-def attention_backward(lens, qt, dot_t, lse, delta, k, v, kt, pair0):
+    dw_ref[...] = jnp.zeros(dw_ref.shape, F32)
+    for seg, copy in enumerate(copies):
+        copy.wait()
+
+        @pl.loop(0, (len_ref[seg] + WKB - 1) // WKB)
+        def _(j):
+            at = pl.ds(pl.multiple_of(j * WKB, WKB), WKB)
+            dw_ref[...] += dot(dkv_ref[seg, :, at], m_ref[seg, at, :])
+
+    dkv0_ref[...] = dkv_ref[0]
+    dkv1_ref[...] = dkv_ref[1]
+
+
+def attention_backward(lens, qt, dot_t, lse, delta, k, v, kt, mem, mem_near, pair0):
     nq = qt.shape[1]
     rows = k.shape[0]
     off = pair0
@@ -290,55 +312,24 @@
     spec = pltpu.PrefetchScalarGridSpec(
         num_scalar_prefetch=1,
         grid=(1,),
-        in_specs=[across, across, stat, stat, keys, keys, keys_t],
-        out_specs=[pl.BlockSpec((2, 2 * PAIR, rows // 2), lambda p, s: (0, 0, 0)),
-                   pl.BlockSpec((2, 64, nq), lambda p, s: (0, 0, 0))],
-        scratch_shapes=[pltpu.VMEM((2, PAIR, nq), BF), pltpu.VMEM((2, PAIR, nq), BF)])
+        in_specs=[across, across, stat, stat, keys, keys, keys_t] + [pl.BlockSpec(memory_space=pltpu.HBM)] * 2,
+        out_specs=[pl.BlockSpec((2 * PAIR, rows // 2), lambda p, s: (0, 0)),
+                   pl.BlockSpec((2 * PAIR, rows // 2), lambda p, s: (0, 0)),
+                   pl.BlockSpec((2, 64, nq), lambda p, s: (0, 0, 0)),
+                   pl.BlockSpec((2 * PAIR, mem.shape[1]), lambda p, s: (0, 0))],
+        scratch_shapes=[pltpu.VMEM((2, PAIR, nq), BF), pltpu.VMEM((2, PAIR, nq), BF),
+                        pltpu.VMEM((2, 2 * PAIR, rows // 2), BF), pltpu.VMEM((2,) + mem.shape, BF),
+                        pltpu.SemaphoreType.DMA((2,))])
     work = 2 * nq * rows
     return pl.pallas_call(
         bwd_kernel,
-        out_shape=[jax.ShapeDtypeStruct((2, 2 * PAIR, rows // 2), BF), jax.ShapeDtypeStruct((2, 64, nq), F32)],
+        out_shape=[jax.ShapeDtypeStruct((2 * PAIR, rows // 2), BF)] * 2
+                  + [jax.ShapeDtypeStruct((2, 64, nq), F32), jax.ShapeDtypeStruct((2 * PAIR, mem.shape[1]), F32)],
         grid_spec=spec,
         compiler_params=pltpu.CompilerParams(vmem_limit_bytes=40 << 20),
         cost_estimate=cost(work * 2000, 8 << 20, work),
         name="attn_bwd",
-    )(lens, qt, dot_t, lse, delta, k, v, kt)
-
-
-def pair_weights_kernel(dkv_ref, m0_ref, m1_ref, o_ref):
-    step = pl.program_id(0)
-    half = pl.num_programs(0) // 2
-
-    @pl.when(step == 0)
-    def _():
-        o_ref[...] = dot(dkv_ref[...], m0_ref[...])
-
-    @pl.when((step > 0) & (step < half))
-    def _():
-        o_ref[...] += dot(dkv_ref[...], m0_ref[...])
-
-    @pl.when(step >= half)
-    def _():
-        o_ref[...] += dot(dkv_ref[...], m1_ref[...])
-
-
-def pair_weights(dkv, mem, mem_near):
-    _, width, rows = dkv.shape
-    dim = mem.shape[1]
-    block = 1024
-    half = rows // block
-    return pl.pallas_call(
-        pair_weights_kernel,
-        grid=(2 * half,),
-        in_specs=[pl.BlockSpec((None, width, block), lambda i: (i // half, 0, i % half)),
-                  pl.BlockSpec((block, dim), lambda i: (jnp.minimum(i, half - 1), 0)),
-                  pl.BlockSpec((block, dim), lambda i: (jnp.maximum(i - half, 0), 0))],
-        out_specs=pl.BlockSpec((width, dim), lambda i: (0, 0)),
-        out_shape=jax.ShapeDtypeStruct((width, dim), F32),
-        compiler_params=pltpu.CompilerParams(vmem_limit_bytes=24 << 20),
-        cost_estimate=cost(4 * rows * dim * width, 8 << 20),
-        name="pair_weights",
-    )(dkv, mem, mem_near)
+    )(lens, qt, dot_t, lse, delta, k, v, kt, mem, mem_near)
 
 
 def combine_kernel(a_ref, b_ref, o_ref, ob_ref, lse_ref):
@@ -475,14 +466,14 @@
     dim, rows = factors[0].shape
     ff = factors[2].shape[1]
     fix = lambda *shape: pl.BlockSpec(shape, lambda i: (0,) * len(shape))
-    act = pl.BlockSpec((rows, FFB), lambda i: (0, i))
-    wide = pl.BlockSpec((dim, FFB), lambda i: (0, i))
-    ins = [fix(dim, rows), fix(rows, dim), act, act, pl.BlockSpec((FFB, rows), lambda i: (i, 0))]
+    act = pl.BlockSpec((rows, WFB), lambda i: (0, i))
+    wide = pl.BlockSpec((dim, WFB), lambda i: (0, i))
+    ins = [fix(dim, rows), fix(rows, dim), act, act, pl.BlockSpec((WFB, rows), lambda i: (i, 0))]
     return pl.pallas_call(
         mlp_weights_kernel,
-        grid=(ff // FFB,),
+        grid=(ff // WFB,),
         in_specs=ins + ins,
-        out_specs=[wide, wide, pl.BlockSpec((FFB, dim), lambda i: (i, 0))],
+        out_specs=[wide, wide, pl.BlockSpec((WFB, dim), lambda i: (i, 0))],
         out_shape=[jax.ShapeDtypeStruct((dim, ff), F32)] * 2 + [jax.ShapeDtypeStruct((ff, dim), F32)],
         compiler_params=pltpu.CompilerParams(vmem_limit_bytes=60 << 20),
         cost_estimate=cost(12 * rows * dim * ff, 50 << 20),
@@ -504,15 +495,14 @@
 def memory_grad(core, mine, near, wkt, wvt):
     rows = mine[0].shape[-1]
     dim = wkt.shape[1]
-    block = pl.BlockSpec((None, 2 * PAIR, MB), lambda i, s: (0, 0, i))
-    block2 = pl.BlockSpec((2 * PAIR, MB), lambda i, s: (0, i))
+    block = pl.BlockSpec((2 * PAIR, MB), lambda i, s: (0, i))
     whole = pl.BlockSpec(wkt.shape, lambda i, s: (0, 0))
     return pl.pallas_call(
         memory_kernel,
         out_shape=jax.ShapeDtypeStruct((rows, dim), F32),
         grid_spec=pltpu.PrefetchScalarGridSpec(
             num_scalar_prefetch=1, grid=(rows // MB,),
-            in_specs=[block] * 3 + [block2] * 3 + [whole, whole],
+            in_specs=[block] * 6 + [whole, whole],
             out_specs=pl.BlockSpec((MB, dim), lambda i, s: (i, 0))),
         compiler_params=pltpu.CompilerParams(vmem_limit_bytes=32 << 20),
         cost_estimate=cost(4 * rows * dim * dim, 16 << 20),
@@ -690,9 +680,8 @@
         mem_near = to_near(memory)
         g_parts = (grad_out, to_far(grad_out))
 
-        first = project(core1, memory, wkt, wvt, 0, ())
+        k, v, kt, vt = project(core1, memory, mem_near, wkt, wvt)
         x_all_b, n1, _, qt_s = queries(place, x_parts, gain1, wqt)
-        k, v, kt, vt = project(core1, mem_near, wkt, wvt, 1, first)
 
         pairs = mine // 2
         pieces = [(pair, 0, n * rows) for pair in range(pairs - 1)]
@@ -738,12 +727,12 @@
         dkvs, dkvs_near, dqs, dws = [], [], [], []
         lens_now = lens
         for pair in range(pairs):
-            dkv, dqt = attention_backward(lens_now, qt_s, do_t, lse, delta, k, v, kt, pair)
+            dkv, dkv_near, dqt, dw = attention_backward(
+                lens_now, qt_s, do_t, lse, delta, k, v, kt, memory, mem_near, pair)
             dqs.append((dqt, to_far(dqt)))
-            dw = pair_weights(dkv, memory, mem_near)
             dws.append((dw, to_far(dw)))
             dkvs.append(dkv)
-            dkvs_near.append(to_near(dkv[1]))
+            dkvs_near.append(to_near(dkv_near))
             lens_now, dw_last = lax.optimization_barrier((lens, dw))
 
         act_t, _ = lax.optimization_barrier((act_t, dw_last))

time: 389 us -> 395 us (1.015)
  Pallas kernels: 224 us -> 196 us
  waiting for transfers between devices: 106 us -> 128 us
  local copies, waits for them, and re-layouts: 24.9 us -> 36.6 us
    ppermute x12, waiting for transfers between devices: 90.3 us -> 114 us  [to_far(): return lax.ppermute(a, 'seq', far)]
    unnamed x137 -> x147, local copies, waits for them, and re-layouts: 21.8 us -> 33.6 us
    pallas_call x4, Pallas kernels: 52.8 us -> 43.8 us  [attention_forward(): pl.pallas_call(fwd_kernel, out_shape=jax.ShapeDtypeStruct((2 * pairs, ORO...]
    pallas_call x2 -> x1, Pallas kernels: 17.7 us -> 10.2 us  [project(): pl.pallas_call(proj_kernel, out_shape=outs, grid_spec=pltpu.PrefetchScala...]
    pallas_call x7 -> x4, Pallas kernels: 102 us -> 95 us  [the longest x3 71.9 us: attention_backward(): pl.pallas_call(bwd_kernel, out_shape=[jax.ShapeDtypeStruct((2 * PAIR, row...]
  transfers between devices with their start and end apart: 34 -> 34, of which waited for: 11 -> 11; matrix products, arithmetic and copies ran while one was open for 2% -> 2% of each run, Pallas kernels for 34% -> 27%
where the time goes in v3:
time: 395 us; the launch traced here: 390 us
  Pallas kernels  196 us (50%)
  waiting for transfers between devices  128 us (32%)
  local copies, waits for them, and re-layouts  36.6 us (9%)
  starting transfers between devices  22.9 us (6%)
    ppermute x12, waiting for transfers between devices, to_far(): return lax.ppermute(a, 'seq', far)  114 us
    pallas_call x3, Pallas kernels, attention_backward(): pl.pallas_call(bwd_kernel, out_shape=[jax.ShapeDtypeStruct((2 * PAIR, row...  71.9 us
    pallas_call x4, Pallas kernels, attention_forward(): pl.pallas_call(fwd_kernel, out_shape=jax.ShapeDtypeStruct((2 * pairs, ORO...  43.8 us
    unnamed x147, local copies, waits for them, and re-layouts  33.6 us
    pallas_call x1, Pallas kernels, mlp_weights(): pl.pallas_call(mlp_weights_kernel, grid=(ff // WFB,), in_specs=ins + ins,...  23.1 us
    pallas_call x1, Pallas kernels, mlp(): pl.pallas_call(mlp_kernel, grid=(ff // FFB,), in_specs=[fix(rows, dim), f...  21.7 us
    ppermute x22, starting transfers between devices, to_near(): return lax.ppermute(a, 'seq', near)  15.5 us
    ppermute x22, waiting for transfers between devices, to_near(): return lax.ppermute(a, 'seq', near)  14.1 us
  transfers between devices with their start and end apart: 34, of which 11 were waited for; matrix products, arithmetic and copies ran while one was open for 2% of the time, Pallas kernels for 27%

profile of v3, /device:TPU:5, one launch (start us, length us, event | category | flops | bytes accessed | tf_op | source)
XLA Modules:
  0.0 389.8 jit_solution(1231556225640011940)
XLA Ops:
  1.4 1.2 collective-permute-start.1
  2.9 9.3 %collective-permute-done.1.x2_ref = bf16[256,768]{1,0:T(8,128)(2,1)S(1)} collective-permute-done((bf16[256,768]{1,0:T(8,128)(2,1)}, bf16[256,768]{1,0:T(8,128)(2,1)S(1)}, u32[]{:S(2)}, u32[]{:S(2)}) %collective-permute-start.1) | collective-permute-done | bytes 393248 | tf_op jit(solution)/shard_map/ppermute | solution.py:655
  12.2 0.9 collective-permute-start.2
  14.6 1.3 copy-done.3
  15.9 1.0 copy-done.35
  16.9 3.7 queries.1
  20.5 1.1 copy-done.32
  21.7 1.1 copy-done.47
  22.9 2.2 copy-done.46
  25.0 10.2 %kv_proj.1 = (bf16[4096,384]{1,0:T(8,128)(2,1)S(1)}, bf16[4096,384]{1,0:T(8,128)(2,1)S(1)}, bf16[384,4096]{1,0:T(8,128)(2,1)S(1)}, bf16[384,4096]{1,0:T(8,128)(2,1)S(1)}) custom-call(s32[1]{0:T(128)} %bitcast.4.core_ref, bf16[2048,768]{1,0:T(8,128)(2,1)S(1)} %copy-done.46, bf16[2048,768]{1,0:T(8,128)(2,1)} %collective-permute-done.3.m1_ref, ...), custom_call_target="tpu_custom_call" | custom-call | flops 4831838208 | bytes 25165824 | tf_op jit(solution)/shard_map/kv_proj/pallas_call | solution.py:60
  35.2 1.7 copy-done.68
  36.9 7.6 %attn_fwd.6.a_ref = f32[2,72,512]{2,1,0:T(8,128)S(1)} custom-call(s32[2]{0:T(128)S(1)} %pad_add_fusion.len_ref, bf16[384,1024]{1,0:T(8,128)(2,1)S(1)} %get-tuple-element.60.qt_ref, bf16[4096,384]{1,0:T(8,128)(2,1)S(1)} %get-tuple-element.62.k_ref, bf16[384,4096]{1,0:T(8,128)(2,1)S(1)} %get-tuple-element.63.vt_ref), custom_call_target="tpu_custom_call" | custom-call | flops 4294967296 | bytes 4194304 | tf_op jit(solution)/shard_map/attn_fwd/pallas_call | solution.py:216
  44.5 14.3 %attn_fwd.5.a_ref = f32[2,72,1024]{2,1,0:T(8,128)S(1)} custom-call(s32[2]{0:T(128)S(1)} %pad_add_fusion.len_ref, bf16[384,1024]{1,0:T(8,128)(2,1)S(1)} %get-tuple-element.60.qt_ref, bf16[4096,384]{1,0:T(8,128)(2,1)S(1)} %get-tuple-element.62.k_ref, bf16[384,4096]{1,0:T(8,128)(2,1)S(1)} %get-tuple-element.63.vt_ref), custom_call_target="tpu_custom_call" | custom-call | flops 8589934592 | bytes 4194304 | tf_op jit(solution)/shard_map/attn_fwd/pallas_call | solution.py:216
  58.8 14.3 %attn_fwd.4.a_ref = f32[2,72,1024]{2,1,0:T(8,128)S(1)} custom-call(s32[2]{0:T(128)S(1)} %pad_add_fusion.len_ref, bf16[384,1024]{1,0:T(8,128)(2,1)S(1)} %get-tuple-element.60.qt_ref, bf16[4096,384]{1,0:T(8,128)(2,1)S(1)} %get-tuple-element.62.k_ref, bf16[384,4096]{1,0:T(8,128)(2,1)S(1)} %get-tuple-element.63.vt_ref), custom_call_target="tpu_custom_call" | custom-call | flops 8589934592 | bytes 4194304 | tf_op jit(solution)/shard_map/attn_fwd/pallas_call | solution.py:216
  73.1 1.5 collective-permute-start.4
  74.6 7.6 %attn_fwd.7.a_ref = f32[2,72,512]{2,1,0:T(8,128)S(1)} custom-call(s32[2]{0:T(128)S(1)} %pad_add_fusion.len_ref, bf16[384,1024]{1,0:T(8,128)(2,1)S(1)} %get-tuple-element.60.qt_ref, bf16[4096,384]{1,0:T(8,128)(2,1)S(1)} %get-tuple-element.62.k_ref, bf16[384,4096]{1,0:T(8,128)(2,1)S(1)} %get-tuple-element.63.vt_ref), custom_call_target="tpu_custom_call" | custom-call | flops 4294967296 | bytes 4194304 | tf_op jit(solution)/shard_map/attn_fwd/pallas_call | solution.py:216
  82.3 1.4 collective-permute-start.9
  83.8 29.2 %collective-permute-done.7.b_ref = f32[2,72,512]{2,1,0:T(8,128)S(1)} collective-permute-done((f32[2,72,512]{2,1,0:T(8,128)S(1)}, f32[2,72,512]{2,1,0:T(8,128)S(1)}, u32[]{:S(2)}, u32[]{:S(2)}) %collective-permute-start.7) | collective-permute-done | bytes 294944 | tf_op jit(solution)/shard_map/ppermute | solution.py:655
  116.5 1.7 collective-permute-start.8
  118.2 1.3 reshape.84.gain_ref
  119.4 10.6 %collective-permute-done.9.x1_ref = f32[256,768]{1,0:T(8,128)} collective-permute-done((f32[256,768]{1,0:T(8,128)S(1)}, f32[256,768]{1,0:T(8,128)}, u32[]{:S(2)}, u32[]{:S(2)}) %collective-permute-start.9) | collective-permute-done | bytes 786464 | tf_op jit(solution)/shard_map/ppermute | solution.py:655
  130.0 1.8 place_rows.1.g_ref
  133.0 0.8 copy-done.33
  133.9 1.5 add_convert_fusion.h_ref
  135.4 21.7 %mlp.1 = (bf16[768,512]{1,0:T(8,128)(2,1)}, bf16[512,768]{1,0:T(8,128)(2,1)}, bf16[512,3072]{1,0:T(8,128)(2,1)}, bf16[512,3072]{1,0:T(8,128)(2,1)}, bf16[3072,51...) custom-call(bf16[512,768]{1,0:T(8,128)(2,1)} %add_convert_fusion.h_ref, ...), custom_call_target="tpu_custom_call" | custom-call | flops 12079595520 | bytes 41943040 | tf_op jit(solution)/shard_map/mlp/pallas_call | solution.py:442
  157.0 1.1 collective-permute-start.10
  158.2 1.2 constant_dynamic-update-slice_fusion.1
  159.4 0.9 collective-permute-done.10
  162.6 0.9 copy-done.67
  163.9 1.9 copy-done.71
  165.8 24.1 %attn_bwd.3 = (bf16[256,2048]{1,0:T(8,128)(2,1)S(1)}, bf16[256,2048]{1,0:T(8,128)(2,1)S(1)}, f32[2,64,1024]{2,1,0:T(8,128)S(1)}, f32[256,768]{1,0:T(8,128)S(1)}) custom-call(s32[2]{0:T(128)S(1)} %copy-done.58, bf16[384,1024]{1,0:T(8,128)(2,1)S(1)} %copy-done.56, bf16[384,1024]{1,0:T(8,128)(2,1)S(1)} %get-tuple-element.111.dot_ref, ...), custom_call_target="tpu_custom_call" | custom-call | flops 16777216000 | bytes 8388608 | tf_op jit(solution)/shard_map/attn_bwd/pallas_call | solution.py:324
  190.0 1.0 copy-done.60
  190.9 23.8 %attn_bwd.4 = (bf16[256,2048]{1,0:T(8,128)(2,1)S(1)}, bf16[256,2048]{1,0:T(8,128)(2,1)S(1)}, f32[2,64,1024]{2,1,0:T(8,128)S(1)}, f32[256,768]{1,0:T(8,128)S(1)}) custom-call(s32[2]{0:T(128)S(1)} %copy-done.58, bf16[384,1024]{1,0:T(8,128)(2,1)S(1)} %copy-done.56, bf16[384,1024]{1,0:T(8,128)(2,1)S(1)} %get-tuple-element.111.dot_ref, ...), custom_call_target="tpu_custom_call" | custom-call | flops 16777216000 | bytes 8388608 | tf_op jit(solution)/shard_map/attn_bwd/pallas_call | solution.py:324
  214.8 1.0 copy-done.62
  215.7 23.9 %attn_bwd.5 = (bf16[256,2048]{1,0:T(8,128)(2,1)S(1)}, bf16[256,2048]{1,0:T(8,128)(2,1)S(1)}, f32[2,64,1024]{2,1,0:T(8,128)S(1)}, f32[256,768]{1,0:T(8,128)S(1)}) custom-call(s32[2]{0:T(128)S(1)} %copy-done.58, bf16[384,1024]{1,0:T(8,128)(2,1)S(1)} %copy-done.56, bf16[384,1024]{1,0:T(8,128)(2,1)S(1)} %get-tuple-element.111.dot_ref, ...), custom_call_target="tpu_custom_call" | custom-call | flops 16777216000 | bytes 8388608 | tf_op jit(solution)/shard_map/attn_bwd/pallas_call | solution.py:324
  239.7 1.0 copy-done.64
  241.1 1.7 collective-permute-start.21
  243.6 0.9 collective-permute-start.23
  244.6 9.1 %collective-permute-done.13.b2_ref = f32[2,64,1024]{2,1,0:T(8,128)S(1)} collective-permute-done((f32[2,64,1024]{2,1,0:T(8,128)S(1)}, f32[2,64,1024]{2,1,0:T(8,128)S(1)}, u32[]{:S(2)}, u32[]{:S(2)}) %collective-permute-start.13) | collective-permute-done | bytes 524320 | tf_op jit(solution)/shard_map/ppermute | solution.py:655
  253.7 2.1 collective-permute-start.20
  255.9 25.9 %collective-permute-done.12.b1_ref = f32[2,64,1024]{2,1,0:T(8,128)S(1)} collective-permute-done((f32[2,64,1024]{2,1,0:T(8,128)S(1)}, f32[2,64,1024]{2,1,0:T(8,128)S(1)}, u32[]{:S(2)}, u32[]{:S(2)}) %collective-permute-start.12) | collective-permute-done | bytes 524320 | tf_op jit(solution)/shard_map/ppermute | solution.py:655
  281.8 2.1 collective-permute-start.15
  284.0 14.6 %collective-permute-done.23.refs_8_ = f32[256,768]{1,0:T(8,128)S(1)} collective-permute-done((f32[256,768]{1,0:T(8,128)S(1)}, f32[256,768]{1,0:T(8,128)S(1)}, u32[]{:S(2)}, u32[]{:S(2)}) %collective-permute-start.23) | collective-permute-done | bytes 786464 | tf_op jit(solution)/shard_map/ppermute | solution.py:655
  298.7 2.1 collective-permute-start.17
  300.8 14.7 %collective-permute-done.22.refs_7_ = f32[256,768]{1,0:T(8,128)S(1)} collective-permute-done((f32[256,768]{1,0:T(8,128)S(1)}, f32[256,768]{1,0:T(8,128)S(1)}, u32[]{:S(2)}, u32[]{:S(2)}) %collective-permute-start.22) | collective-permute-done | bytes 786464 | tf_op jit(solution)/shard_map/ppermute | solution.py:655
  315.5 1.3 collective-permute-start.31
  316.8 0.9 copy-done.17
  318.2 1.0 copy-done.27
  320.3 12.1 %collective-permute-done.14.near_ref = bf16[384,1024]{1,0:T(8,128)(2,1)S(1)} collective-permute-done((bf16[384,1024]{1,0:T(8,128)(2,1)S(1)}, bf16[384,1024]{1,0:T(8,128)(2,1)S(1)}, u32[]{:S(2)}, u32[]{:S(2)}) %collective-permute-start.14) | collective-permute-done | bytes 786464 | tf_op jit(solution)/shard_map/ppermute | solution.py:652
  333.5 0.9 copy-done.19
  334.8 0.9 copy-done.15
  337.2 2.6 out_proj_grad.1
  340.4 7.5 %memory_grad.1 = f32[2048,768]{1,0:T(8,128)} custom-call(s32[1]{0:T(128)} %bitcast.4.core_ref, bf16[256,2048]{1,0:T(8,128)(2,1)S(1)} %copy-done.61, bf16[256,2048]{1,0:T(8,128)(2,1)S(1)} %copy-done.63, bf16[256,2048]{1,0:T(8,128)(2,1)S(1)} %copy-done.65, bf16[256,2048]{1,0:T(8,128)(2,1)S(1)} %collective-permute-done.15.b0_ref, ...), custom_call_target="tpu_custom_call" | custom-call | flops 4831838208 | bytes 16777216 | tf_op jit(solution)/shard_map/memory_grad/pallas_call | solution.py:500
  347.9 5.5 %query_grad.1 = (f32[768,768]{1,0:T(8,128)}, f32[256,768]{1,0:T(8,128)}, f32[1,768]{1,0:T(1,128)S(1)}) custom-call(s32[5]{0:T(128)S(1)} %stack.32.place_ref, bf16[384,1024]{1,0:T(8,128)(2,1)S(1)} %sum_queries.1.mine_ref, bf16[384,1024]{1,0:T(8,128)(2,1)S(1)} %collective-permute-done.14.near_ref, bf16[1024,768]{1,0:T(8,128)(2,1)S(1)} %copy-done.48, ...), custom_call_target="tpu_custom_call" | custom-call | flops 2415919104 | bytes 10485760 | tf_op jit(solution)/shard_map/query_grad/pallas_call | solution.py:583
  354.1 1.1 copy-done.10
  355.2 1.1 copy-done.12
  356.4 1.1 copy-done.14
  357.5 1.1 copy-done.16
  358.6 1.1 copy-done.18
  359.8 1.1 copy-done.20
  360.9 1.1 copy-done.22
  362.0 1.1 copy-done.24
  363.2 3.2 key_weights.1
  366.5 23.1 %mlp_weights.1 = (f32[768,3072]{1,0:T(8,128)}, f32[768,3072]{1,0:T(8,128)}, f32[3072,768]{1,0:T(8,128)}) custom-call(bf16[768,512]{1,0:T(8,128)(2,1)} %get-tuple-element.101.n2t_ref, bf16[512,768]{1,0:T(8,128)(2,1)} %get-tuple-element.102.gt_ref, bf16[512,3072]{1,0:T(8,128)(2,1)} %get-tuple-element.103.dgate_ref, ...), custom_call_target="tpu_custom_call" | custom-call | flops 14495514624 | bytes 52428800 | tf_op jit(solution)/shard_map/mlp_weights/pallas_call | solution.py:472
  (187 shorter events, 16.4 us)
Async XLA Ops:
  0.6 131.2 %copy-start = (bf16[12,64,768]{2,1,0:T(8,128)(2,1)S(1)}, bf16[12,64,768]{2,1,0:T(8,128)(2,1)}, u32[]{:S(2)}) copy-start(bf16[12,64,768]{2,1,0:T(8,128)(2,1)} %param.21) | copy-start | bytes 3538948
  0.7 22.2 %collective-permute-start.3 = (bf16[2048,768]{1,0:T(8,128)(2,1)}, bf16[2048,768]{1,0:T(8,128)(2,1)}, u32[]{:S(2)}, u32[]{:S(2)}) collective-permute-start(bf16[2048,768]{1,0:T(8,128)(2,1)} %m0_ref.7), channel_id=1, source_target_pairs={{0,1},{1,0},{2,3},{3,2},{4,5},{5,4},{6,7},{7,6}} | collective-permute-start | bytes 9437192 | tf_op jit(solution)/shard_map/ppermute | solution.py:652
  1.4 10.8 %collective-permute-start.1 = (bf16[256,768]{1,0:T(8,128)(2,1)}, bf16[256,768]{1,0:T(8,128)(2,1)S(1)}, u32[]{:S(2)}, u32[]{:S(2)}) collective-permute-start(bf16[256,768]{1,0:T(8,128)(2,1)} %x0_ref.2), channel_id=1, source_target_pairs={{0,2},{1,3},{2,0},{3,1},{4,6},{5,7},{6,4},{7,5}} | collective-permute-start | bytes 1179656 | tf_op jit(solution)/shard_map/ppermute | solution.py:655
  2.6 12.0 %collective-permute-start = (bf16[256,768]{1,0:T(8,128)(2,1)}, bf16[256,768]{1,0:T(8,128)(2,1)S(1)}, u32[]{:S(2)}, u32[]{:S(2)}) collective-permute-start(bf16[256,768]{1,0:T(8,128)(2,1)} %x0_ref.2), channel_id=1, source_target_pairs={{0,1},{1,0},{2,3},{3,2},{4,5},{5,4},{6,7},{7,6}} | collective-permute-start | bytes 1179656 | tf_op jit(solution)/shard_map/ppermute | solution.py:652
  12.2 2.4 collective-permute-start.2
  14.6 60.0 %copy-start.57 = (s32[2]{0:T(128)}, s32[2]{0:T(128)S(1)}, u32[]{:S(2)}) copy-start(s32[2]{0:T(128)S(1)} %pad_add_fusion.len_ref) | copy-start | bytes 28
  16.9 6.0 %copy-start.49 = (bf16[768,12,64]{0,2,1:T(8,128)(2,1)S(1)}, bf16[768,12,64]{0,2,1:T(8,128)(2,1)}, u32[]{:S(2)}) copy-start(bf16[768,12,64]{0,2,1:T(8,128)(2,1)} %param.19) | copy-start | bytes 3538948
  16.9 6.0 %copy-start.51 = (bf16[768,12,64]{0,2,1:T(8,128)(2,1)S(1)}, bf16[768,12,64]{0,2,1:T(8,128)(2,1)}, u32[]{:S(2)}) copy-start(bf16[768,12,64]{0,2,1:T(8,128)(2,1)} %param.20) | copy-start | bytes 3538948
  22.8 51.8 %copy-start.55 = (bf16[384,1024]{1,0:T(8,128)(2,1)}, bf16[384,1024]{1,0:T(8,128)(2,1)S(1)}, u32[]{:S(2)}) copy-start(bf16[384,1024]{1,0:T(8,128)(2,1)S(1)} %get-tuple-element.60.qt_ref) | copy-start | bytes 2359300
  36.9 7.6 %copy-start.70 = (bf16[384,4096]{1,0:T(8,128)(2,1)}, bf16[384,4096]{1,0:T(8,128)(2,1)S(1)}, u32[]{:S(2)}) copy-start(bf16[384,4096]{1,0:T(8,128)(2,1)S(1)} %get-tuple-element.78.kt_ref) | copy-start | bytes 9437188
  36.9 37.8 %copy-start.66 = (bf16[4096,384]{1,0:T(8,128)(2,1)}, bf16[4096,384]{1,0:T(8,128)(2,1)S(1)}, u32[]{:S(2)}) copy-start(bf16[4096,384]{1,0:T(8,128)(2,1)S(1)} %get-tuple-element.62.k_ref) | copy-start | bytes 9437188
  73.1 9.2 %copy-start.25 = (f32[256,768]{1,0:T(8,128)S(1)}, f32[256,768]{1,0:T(8,128)}, u32[]{:S(2)}) copy-start(f32[256,768]{1,0:T(8,128)} %x0_ref.3) | copy-start | bytes 2359300
  73.1 10.7 %collective-permute-start.6 = (f32[2,72,512]{2,1,0:T(8,128)S(1)}, f32[2,72,512]{2,1,0:T(8,128)S(1)}, u32[]{:S(2)}, u32[]{:S(2)}) collective-permute-start(f32[2,72,512]{2,1,0:T(8,128)S(1)} %attn_fwd.6.a_ref), channel_id=1, source_target_pairs={{0,2},{1,3},{2,0},{3,1},{4,6},{5,7},{6,4},{7,5}} | collective-permute-start | bytes 884744 | tf_op jit(solution)/shard_map/ppermute | solution.py:655
  73.1 40.6 %collective-permute-start.4 = (f32[2,72,1024]{2,1,0:T(8,128)S(1)}, f32[2,72,1024]{2,1,0:T(8,128)S(1)}, u32[]{:S(2)}, u32[]{:S(2)}) collective-permute-start(f32[2,72,1024]{2,1,0:T(8,128)S(1)} %attn_fwd.4.a_ref), channel_id=1, source_target_pairs={{0,2},{1,3},{2,0},{3,1},{4,6},{5,7},{6,4},{7,5}} | collective-permute-start | bytes 1769480 | tf_op jit(solution)/shard_map/ppermute | solution.py:655
  74.6 39.4 %collective-permute-start.5 = (f32[2,72,1024]{2,1,0:T(8,128)S(1)}, f32[2,72,1024]{2,1,0:T(8,128)S(1)}, u32[]{:S(2)}, u32[]{:S(2)}) collective-permute-start(f32[2,72,1024]{2,1,0:T(8,128)S(1)} %attn_fwd.5.a_ref), channel_id=1, source_target_pairs={{0,2},{1,3},{2,0},{3,1},{4,6},{5,7},{6,4},{7,5}} | collective-permute-start | bytes 1769480 | tf_op jit(solution)/shard_map/ppermute | solution.py:655
  82.3 30.8 %collective-permute-start.7 = (f32[2,72,512]{2,1,0:T(8,128)S(1)}, f32[2,72,512]{2,1,0:T(8,128)S(1)}, u32[]{:S(2)}, u32[]{:S(2)}) collective-permute-start(f32[2,72,512]{2,1,0:T(8,128)S(1)} %attn_fwd.7.a_ref), channel_id=1, source_target_pairs={{0,2},{1,3},{2,0},{3,1},{4,6},{5,7},{6,4},{7,5}} | collective-permute-start | bytes 884744 | tf_op jit(solution)/shard_map/ppermute | solution.py:655
  82.3 47.7 %collective-permute-start.9 = (f32[256,768]{1,0:T(8,128)S(1)}, f32[256,768]{1,0:T(8,128)}, u32[]{:S(2)}, u32[]{:S(2)}) collective-permute-start(f32[256,768]{1,0:T(8,128)S(1)} %copy-done.25), channel_id=1, source_target_pairs={{0,2},{1,3},{2,0},{3,1},{4,6},{5,7},{6,4},{7,5}} | collective-permute-start | bytes 2359304 | tf_op jit(solution)/shard_map/ppermute | solution.py:655
  83.8 29.3 %copy-start.36 = (f32[2,64,512]{2,1,0:T(8,128)}, f32[2,64,512]{2,1,0:T(8,128)S(1)}, u32[]{:S(2)}) copy-start(f32[2,64,512]{2,1,0:T(8,128)S(1)} %get-tuple-element.75) | copy-start | bytes 786436
  83.8 29.3 %copy-start.42 = (f32[2,1,512]{2,1,0:T(1,128)}, f32[2,1,512]{2,1,0:T(1,128)S(1)}, u32[]{:S(2)}) copy-start(f32[2,1,512]{2,1,0:T(1,128)S(1)} %get-tuple-element.71) | copy-start | bytes 12292
  116.5 16.0 %collective-permute-start.8 = (bf16[384,512]{1,0:T(8,128)(2,1)S(1)}, bf16[384,512]{1,0:T(8,128)(2,1)S(1)}, u32[]{:S(2)}, u32[]{:S(2)}) collective-permute-start(bf16[384,512]{1,0:T(8,128)(2,1)S(1)} %get-tuple-element.110), channel_id=1, source_target_pairs={{0,1},{1,0},{2,3},{3,2},{4,5},{5,4},{6,7},{7,6}} | collective-permute-start | bytes 1179656 | tf_op jit(solution)/shard_map/ppermute | solution.py:652
  135.4 22.8 %copy-start.41 = (f32[2,1,1024]{2,1,0:T(1,128)S(1)}, f32[2,1,1024]{2,1,0:T(1,128)}, u32[]{:S(2)}) copy-start(f32[2,1,1024]{2,1,0:T(1,128)} %copy-done.40) | copy-start | bytes 24580
  135.4 22.8 %copy-start.43 = (f32[2,1,512]{2,1,0:T(1,128)S(1)}, f32[2,1,512]{2,1,0:T(1,128)}, u32[]{:S(2)}) copy-start(f32[2,1,512]{2,1,0:T(1,128)} %copy-done.42) | copy-start | bytes 12292
  135.4 22.8 %copy-start.45 = (f32[2,1,512]{2,1,0:T(1,128)S(1)}, f32[2,1,512]{2,1,0:T(1,128)}, u32[]{:S(2)}) copy-start(f32[2,1,512]{2,1,0:T(1,128)} %copy-done.44) | copy-start | bytes 12292
  157.0 3.2 collective-permute-start.10
  158.1 84.7 %collective-permute-start.27 = (bf16[384,512]{1,0:T(8,128)(2,1)}, bf16[384,512]{1,0:T(8,128)(2,1)S(1)}, u32[]{:S(2)}, u32[]{:S(2)}) collective-permute-start(bf16[384,512]{1,0:T(8,128)(2,1)} %get-tuple-element.109), channel_id=1, source_target_pairs={{0,1},{1,0},{2,3},{3,2},{4,5},{5,4},{6,7},{7,6}} | collective-permute-start | bytes 1179656 | tf_op jit(solution)/shard_map/ppermute | solution.py:652
  190.9 23.8 %copy-start.54 = (bf16[256,2048]{1,0:T(8,128)(2,1)}, bf16[256,2048]{1,0:T(8,128)(2,1)S(1)}, u32[]{:S(2)}) copy-start(bf16[256,2048]{1,0:T(8,128)(2,1)S(1)} %get-tuple-element.92) | copy-start | bytes 3145732
  190.9 52.7 %collective-permute-start.11 = (f32[2,64,1024]{2,1,0:T(8,128)S(1)}, f32[2,64,1024]{2,1,0:T(8,128)S(1)}, u32[]{:S(2)}, u32[]{:S(2)}) collective-permute-start(f32[2,64,1024]{2,1,0:T(8,128)S(1)} %get-tuple-element.79.a0_ref), channel_id=1, source_target_pairs={{0,2},{1,3},{2,0},{3,1},{4,6},{5,7},{6,4},{7,5}} | collective-permute-start | bytes 1572872 | tf_op jit(solution)/shard_map/ppermute | solution.py:655
  215.7 24.0 %copy-start.53 = (bf16[256,2048]{1,0:T(8,128)(2,1)}, bf16[256,2048]{1,0:T(8,128)(2,1)S(1)}, u32[]{:S(2)}) copy-start(bf16[256,2048]{1,0:T(8,128)(2,1)S(1)} %get-tuple-element.93) | copy-start | bytes 3145732
  215.7 27.4 %copy-start.26 = (f32[2,64,1024]{2,1,0:T(8,128)}, f32[2,64,1024]{2,1,0:T(8,128)S(1)}, u32[]{:S(2)}) copy-start(f32[2,64,1024]{2,1,0:T(8,128)S(1)} %get-tuple-element.82.a1_ref) | copy-start | bytes 1572868
  215.7 24.9 %copy-start.72 = (f32[1,768]{1,0:T(1,128)S(1)}, f32[1,768]{1,0:T(1,128)}, u32[]{:S(2)}) copy-start(f32[1,768]{1,0:T(1,128)} %get-tuple-element.100) | copy-start | bytes 9220
  240.7 79.1 %copy-start.5 = (f32[256,768]{1,0:T(8,128)}, f32[256,768]{1,0:T(8,128)S(1)}, u32[]{:S(2)}) copy-start(f32[256,768]{1,0:T(8,128)S(1)} %get-tuple-element.97.refs_2_) | copy-start | bytes 2359300
  240.7 13.1 %collective-permute-start.13 = (f32[2,64,1024]{2,1,0:T(8,128)S(1)}, f32[2,64,1024]{2,1,0:T(8,128)S(1)}, u32[]{:S(2)}, u32[]{:S(2)}) collective-permute-start(f32[2,64,1024]{2,1,0:T(8,128)S(1)} %get-tuple-element.85.a2_ref), channel_id=1, source_target_pairs={{0,2},{1,3},{2,0},{3,1},{4,6},{5,7},{6,4},{7,5}} | collective-permute-start | bytes 1572872 | tf_op jit(solution)/shard_map/ppermute | solution.py:655
  240.7 2.4 collective-permute-start.28
  241.1 42.9 %collective-permute-start.21 = (f32[256,768]{1,0:T(8,128)S(1)}, f32[256,768]{1,0:T(8,128)S(1)}, u32[]{:S(2)}, u32[]{:S(2)}) collective-permute-start(f32[256,768]{1,0:T(8,128)S(1)} %get-tuple-element.80.refs_0_), channel_id=1, source_target_pairs={{0,2},{1,3},{2,0},{3,1},{4,6},{5,7},{6,4},{7,5}} | collective-permute-start | bytes 2359304 | tf_op jit(solution)/shard_map/ppermute | solution.py:655
  242.8 41.1 %collective-permute-start.18 = (f32[256,768]{1,0:T(8,128)S(1)}, f32[256,768]{1,0:T(8,128)S(1)}, u32[]{:S(2)}, u32[]{:S(2)}) collective-permute-start(f32[256,768]{1,0:T(8,128)S(1)} %get-tuple-element.80.refs_0_), channel_id=1, source_target_pairs={{0,1},{1,0},{2,3},{3,2},{4,5},{5,4},{6,7},{7,6}} | collective-permute-start | bytes 2359304 | tf_op jit(solution)/shard_map/ppermute | solution.py:652
  243.1 38.7 %collective-permute-start.12 = (f32[2,64,1024]{2,1,0:T(8,128)S(1)}, f32[2,64,1024]{2,1,0:T(8,128)S(1)}, u32[]{:S(2)}, u32[]{:S(2)}) collective-permute-start(f32[2,64,1024]{2,1,0:T(8,128)S(1)} %get-tuple-element.82.a1_ref), channel_id=1, source_target_pairs={{0,2},{1,3},{2,0},{3,1},{4,6},{5,7},{6,4},{7,5}} | collective-permute-start | bytes 1572872 | tf_op jit(solution)/shard_map/ppermute | solution.py:655
  243.6 55.0 %collective-permute-start.23 = (f32[256,768]{1,0:T(8,128)S(1)}, f32[256,768]{1,0:T(8,128)S(1)}, u32[]{:S(2)}, u32[]{:S(2)}) collective-permute-start(f32[256,768]{1,0:T(8,128)S(1)} %get-tuple-element.97.refs_2_), channel_id=1, source_target_pairs={{0,2},{1,3},{2,0},{3,1},{4,6},{5,7},{6,4},{7,5}} | collective-permute-start | bytes 2359304 | tf_op jit(solution)/shard_map/ppermute | solution.py:655
  253.7 47.1 %collective-permute-start.20 = (f32[256,768]{1,0:T(8,128)S(1)}, f32[256,768]{1,0:T(8,128)S(1)}, u32[]{:S(2)}, u32[]{:S(2)}) collective-permute-start(f32[256,768]{1,0:T(8,128)S(1)} %get-tuple-element.97.refs_2_), channel_id=1, source_target_pairs={{0,1},{1,0},{2,3},{3,2},{4,5},{5,4},{6,7},{7,6}} | collective-permute-start | bytes 2359304 | tf_op jit(solution)/shard_map/ppermute | solution.py:652
  281.8 35.9 %collective-permute-start.15 = (bf16[256,2048]{1,0:T(8,128)(2,1)}, bf16[256,2048]{1,0:T(8,128)(2,1)S(1)}, u32[]{:S(2)}, u32[]{:S(2)}) collective-permute-start(bf16[256,2048]{1,0:T(8,128)(2,1)} %copy-done.54), channel_id=1, source_target_pairs={{0,1},{1,0},{2,3},{3,2},{4,5},{5,4},{6,7},{7,6}} | collective-permute-start | bytes 3145736 | tf_op jit(solution)/shard_map/ppermute | solution.py:652
  284.0 35.8 %copy-start.7 = (f32[256,768]{1,0:T(8,128)}, f32[256,768]{1,0:T(8,128)S(1)}, u32[]{:S(2)}) copy-start(f32[256,768]{1,0:T(8,128)S(1)} %collective-permute-done.21.refs_6_) | copy-start | bytes 2359300
  284.0 31.6 %collective-permute-start.22 = (f32[256,768]{1,0:T(8,128)S(1)}, f32[256,768]{1,0:T(8,128)S(1)}, u32[]{:S(2)}, u32[]{:S(2)}) collective-permute-start(f32[256,768]{1,0:T(8,128)S(1)} %get-tuple-element.83.refs_1_), channel_id=1, source_target_pairs={{0,2},{1,3},{2,0},{3,1},{4,6},{5,7},{6,4},{7,5}} | collective-permute-start | bytes 2359304 | tf_op jit(solution)/shard_map/ppermute | solution.py:655
  284.0 35.8 %copy-start.9 = (f32[256,768]{1,0:T(8,128)}, f32[256,768]{1,0:T(8,128)S(1)}, u32[]{:S(2)}) copy-start(f32[256,768]{1,0:T(8,128)S(1)} %collective-permute-done.18.refs_3_) | copy-start | bytes 2359300
  284.0 32.8 %collective-permute-start.19 = (f32[256,768]{1,0:T(8,128)S(1)}, f32[256,768]{1,0:T(8,128)S(1)}, u32[]{:S(2)}, u32[]{:S(2)}) collective-permute-start(f32[256,768]{1,0:T(8,128)S(1)} %get-tuple-element.83.refs_1_), channel_id=1, source_target_pairs={{0,1},{1,0},{2,3},{3,2},{4,5},{5,4},{6,7},{7,6}} | collective-permute-start | bytes 2359304 | tf_op jit(solution)/shard_map/ppermute | solution.py:652
  298.7 33.7 %copy-start.11 = (f32[256,768]{1,0:T(8,128)}, f32[256,768]{1,0:T(8,128)S(1)}, u32[]{:S(2)}) copy-start(f32[256,768]{1,0:T(8,128)S(1)} %collective-permute-done.23.refs_8_) | copy-start | bytes 2359300
  298.7 21.1 %collective-permute-start.17 = (bf16[256,2048]{1,0:T(8,128)(2,1)S(1)}, bf16[256,2048]{1,0:T(8,128)(2,1)S(1)}, u32[]{:S(2)}, u32[]{:S(2)}) collective-permute-start(bf16[256,2048]{1,0:T(8,128)(2,1)S(1)} %get-tuple-element.94), channel_id=1, source_target_pairs={{0,1},{1,0},{2,3},{3,2},{4,5},{5,4},{6,7},{7,6}} | collective-permute-start | bytes 3145736 | tf_op jit(solution)/shard_map/ppermute | solution.py:652
  300.8 18.9 %copy-start.13 = (f32[256,768]{1,0:T(8,128)}, f32[256,768]{1,0:T(8,128)S(1)}, u32[]{:S(2)}) copy-start(f32[256,768]{1,0:T(8,128)S(1)} %collective-permute-done.20.refs_5_) | copy-start | bytes 2359300
  300.8 19.0 %collective-permute-start.16 = (bf16[256,2048]{1,0:T(8,128)(2,1)}, bf16[256,2048]{1,0:T(8,128)(2,1)S(1)}, u32[]{:S(2)}, u32[]{:S(2)}) collective-permute-start(bf16[256,2048]{1,0:T(8,128)(2,1)} %copy-done.53), channel_id=1, source_target_pairs={{0,1},{1,0},{2,3},{3,2},{4,5},{5,4},{6,7},{7,6}} | collective-permute-start | bytes 3145736 | tf_op jit(solution)/shard_map/ppermute | solution.py:652
  315.5 50.9 %collective-permute-start.31 = (bf16[512,3072]{1,0:T(8,128)(2,1)}, bf16[512,3072]{1,0:T(8,128)(2,1)}, u32[]{:S(2)}, u32[]{:S(2)}) collective-permute-start(bf16[512,3072]{1,0:T(8,128)(2,1)} %get-tuple-element.103.dgate_ref), channel_id=1, source_target_pairs={{0,1},{1,0},{2,3},{3,2},{4,5},{5,4},{6,7},{7,6}} | collective-permute-start | bytes 9437192 | tf_op jit(solution)/shard_map/ppermute | solution.py:652
  317.7 48.7 %collective-permute-start.32 = (bf16[512,3072]{1,0:T(8,128)(2,1)}, bf16[512,3072]{1,0:T(8,128)(2,1)}, u32[]{:S(2)}, u32[]{:S(2)}) collective-permute-start(bf16[512,3072]{1,0:T(8,128)(2,1)} %get-tuple-element.104.dup_ref), channel_id=1, source_target_pairs={{0,1},{1,0},{2,3},{3,2},{4,5},{5,4},{6,7},{7,6}} | collective-permute-start | bytes 9437192 | tf_op jit(solution)/shard_map/ppermute | solution.py:652
  317.7 48.7 %collective-permute-start.33 = (bf16[3072,512]{1,0:T(8,128)(2,1)}, bf16[3072,512]{1,0:T(8,128)(2,1)}, u32[]{:S(2)}, u32[]{:S(2)}) collective-permute-start(bf16[3072,512]{1,0:T(8,128)(2,1)} %get-tuple-element.105.ut_ref), channel_id=1, source_target_pairs={{0,1},{1,0},{2,3},{3,2},{4,5},{5,4},{6,7},{7,6}} | collective-permute-start | bytes 9437192 | tf_op jit(solution)/shard_map/ppermute | solution.py:652
  319.8 12.7 %collective-permute-start.14 = (bf16[384,1024]{1,0:T(8,128)(2,1)S(1)}, bf16[384,1024]{1,0:T(8,128)(2,1)S(1)}, u32[]{:S(2)}, u32[]{:S(2)}) collective-permute-start(bf16[384,1024]{1,0:T(8,128)(2,1)S(1)} %sum_queries.1.mine_ref), channel_id=1, source_target_pairs={{0,1},{1,0},{2,3},{3,2},{4,5},{5,4},{6,7},{7,6}} | collective-permute-start | bytes 2359304 | tf_op jit(solution)/shard_map/ppermute | solution.py:652
  319.8 13.7 %collective-permute-start.24 = (f32[256,768]{1,0:T(8,128)S(1)}, f32[256,768]{1,0:T(8,128)S(1)}, u32[]{:S(2)}, u32[]{:S(2)}) collective-permute-start(f32[256,768]{1,0:T(8,128)S(1)} %collective-permute-done.21.refs_6_), channel_id=1, source_target_pairs={{0,1},{1,0},{2,3},{3,2},{4,5},{5,4},{6,7},{7,6}} | collective-permute-start | bytes 2359304 | tf_op jit(solution)/shard_map/ppermute | solution.py:652
  332.4 3.9 collective-permute-start.26
  334.4 2.3 collective-permute-start.25
  336.3 30.1 %collective-permute-start.29 = (bf16[768,512]{1,0:T(8,128)(2,1)}, bf16[768,512]{1,0:T(8,128)(2,1)}, u32[]{:S(2)}, u32[]{:S(2)}) collective-permute-start(bf16[768,512]{1,0:T(8,128)(2,1)} %get-tuple-element.101.n2t_ref), channel_id=1, source_target_pairs={{0,1},{1,0},{2,3},{3,2},{4,5},{5,4},{6,7},{7,6}} | collective-permute-start | bytes 2359304 | tf_op jit(solution)/shard_map/ppermute | solution.py:652
  336.7 3.7 copy-start.65
  336.8 29.7 %collective-permute-start.30 = (bf16[512,768]{1,0:T(8,128)(2,1)}, bf16[512,768]{1,0:T(8,128)(2,1)}, u32[]{:S(2)}, u32[]{:S(2)}) collective-permute-start(bf16[512,768]{1,0:T(8,128)(2,1)} %get-tuple-element.102.gt_ref), channel_id=1, source_target_pairs={{0,1},{1,0},{2,3},{3,2},{4,5},{5,4},{6,7},{7,6}} | collective-permute-start | bytes 2359304 | tf_op jit(solution)/shard_map/ppermute | solution.py:652
  340.4 7.5 %copy-start.4 = (bf16[768,12,64]{0,2,1:T(8,128)(2,1)S(1)}, bf16[768,12,64]{0,2,1:T(8,128)(2,1)}, u32[]{:S(2)}) copy-start(bf16[768,12,64]{0,2,1:T(8,128)(2,1)} %param.18) | copy-start | bytes 3538948
  340.4 7.5 %copy-start.34 = (bf16[1024,768]{1,0:T(8,128)(2,1)S(1)}, bf16[1024,768]{1,0:T(8,128)(2,1)}, u32[]{:S(2)}) copy-start(bf16[1024,768]{1,0:T(8,128)(2,1)} %copy-done.32) | copy-start | bytes 4718596
  340.4 7.5 %copy-start.48 = (bf16[1024,768]{1,0:T(8,128)(2,1)S(1)}, bf16[1024,768]{1,0:T(8,128)(2,1)}, u32[]{:S(2)}) copy-start(bf16[1024,768]{1,0:T(8,128)(2,1)} %copy-done.47) | copy-start | bytes 4718596
  340.4 7.5 %copy-start.59 = (f32[512,768]{1,0:T(8,128)S(1)}, f32[512,768]{1,0:T(8,128)}, u32[]{:S(2)}) copy-start(f32[512,768]{1,0:T(8,128)} %get-tuple-element.87.dh_ref) | copy-start | bytes 4718596
  347.9 6.2 %copy-start.6 = (f32[256,768]{1,0:T(8,128)S(1)}, f32[256,768]{1,0:T(8,128)}, u32[]{:S(2)}) copy-start(f32[256,768]{1,0:T(8,128)} %copy-done.5) | copy-start | bytes 2359300
  347.9 6.2 %copy-start.8 = (f32[256,768]{1,0:T(8,128)S(1)}, f32[256,768]{1,0:T(8,128)}, u32[]{:S(2)}) copy-start(f32[256,768]{1,0:T(8,128)} %copy-done.7) | copy-start | bytes 2359300
  366.4 23.1 %copy-start.1 = (bf16[12,64,768]{2,1,0:T(8,128)(2,1)S(1)}, bf16[12,64,768]{2,1,0:T(8,128)(2,1)}, u32[]{:S(2)}) copy-start(bf16[12,64,768]{2,1,0:T(8,128)(2,1)} %param.21) | copy-start | bytes 3538948
  (43 other events, 68.4 us)

commit v4 on v3

--- a/solution.py
+++ b/solution.py
@@ -18,7 +18,7 @@
 PAIR = 128
 OROWS = 72
 FFB = 512
-WFB = 1024
+WFB = 512
 MB = 512
 
 
@@ -34,41 +34,39 @@
     return pl.CostEstimate(flops=int(flops), bytes_accessed=int(bytes_accessed), transcendentals=int(exps))
 
 
-def proj_kernel(core_ref, m0_ref, m1_ref, wk_ref, wv_ref, k_ref, v_ref, kt_ref, vt_ref):
-    step = pl.program_id(0)
-    half = pl.num_programs(0) // 2
-    for seg, m_ref in enumerate((m0_ref, m1_ref)):
-        @pl.when((step >= half) == (seg == 1))
-        def _():
-            m = m_ref[...]
-            k = dot_nt(m, wk_ref[...]).astype(BF)
-            v = dot_nt(m, wv_ref[...]).astype(BF)
-            k_ref[...] = k
-            v_ref[...] = v
-            kt_ref[...] = k.T
-            vt_ref[...] = v.T
-
-
-def project(core, mem, mem_near, wkt, wvt):
+def proj_kernel(core_ref, m_ref, wk_ref, wv_ref, *refs):
+    k_ref, v_ref, kt_ref, vt_ref = refs[-4:]
+    m = m_ref[...]
+    k = dot_nt(m, wk_ref[...]).astype(BF)
+    v = dot_nt(m, wv_ref[...]).astype(BF)
+    k_ref[...] = k
+    v_ref[...] = v
+    kt_ref[...] = k.T
+    vt_ref[...] = v.T
+
+
+def project(core, mem, wkt, wvt, seg, before):
     rows, dim = mem.shape
     width = wkt.shape[0] // 2
-    half = rows // MB
+    steps = rows // MB
+    base = seg * steps
     weights = pl.BlockSpec((width, dim), lambda i, s: (s[0], 0))
-    down = pl.BlockSpec((MB, width), lambda i, s: (i, 0))
-    across = pl.BlockSpec((width, MB), lambda i, s: (0, i))
+    down = pl.BlockSpec((MB, width), lambda i, s: (base + i, 0))
+    across = pl.BlockSpec((width, MB), lambda i, s: (0, base + i))
     outs = [jax.ShapeDtypeStruct((2 * rows, width), BF)] * 2 + [jax.ShapeDtypeStruct((width, 2 * rows), BF)] * 2
     return pl.pallas_call(
         proj_kernel,
         out_shape=outs,
         grid_spec=pltpu.PrefetchScalarGridSpec(
-            num_scalar_prefetch=1, grid=(2 * half,),
-            in_specs=[pl.BlockSpec((MB, dim), lambda i, s: (jnp.minimum(i, half - 1), 0)),
-                      pl.BlockSpec((MB, dim), lambda i, s: (jnp.maximum(i - half, 0), 0)), weights, weights],
+            num_scalar_prefetch=1, grid=(steps,),
+            in_specs=[pl.BlockSpec((MB, dim), lambda i, s: (i, 0)), weights, weights]
+                     + [pl.BlockSpec(memory_space=pl.ANY)] * len(before),
             out_specs=[down, down, across, across]),
-        compiler_params=pltpu.CompilerParams(vmem_limit_bytes=24 << 20),
-        cost_estimate=cost(8 * rows * dim * width, 24 << 20),
+        input_output_aliases={4 + i: i for i in range(len(before))},
+        compiler_params=pltpu.CompilerParams(vmem_limit_bytes=60 << 20),
+        cost_estimate=cost(4 * rows * dim * width, 12 << 20),
         name="kv_proj",
-    )(core, mem, mem_near, wkt, wvt)
+    )(core, mem, wkt, wvt, *before)
 
 
 def query_kernel(place_ref, x0_ref, x1_ref, x2_ref, x3_ref, gain_ref, wq_ref, x_ref, n_ref, q_ref, qt_ref):
@@ -101,7 +99,7 @@
                                     pl.BlockSpec((width, dim), lambda i, s: (s[n], 0))],
             out_specs=[put, put, pl.BlockSpec((rows, width), lambda i, s: (s[i], 0)),
                        pl.BlockSpec((width, rows), lambda i, s: (0, s[i]))]),
-        compiler_params=pltpu.CompilerParams(vmem_limit_bytes=24 << 20),
+        compiler_params=pltpu.CompilerParams(vmem_limit_bytes=60 << 20),
         cost_estimate=cost(2 * n * rows * dim * width, 6 << 20),
         name="queries",
     )(place, *parts, gain, wqt)
@@ -124,7 +122,7 @@
             num_scalar_prefetch=1, grid=(n,),
             in_specs=[pl.BlockSpec((rows, dim), lambda i, s: (0, 0))] * n,
             out_specs=pl.BlockSpec((rows, dim), lambda i, s: (s[2 * i], 0))),
-        compiler_params=pltpu.CompilerParams(vmem_limit_bytes=16 << 20),
+        compiler_params=pltpu.CompilerParams(vmem_limit_bytes=62 << 20),
         cost_estimate=cost(n * rows * dim, 6 << 20),
         name="place_rows",
     )(place, *parts)
@@ -326,7 +324,7 @@
         out_shape=[jax.ShapeDtypeStruct((2 * PAIR, rows // 2), BF)] * 2
                   + [jax.ShapeDtypeStruct((2, 64, nq), F32), jax.ShapeDtypeStruct((2 * PAIR, mem.shape[1]), F32)],
         grid_spec=spec,
-        compiler_params=pltpu.CompilerParams(vmem_limit_bytes=40 << 20),
+        compiler_params=pltpu.CompilerParams(vmem_limit_bytes=32 << 20),
         cost_estimate=cost(work * 2000, 8 << 20, work),
         name="attn_bwd",
     )(lens, qt, dot_t, lse, delta, k, v, kt, mem, mem_near)
@@ -354,7 +352,7 @@
         out_specs=[fix(2, 64, nq), fix(PAIR, nq), fix(2, 1, nq)],
         out_shape=[jax.ShapeDtypeStruct((2, 64, nq), F32), jax.ShapeDtypeStruct((PAIR, nq), BF),
                    jax.ShapeDtypeStruct((2, 1, nq), F32)],
-        compiler_params=pltpu.CompilerParams(vmem_limit_bytes=16 << 20),
+        compiler_params=pltpu.CompilerParams(vmem_limit_bytes=62 << 20),
         cost_estimate=cost(500 * nq, 2 << 20),
         name="combine",
     )(a, b)
@@ -504,7 +502,7 @@
             num_scalar_prefetch=1, grid=(rows // MB,),
             in_specs=[block] * 6 + [whole, whole],
             out_specs=pl.BlockSpec((MB, dim), lambda i, s: (i, 0))),
-        compiler_params=pltpu.CompilerParams(vmem_limit_bytes=32 << 20),
+        compiler_params=pltpu.CompilerParams(vmem_limit_bytes=60 << 20),
         cost_estimate=cost(4 * rows * dim * dim, 16 << 20),
         name="memory_grad",
     )(core, *mine, *near, wkt, wvt)
@@ -618,7 +616,7 @@
             num_scalar_prefetch=1, grid=(2 * pairs,),
             in_specs=[pl.BlockSpec((2 * PAIR, dim), lambda i, s: (0, 0))] * (4 * pairs),
             out_specs=[out, out]),
-        compiler_params=pltpu.CompilerParams(vmem_limit_bytes=24 << 20),
+        compiler_params=pltpu.CompilerParams(vmem_limit_bytes=60 << 20),
         cost_estimate=cost(4 * pairs * PAIR * dim, 10 << 20),
         name="key_weights",
     )(core, *parts, *others)
@@ -680,8 +678,9 @@
         mem_near = to_near(memory)
         g_parts = (grad_out, to_far(grad_out))
 
-        k, v, kt, vt = project(core1, memory, mem_near, wkt, wvt)
+        first = project(core1, memory, wkt, wvt, 0, ())
         x_all_b, n1, _, qt_s = queries(place, x_parts, gain1, wqt)
+        k, v, kt, vt = project(core1, mem_near, wkt, wvt, 1, first)
 
         pairs = mine // 2
         pieces = [(pair, 0, n * rows) for pair in range(pairs - 1)]
@@ -751,7 +750,8 @@
 
         mine_near = []
         for a, b in dws:
-            mine_near.append((to_near(a), to_near(b)))
+            a_near = to_near(a)
+            mine_near.append((a_near, to_near(b)))
         g_wkt, g_wvt = key_weights(core1, [a for a, _ in dws] + [a for a, _ in mine_near],
                                    [b for _, b in dws] + [b for _, b in mine_near])
         g_wq, g_wk, g_wv = as_weight(g_wqt), as_weight(g_wkt), as_weight(g_wvt)

time: 395 us -> 398 us (level)
  Pallas kernels: 196 us -> 219 us
  local copies, waits for them, and re-layouts: 36.6 us -> 20.2 us
  waiting for transfers between devices: 128 us -> 122 us
    unnamed x147 -> x105, local copies, waits for them, and re-layouts: 33.6 us -> 16.8 us
    pallas_call x4, Pallas kernels: 0.45 us -> 8.2 us  [combine(): pl.pallas_call(combine_kernel, grid=(1,), in_specs=[fix(2, rows, nq)] * 2...]
    ppermute x12, waiting for transfers between devices: 114 us -> 108 us  [to_far(): return lax.ppermute(a, 'seq', far)]
    pallas_call x1 -> x2, Pallas kernels: 10.2 us -> 14.4 us  [project(): pl.pallas_call(proj_kernel, out_shape=outs, grid_spec=pltpu.PrefetchScala...]
  transfers between devices with their start and end apart: 34 -> 34, of which waited for: 11 -> 12; matrix products, arithmetic and copies ran while one was open for 2% -> 2% of each run, Pallas kernels for 27% -> 34%
where the time goes in v4:
time: 398 us; the launch traced here: 392 us
  Pallas kernels  219 us (55%)
  waiting for transfers between devices  122 us (31%)
  starting transfers between devices  22 us (6%)
  local copies, waits for them, and re-layouts  20.2 us (5%)
    ppermute x12, waiting for transfers between devices, to_far(): return lax.ppermute(a, 'seq', far)  108 us
    pallas_call x3, Pallas kernels, attention_backward(): pl.pallas_call(bwd_kernel, out_shape=[jax.ShapeDtypeStruct((2 * PAIR, row...  72.2 us
    pallas_call x4, Pallas kernels, attention_forward(): pl.pallas_call(fwd_kernel, out_shape=jax.ShapeDtypeStruct((2 * pairs, ORO...  45.1 us
    pallas_call x1, Pallas kernels, mlp(): pl.pallas_call(mlp_kernel, grid=(ff // FFB,), in_specs=[fix(rows, dim), f...  21.8 us
    pallas_call x1, Pallas kernels, mlp_weights(): pl.pallas_call(mlp_weights_kernel, grid=(ff // WFB,), in_specs=ins + ins,...  21.4 us
    unnamed x105, local copies, waits for them, and re-layouts  16.8 us
    ppermute x22, waiting for transfers between devices, to_near(): return lax.ppermute(a, 'seq', near)  14.8 us
    ppermute x22, starting transfers between devices, to_near(): return lax.ppermute(a, 'seq', near)  14.7 us
  transfers between devices with their start and end apart: 34, of which 12 were waited for; matrix products, arithmetic and copies ran while one was open for 2% of the time, Pallas kernels for 34%

profile of v4, /device:TPU:5, one launch (start us, length us, event | category | flops | bytes accessed | tf_op | source)
XLA Modules:
  0.0 392.4 jit_solution(17595891277759270555)
XLA Ops:
  0.7 0.7 collective-permute-start.3
  1.4 1.2 collective-permute-start.1
  2.9 9.3 %collective-permute-done.1.x2_ref = bf16[256,768]{1,0:T(8,128)(2,1)S(1)} collective-permute-done((bf16[256,768]{1,0:T(8,128)(2,1)}, bf16[256,768]{1,0:T(8,128)(2,1)S(1)}, u32[]{:S(2)}, u32[]{:S(2)}) %collective-permute-start.1) | collective-permute-done | bytes 393248 | tf_op jit(solution)/shard_map/ppermute | solution.py:653
  12.2 0.9 collective-permute-start.2
  13.8 1.3 reshape.82.gain_ref
  15.7 7.2 %kv_proj.2 = (bf16[4096,384]{1,0:T(8,128)(2,1)}, bf16[4096,384]{1,0:T(8,128)(2,1)}, bf16[384,4096]{1,0:T(8,128)(2,1)}, bf16[384,4096]{1,0:T(8,128)(2,1)}) custom-call(s32[1]{0:T(128)} %bitcast.4.core_ref, bf16[2048,768]{1,0:T(8,128)(2,1)} %m0_ref.5, bf16[768,768]{1,0:T(8,128)(2,1)} %bitcast.40, bf16[768,768]{1,0:T(8,128)(2,1)} %bitcast.43), custom_call_target="tpu_custom_call" | custom-call | flops 2415919104 | bytes 12582912 | tf_op jit(solution)/shard_map/kv_proj/pallas_call | solution.py:57
  22.9 0.7 copy-done.39
  23.7 6.1 %queries.1 = (bf16[1024,768]{1,0:T(8,128)(2,1)}, bf16[1024,768]{1,0:T(8,128)(2,1)}, bf16[1024,384]{1,0:T(8,128)(2,1)}, bf16[384,1024]{1,0:T(8,128)(2,1)}) custom-call(s32[5]{0:T(128)} %stack.32.place_ref, bf16[256,768]{1,0:T(8,128)(2,1)} %x0_ref.2, bf16[256,768]{1,0:T(8,128)(2,1)} %copy-done.39, bf16[256,768]{1,0:T(8,128)(2,1)} %copy-done.38, ...), custom_call_target="tpu_custom_call" | custom-call | flops 603979776 | bytes 6291456 | tf_op jit(solution)/shard_map/queries/pallas_call | solution.py:92
  29.8 7.3 %kv_proj.3 = (bf16[4096,384]{1,0:T(8,128)(2,1)}, bf16[4096,384]{1,0:T(8,128)(2,1)}, bf16[384,4096]{1,0:T(8,128)(2,1)}, bf16[384,4096]{1,0:T(8,128)(2,1)}) custom-call(s32[1]{0:T(128)} %bitcast.4.core_ref, bf16[2048,768]{1,0:T(8,128)(2,1)} %collective-permute-done.3.m_ref.m1_ref, ...), custom_call_target="tpu_custom_call", output_to_operand_aliasing={{0}: (4, {}), {1}: (5, {}), {2}: (6, {}), {3}: (7, {})} | custom-call | flops 2415919104 | bytes 12582912 | tf_op jit(solution)/shard_map/kv_proj/pallas_call | solution.py:57
  37.1 1.9 copy-done.2
  39.0 1.9 copy-done.6
  40.8 7.6 %attn_fwd.6.a_ref = f32[2,72,512]{2,1,0:T(8,128)S(1)} custom-call(s32[2]{0:T(128)S(1)} %pad_add_fusion.len_ref, bf16[384,1024]{1,0:T(8,128)(2,1)S(1)} %copy-done.19, bf16[4096,384]{1,0:T(8,128)(2,1)S(1)} %copy-done.2, bf16[384,4096]{1,0:T(8,128)(2,1)S(1)} %copy-done.6), custom_call_target="tpu_custom_call" | custom-call | flops 4294967296 | bytes 4194304 | tf_op jit(solution)/shard_map/attn_fwd/pallas_call | solution.py:214
  48.4 14.3 %attn_fwd.5.a_ref = f32[2,72,1024]{2,1,0:T(8,128)S(1)} custom-call(s32[2]{0:T(128)S(1)} %pad_add_fusion.len_ref, bf16[384,1024]{1,0:T(8,128)(2,1)S(1)} %copy-done.19, bf16[4096,384]{1,0:T(8,128)(2,1)S(1)} %copy-done.2, bf16[384,4096]{1,0:T(8,128)(2,1)S(1)} %copy-done.6), custom_call_target="tpu_custom_call" | custom-call | flops 8589934592 | bytes 4194304 | tf_op jit(solution)/shard_map/attn_fwd/pallas_call | solution.py:214
  62.7 14.9 %attn_fwd.4.a_ref = f32[2,72,1024]{2,1,0:T(8,128)} custom-call(s32[2]{0:T(128)S(1)} %pad_add_fusion.len_ref, bf16[384,1024]{1,0:T(8,128)(2,1)S(1)} %copy-done.19, bf16[4096,384]{1,0:T(8,128)(2,1)S(1)} %copy-done.2, bf16[384,4096]{1,0:T(8,128)(2,1)S(1)} %copy-done.6), custom_call_target="tpu_custom_call" | custom-call | flops 8589934592 | bytes 4194304 | tf_op jit(solution)/shard_map/attn_fwd/pallas_call | solution.py:214
  77.7 1.5 collective-permute-start.4
  79.2 8.3 %attn_fwd.7.a_ref = f32[2,72,512]{2,1,0:T(8,128)} custom-call(s32[2]{0:T(128)S(1)} %pad_add_fusion.len_ref, bf16[384,1024]{1,0:T(8,128)(2,1)S(1)} %copy-done.19, bf16[4096,384]{1,0:T(8,128)(2,1)S(1)} %copy-done.2, bf16[384,4096]{1,0:T(8,128)(2,1)S(1)} %copy-done.6), custom_call_target="tpu_custom_call" | custom-call | flops 4294967296 | bytes 4194304 | tf_op jit(solution)/shard_map/attn_fwd/pallas_call | solution.py:214
  87.5 1.5 collective-permute-start.9
  89.0 1.9 combine.6
  90.8 27.1 %collective-permute-done.7.b_ref = f32[2,72,512]{2,1,0:T(8,128)} collective-permute-done((f32[2,72,512]{2,1,0:T(8,128)}, f32[2,72,512]{2,1,0:T(8,128)}, u32[]{:S(2)}, u32[]{:S(2)}) %collective-permute-start.7) | collective-permute-done | bytes 294944 | tf_op jit(solution)/shard_map/ppermute | solution.py:653
  117.9 1.9 combine.7
  119.8 2.2 combine.4
  122.0 2.2 combine.5
  124.3 1.2 maximum_maximum_fusion.mine_ref
  125.5 0.9 fusion.13
  126.4 1.3 collective-permute-start.8
  128.4 6.4 %collective-permute-done.9.x1_ref = f32[256,768]{1,0:T(8,128)} collective-permute-done((f32[256,768]{1,0:T(8,128)}, f32[256,768]{1,0:T(8,128)}, u32[]{:S(2)}, u32[]{:S(2)}) %collective-permute-start.9) | collective-permute-done | bytes 786464 | tf_op jit(solution)/shard_map/ppermute | solution.py:653
  134.8 3.3 place_rows.1.g_ref
  138.7 0.8 copy-done.12
  139.4 2.5 add_convert_fusion.h_ref
  142.0 21.8 %mlp.1 = (bf16[768,512]{1,0:T(8,128)(2,1)}, bf16[512,768]{1,0:T(8,128)(2,1)}, bf16[512,3072]{1,0:T(8,128)(2,1)}, bf16[512,3072]{1,0:T(8,128)(2,1)}, bf16[3072,51...) custom-call(bf16[512,768]{1,0:T(8,128)(2,1)} %add_convert_fusion.h_ref, ...), custom_call_target="tpu_custom_call" | custom-call | flops 12079595520 | bytes 41943040 | tf_op jit(solution)/shard_map/mlp/pallas_call | solution.py:440
  163.8 0.9 collective-permute-start.10
  164.8 1.3 constant_dynamic-update-slice_fusion.1
  166.1 0.7 collective-permute-done.10
  166.9 0.8 fusion.14
  169.1 1.2 copy-done.3
  170.3 24.3 %attn_bwd.3 = (bf16[256,2048]{1,0:T(8,128)(2,1)S(1)}, bf16[256,2048]{1,0:T(8,128)(2,1)S(1)}, f32[2,64,1024]{2,1,0:T(8,128)S(1)}, f32[256,768]{1,0:T(8,128)S(1)}) custom-call(s32[2]{0:T(128)S(1)} %pad_add_fusion.len_ref, bf16[384,1024]{1,0:T(8,128)(2,1)S(1)} %copy-done.20, bf16[384,1024]{1,0:T(8,128)(2,1)S(1)} %get-tuple-element.119.dot_ref, ...), custom_call_target="tpu_custom_call" | custom-call | flops 16777216000 | bytes 8388608 | tf_op jit(solution)/shard_map/attn_bwd/pallas_call | solution.py:322
  194.6 1.0 copy-done.24
  195.6 23.9 %attn_bwd.4 = (bf16[256,2048]{1,0:T(8,128)(2,1)S(1)}, bf16[256,2048]{1,0:T(8,128)(2,1)S(1)}, f32[2,64,1024]{2,1,0:T(8,128)S(1)}, f32[256,768]{1,0:T(8,128)S(1)}) custom-call(s32[2]{0:T(128)S(1)} %pad_add_fusion.len_ref, bf16[384,1024]{1,0:T(8,128)(2,1)S(1)} %copy-done.20, bf16[384,1024]{1,0:T(8,128)(2,1)S(1)} %get-tuple-element.119.dot_ref, ...), custom_call_target="tpu_custom_call" | custom-call | flops 16777216000 | bytes 8388608 | tf_op jit(solution)/shard_map/attn_bwd/pallas_call | solution.py:322
  219.5 1.0 copy-done.25
  220.5 24.0 %attn_bwd.5 = (bf16[256,2048]{1,0:T(8,128)(2,1)S(1)}, bf16[256,2048]{1,0:T(8,128)(2,1)S(1)}, f32[2,64,1024]{2,1,0:T(8,128)S(1)}, f32[256,768]{1,0:T(8,128)S(1)}) custom-call(s32[2]{0:T(128)S(1)} %pad_add_fusion.len_ref, bf16[384,1024]{1,0:T(8,128)(2,1)S(1)} %copy-done.20, bf16[384,1024]{1,0:T(8,128)(2,1)S(1)} %get-tuple-element.119.dot_ref, ...), custom_call_target="tpu_custom_call" | custom-call | flops 16777216000 | bytes 8388608 | tf_op jit(solution)/shard_map/attn_bwd/pallas_call | solution.py:322
  245.0 1.7 collective-permute-start.21
  247.5 0.9 collective-permute-start.23
  248.4 9.2 %collective-permute-done.13.b2_ref = f32[2,64,1024]{2,1,0:T(8,128)S(1)} collective-permute-done((f32[2,64,1024]{2,1,0:T(8,128)S(1)}, f32[2,64,1024]{2,1,0:T(8,128)S(1)}, u32[]{:S(2)}, u32[]{:S(2)}) %collective-permute-start.13) | collective-permute-done | bytes 524320 | tf_op jit(solution)/shard_map/ppermute | solution.py:653
  257.7 2.1 collective-permute-start.20
  259.7 26.0 %collective-permute-done.12.b1_ref = f32[2,64,1024]{2,1,0:T(8,128)S(1)} collective-permute-done((f32[2,64,1024]{2,1,0:T(8,128)S(1)}, f32[2,64,1024]{2,1,0:T(8,128)S(1)}, u32[]{:S(2)}, u32[]{:S(2)}) %collective-permute-start.12) | collective-permute-done | bytes 524320 | tf_op jit(solution)/shard_map/ppermute | solution.py:653
  285.8 2.1 collective-permute-start.15
  287.9 14.7 %collective-permute-done.23.refs_8_ = f32[256,768]{1,0:T(8,128)S(1)} collective-permute-done((f32[256,768]{1,0:T(8,128)S(1)}, f32[256,768]{1,0:T(8,128)S(1)}, u32[]{:S(2)}, u32[]{:S(2)}) %collective-permute-start.23) | collective-permute-done | bytes 786464 | tf_op jit(solution)/shard_map/ppermute | solution.py:653
  302.6 2.1 collective-permute-start.17
  304.7 14.8 %collective-permute-done.22.refs_7_ = f32[256,768]{1,0:T(8,128)S(1)} collective-permute-done((f32[256,768]{1,0:T(8,128)S(1)}, f32[256,768]{1,0:T(8,128)S(1)}, u32[]{:S(2)}, u32[]{:S(2)}) %collective-permute-start.22) | collective-permute-done | bytes 786464 | tf_op jit(solution)/shard_map/ppermute | solution.py:653
  319.5 1.2 collective-permute-start.31
  320.7 0.9 copy-done.32
  323.0 0.7 copy-done.50
  324.0 12.3 %collective-permute-done.14.near_ref = bf16[384,1024]{1,0:T(8,128)(2,1)S(1)} collective-permute-done((bf16[384,1024]{1,0:T(8,128)(2,1)S(1)}, bf16[384,1024]{1,0:T(8,128)(2,1)S(1)}, u32[]{:S(2)}, u32[]{:S(2)}) %collective-permute-start.14) | collective-permute-done | bytes 786464 | tf_op jit(solution)/shard_map/ppermute | solution.py:650
  336.7 0.7 collective-permute-done.24.refs_9_
  337.8 0.6 add_reduce_fusion
  339.0 0.7 collective-permute-done.25.refs_10_
  340.1 3.6 out_proj_grad.1
  343.8 10.0 %memory_grad.1 = f32[2048,768]{1,0:T(8,128)} custom-call(s32[1]{0:T(128)} %bitcast.4.core_ref, bf16[256,2048]{1,0:T(8,128)(2,1)} %copy-done.24, bf16[256,2048]{1,0:T(8,128)(2,1)} %copy-done.25, bf16[256,2048]{1,0:T(8,128)(2,1)} %copy-done.26, bf16[256,2048]{1,0:T(8,128)(2,1)} %copy-done.49, bf16[256,2048]{1,0:T(8,128)(2,1)} %copy-done.51, ...), custom_call_target="tpu_custom_call" | custom-call | flops 4831838208 | bytes 16777216 | tf_op jit(solution)/shard_map/memory_grad/pallas_call | solution.py:498
  353.8 1.4 copy-done.18
  355.2 1.1 copy-done.22
  356.3 1.4 copy-done.23
  357.7 5.5 %query_grad.1 = (f32[768,768]{1,0:T(8,128)}, f32[256,768]{1,0:T(8,128)}, f32[1,768]{1,0:T(1,128)S(1)}) custom-call(s32[5]{0:T(128)S(1)} %copy-done.16, bf16[384,1024]{1,0:T(8,128)(2,1)S(1)} %sum_queries.1.mine_ref, bf16[384,1024]{1,0:T(8,128)(2,1)S(1)} %copy-done.22, bf16[1024,768]{1,0:T(8,128)(2,1)S(1)} %copy-done.18, bf16[768,768]{1,0:T(8,128)(2,1)S(1)} %bitcast.37, ...), custom_call_target="tpu_custom_call" | custom-call | flops 2415919104 | bytes 10485760 | tf_op jit(solution)/shard_map/query_grad/pallas_call | solution.py:581
  363.8 6.9 %key_weights.1 = (f32[768,768]{1,0:T(8,128)}, f32[768,768]{1,0:T(8,128)}) custom-call(s32[1]{0:T(128)} %bitcast.4.core_ref, f32[256,768]{1,0:T(8,128)} %copy-done.8, f32[256,768]{1,0:T(8,128)} %copy-done.9, f32[256,768]{1,0:T(8,128)} %copy-done.10, f32[256,768]{1,0:T(8,128)} %copy-done.28, f32[256,768]{1,0:T(8,128)} %copy-done.32, f32[256,768]{1,0:T(8,128)} %copy-done.30, ...), custom_call_target="tpu_custom_call" | custom-call | flops 1179648 | bytes 10485760 | tf_op jit(solution)/shard_map/key_weights/pallas_call | solution.py:612
  370.8 21.4 %mlp_weights.1 = (f32[768,3072]{1,0:T(8,128)}, f32[768,3072]{1,0:T(8,128)}, f32[3072,768]{1,0:T(8,128)}) custom-call(bf16[768,512]{1,0:T(8,128)(2,1)} %get-tuple-element.109.n2t_ref, bf16[512,768]{1,0:T(8,128)(2,1)} %get-tuple-element.110.gt_ref, bf16[512,3072]{1,0:T(8,128)(2,1)} %get-tuple-element.111.dgate_ref, ...), custom_call_target="tpu_custom_call" | custom-call | flops 14495514624 | bytes 52428800 | tf_op jit(solution)/shard_map/mlp_weights/pallas_call | solution.py:470
  (146 shorter events, 9.2 us)
Async XLA Ops:
  0.6 137.4 %copy-start = (bf16[12,64,768]{2,1,0:T(8,128)(2,1)S(1)}, bf16[12,64,768]{2,1,0:T(8,128)(2,1)}, u32[]{:S(2)}) copy-start(bf16[12,64,768]{2,1,0:T(8,128)(2,1)} %param.21) | copy-start | bytes 3538948
  0.7 29.1 %collective-permute-start.3 = (bf16[2048,768]{1,0:T(8,128)(2,1)}, bf16[2048,768]{1,0:T(8,128)(2,1)}, u32[]{:S(2)}, u32[]{:S(2)}) collective-permute-start(bf16[2048,768]{1,0:T(8,128)(2,1)} %m0_ref.5), channel_id=1, source_target_pairs={{0,1},{1,0},{2,3},{3,2},{4,5},{5,4},{6,7},{7,6}} | collective-permute-start | bytes 9437192 | tf_op jit(solution)/shard_map/ppermute | solution.py:650
  1.4 10.8 %collective-permute-start.1 = (bf16[256,768]{1,0:T(8,128)(2,1)}, bf16[256,768]{1,0:T(8,128)(2,1)S(1)}, u32[]{:S(2)}, u32[]{:S(2)}) collective-permute-start(bf16[256,768]{1,0:T(8,128)(2,1)} %x0_ref.2), channel_id=1, source_target_pairs={{0,2},{1,3},{2,0},{3,1},{4,6},{5,7},{6,4},{7,5}} | collective-permute-start | bytes 1179656 | tf_op jit(solution)/shard_map/ppermute | solution.py:653
  2.6 20.3 %collective-permute-start = (bf16[256,768]{1,0:T(8,128)(2,1)}, bf16[256,768]{1,0:T(8,128)(2,1)S(1)}, u32[]{:S(2)}, u32[]{:S(2)}) collective-permute-start(bf16[256,768]{1,0:T(8,128)(2,1)} %x0_ref.2), channel_id=1, source_target_pairs={{0,1},{1,0},{2,3},{3,2},{4,5},{5,4},{6,7},{7,6}} | collective-permute-start | bytes 1179656 | tf_op jit(solution)/shard_map/ppermute | solution.py:650
  12.2 10.6 %copy-start.38 = (bf16[256,768]{1,0:T(8,128)(2,1)}, bf16[256,768]{1,0:T(8,128)(2,1)S(1)}, u32[]{:S(2)}) copy-start(bf16[256,768]{1,0:T(8,128)(2,1)S(1)} %collective-permute-done.1.x2_ref) | copy-start | bytes 1179652
  12.2 10.7 %collective-permute-start.2 = (bf16[256,768]{1,0:T(8,128)(2,1)S(1)}, bf16[256,768]{1,0:T(8,128)(2,1)S(1)}, u32[]{:S(2)}, u32[]{:S(2)}) collective-permute-start(bf16[256,768]{1,0:T(8,128)(2,1)S(1)} %collective-permute-done.1.x2_ref), channel_id=1, source_target_pairs={{0,1},{1,0},{2,3},{3,2},{4,5},{5,4},{6,7},{7,6}} | collective-permute-start | bytes 1179656 | tf_op jit(solution)/shard_map/ppermute | solution.py:650
  29.8 7.3 %copy-start.19 = (bf16[384,1024]{1,0:T(8,128)(2,1)S(1)}, bf16[384,1024]{1,0:T(8,128)(2,1)}, u32[]{:S(2)}) copy-start(bf16[384,1024]{1,0:T(8,128)(2,1)} %get-tuple-element.64.qt_ref) | copy-start | bytes 2359300
  48.4 29.3 %copy-start.14 = (f32[2,72,512]{2,1,0:T(8,128)}, f32[2,72,512]{2,1,0:T(8,128)S(1)}, u32[]{:S(2)}) copy-start(f32[2,72,512]{2,1,0:T(8,128)S(1)} %attn_fwd.6.a_ref) | copy-start | bytes 884740
  62.7 16.4 %copy-start.11 = (f32[2,72,1024]{2,1,0:T(8,128)}, f32[2,72,1024]{2,1,0:T(8,128)S(1)}, u32[]{:S(2)}) copy-start(f32[2,72,1024]{2,1,0:T(8,128)S(1)} %attn_fwd.5.a_ref) | copy-start | bytes 1769476
  77.7 11.3 %collective-permute-start.6 = (f32[2,72,512]{2,1,0:T(8,128)S(1)}, f32[2,72,512]{2,1,0:T(8,128)}, u32[]{:S(2)}, u32[]{:S(2)}) collective-permute-start(f32[2,72,512]{2,1,0:T(8,128)S(1)} %attn_fwd.6.a_ref), channel_id=1, source_target_pairs={{0,2},{1,3},{2,0},{3,1},{4,6},{5,7},{6,4},{7,5}} | collective-permute-start | bytes 884744 | tf_op jit(solution)/shard_map/ppermute | solution.py:653
  77.7 42.1 %collective-permute-start.4 = (f32[2,72,1024]{2,1,0:T(8,128)}, f32[2,72,1024]{2,1,0:T(8,128)}, u32[]{:S(2)}, u32[]{:S(2)}) collective-permute-start(f32[2,72,1024]{2,1,0:T(8,128)} %attn_fwd.4.a_ref), channel_id=1, source_target_pairs={{0,2},{1,3},{2,0},{3,1},{4,6},{5,7},{6,4},{7,5}} | collective-permute-start | bytes 1769480 | tf_op jit(solution)/shard_map/ppermute | solution.py:653
  79.1 42.9 %collective-permute-start.5 = (f32[2,72,1024]{2,1,0:T(8,128)S(1)}, f32[2,72,1024]{2,1,0:T(8,128)}, u32[]{:S(2)}, u32[]{:S(2)}) collective-permute-start(f32[2,72,1024]{2,1,0:T(8,128)S(1)} %attn_fwd.5.a_ref), channel_id=1, source_target_pairs={{0,2},{1,3},{2,0},{3,1},{4,6},{5,7},{6,4},{7,5}} | collective-permute-start | bytes 1769480 | tf_op jit(solution)/shard_map/ppermute | solution.py:653
  87.5 30.4 %collective-permute-start.7 = (f32[2,72,512]{2,1,0:T(8,128)}, f32[2,72,512]{2,1,0:T(8,128)}, u32[]{:S(2)}, u32[]{:S(2)}) collective-permute-start(f32[2,72,512]{2,1,0:T(8,128)} %attn_fwd.7.a_ref), channel_id=1, source_target_pairs={{0,2},{1,3},{2,0},{3,1},{4,6},{5,7},{6,4},{7,5}} | collective-permute-start | bytes 884744 | tf_op jit(solution)/shard_map/ppermute | solution.py:653
  87.5 47.3 %collective-permute-start.9 = (f32[256,768]{1,0:T(8,128)}, f32[256,768]{1,0:T(8,128)}, u32[]{:S(2)}, u32[]{:S(2)}) collective-permute-start(f32[256,768]{1,0:T(8,128)} %x0_ref.3), channel_id=1, source_target_pairs={{0,2},{1,3},{2,0},{3,1},{4,6},{5,7},{6,4},{7,5}} | collective-permute-start | bytes 2359304 | tf_op jit(solution)/shard_map/ppermute | solution.py:653
  126.4 12.2 %collective-permute-start.8 = (bf16[384,512]{1,0:T(8,128)(2,1)}, bf16[384,512]{1,0:T(8,128)(2,1)}, u32[]{:S(2)}, u32[]{:S(2)}) collective-permute-start(bf16[384,512]{1,0:T(8,128)(2,1)} %get-tuple-element.118), channel_id=1, source_target_pairs={{0,1},{1,0},{2,3},{3,2},{4,5},{5,4},{6,7},{7,6}} | collective-permute-start | bytes 1179656 | tf_op jit(solution)/shard_map/ppermute | solution.py:650
  141.9 22.8 %copy-start.43 = (f32[2,1,1024]{2,1,0:T(1,128)S(1)}, f32[2,1,1024]{2,1,0:T(1,128)}, u32[]{:S(2)}) copy-start(f32[2,1,1024]{2,1,0:T(1,128)} %get-tuple-element.77) | copy-start | bytes 24580
  141.9 22.8 %copy-start.44 = (f32[2,1,1024]{2,1,0:T(1,128)S(1)}, f32[2,1,1024]{2,1,0:T(1,128)}, u32[]{:S(2)}) copy-start(f32[2,1,1024]{2,1,0:T(1,128)} %get-tuple-element.78) | copy-start | bytes 24580
  141.9 22.8 %copy-start.45 = (f32[2,1,512]{2,1,0:T(1,128)S(1)}, f32[2,1,512]{2,1,0:T(1,128)}, u32[]{:S(2)}) copy-start(f32[2,1,512]{2,1,0:T(1,128)} %get-tuple-element.79) | copy-start | bytes 12292
  141.9 22.8 %copy-start.46 = (f32[2,1,512]{2,1,0:T(1,128)S(1)}, f32[2,1,512]{2,1,0:T(1,128)}, u32[]{:S(2)}) copy-start(f32[2,1,512]{2,1,0:T(1,128)} %get-tuple-element.80) | copy-start | bytes 12292
  141.9 25.8 %copy-start.37 = (f32[2,64,1024]{2,1,0:T(8,128)S(1)}, f32[2,64,1024]{2,1,0:T(8,128)}, u32[]{:S(2)}) copy-start(f32[2,64,1024]{2,1,0:T(8,128)} %get-tuple-element.82) | copy-start | bytes 1572868
  142.0 25.8 %copy-start.41 = (f32[2,64,512]{2,1,0:T(8,128)S(1)}, f32[2,64,512]{2,1,0:T(8,128)}, u32[]{:S(2)}) copy-start(f32[2,64,512]{2,1,0:T(8,128)} %get-tuple-element.83) | copy-start | bytes 786436
  142.0 25.8 %copy-start.42 = (f32[2,64,512]{2,1,0:T(8,128)S(1)}, f32[2,64,512]{2,1,0:T(8,128)}, u32[]{:S(2)}) copy-start(f32[2,64,512]{2,1,0:T(8,128)} %get-tuple-element.84) | copy-start | bytes 786436
  142.0 26.4 %copy-start.17 = (bf16[2048,768]{1,0:T(8,128)(2,1)S(1)}, bf16[2048,768]{1,0:T(8,128)(2,1)}, u32[]{:S(2)}) copy-start(bf16[2048,768]{1,0:T(8,128)(2,1)} %m0_ref.5) | copy-start | bytes 9437188
  163.8 3.0 collective-permute-start.10
  164.7 82.0 %collective-permute-start.27 = (bf16[384,512]{1,0:T(8,128)(2,1)}, bf16[384,512]{1,0:T(8,128)(2,1)S(1)}, u32[]{:S(2)}, u32[]{:S(2)}) collective-permute-start(bf16[384,512]{1,0:T(8,128)(2,1)} %get-tuple-element.117), channel_id=1, source_target_pairs={{0,1},{1,0},{2,3},{3,2},{4,5},{5,4},{6,7},{7,6}} | collective-permute-start | bytes 1179656 | tf_op jit(solution)/shard_map/ppermute | solution.py:650
  195.6 51.1 %copy-start.8 = (f32[256,768]{1,0:T(8,128)}, f32[256,768]{1,0:T(8,128)S(1)}, u32[]{:S(2)}) copy-start(f32[256,768]{1,0:T(8,128)S(1)} %get-tuple-element.88.refs_0_) | copy-start | bytes 2359300
  195.6 51.9 %collective-permute-start.11 = (f32[2,64,1024]{2,1,0:T(8,128)S(1)}, f32[2,64,1024]{2,1,0:T(8,128)S(1)}, u32[]{:S(2)}, u32[]{:S(2)}) collective-permute-start(f32[2,64,1024]{2,1,0:T(8,128)S(1)} %get-tuple-element.87.a0_ref), channel_id=1, source_target_pairs={{0,2},{1,3},{2,0},{3,1},{4,6},{5,7},{6,4},{7,5}} | collective-permute-start | bytes 1572872 | tf_op jit(solution)/shard_map/ppermute | solution.py:653
  220.5 67.4 %copy-start.9 = (f32[256,768]{1,0:T(8,128)}, f32[256,768]{1,0:T(8,128)S(1)}, u32[]{:S(2)}) copy-start(f32[256,768]{1,0:T(8,128)S(1)} %get-tuple-element.91.refs_1_) | copy-start | bytes 2359300
  220.5 24.1 %copy-start.47 = (f32[1,768]{1,0:T(1,128)S(1)}, f32[1,768]{1,0:T(1,128)}, u32[]{:S(2)}) copy-start(f32[1,768]{1,0:T(1,128)} %get-tuple-element.108) | copy-start | bytes 9220
  244.5 78.2 %copy-start.10 = (f32[256,768]{1,0:T(8,128)}, f32[256,768]{1,0:T(8,128)S(1)}, u32[]{:S(2)}) copy-start(f32[256,768]{1,0:T(8,128)S(1)} %get-tuple-element.105.refs_2_) | copy-start | bytes 2359300
  244.5 78.2 %copy-start.26 = (bf16[256,2048]{1,0:T(8,128)(2,1)}, bf16[256,2048]{1,0:T(8,128)(2,1)S(1)}, u32[]{:S(2)}) copy-start(bf16[256,2048]{1,0:T(8,128)(2,1)S(1)} %get-tuple-element.99.a2_ref) | copy-start | bytes 3145732
  244.5 13.1 %collective-permute-start.13 = (f32[2,64,1024]{2,1,0:T(8,128)S(1)}, f32[2,64,1024]{2,1,0:T(8,128)S(1)}, u32[]{:S(2)}, u32[]{:S(2)}) collective-permute-start(f32[2,64,1024]{2,1,0:T(8,128)S(1)} %get-tuple-element.93.a2_ref), channel_id=1, source_target_pairs={{0,2},{1,3},{2,0},{3,1},{4,6},{5,7},{6,4},{7,5}} | collective-permute-start | bytes 1572872 | tf_op jit(solution)/shard_map/ppermute | solution.py:653
  244.6 2.4 collective-permute-start.28
  245.0 42.8 %collective-permute-start.21 = (f32[256,768]{1,0:T(8,128)S(1)}, f32[256,768]{1,0:T(8,128)S(1)}, u32[]{:S(2)}, u32[]{:S(2)}) collective-permute-start(f32[256,768]{1,0:T(8,128)S(1)} %get-tuple-element.88.refs_0_), channel_id=1, source_target_pairs={{0,2},{1,3},{2,0},{3,1},{4,6},{5,7},{6,4},{7,5}} | collective-permute-start | bytes 2359304 | tf_op jit(solution)/shard_map/ppermute | solution.py:653
  246.7 41.1 %collective-permute-start.18 = (f32[256,768]{1,0:T(8,128)S(1)}, f32[256,768]{1,0:T(8,128)S(1)}, u32[]{:S(2)}, u32[]{:S(2)}) collective-permute-start(f32[256,768]{1,0:T(8,128)S(1)} %get-tuple-element.88.refs_0_), channel_id=1, source_target_pairs={{0,1},{1,0},{2,3},{3,2},{4,5},{5,4},{6,7},{7,6}} | collective-permute-start | bytes 2359304 | tf_op jit(solution)/shard_map/ppermute | solution.py:650
  247.0 38.8 %collective-permute-start.12 = (f32[2,64,1024]{2,1,0:T(8,128)S(1)}, f32[2,64,1024]{2,1,0:T(8,128)S(1)}, u32[]{:S(2)}, u32[]{:S(2)}) collective-permute-start(f32[2,64,1024]{2,1,0:T(8,128)S(1)} %get-tuple-element.90.a1_ref), channel_id=1, source_target_pairs={{0,2},{1,3},{2,0},{3,1},{4,6},{5,7},{6,4},{7,5}} | collective-permute-start | bytes 1572872 | tf_op jit(solution)/shard_map/ppermute | solution.py:653
  247.5 55.1 %collective-permute-start.23 = (f32[256,768]{1,0:T(8,128)S(1)}, f32[256,768]{1,0:T(8,128)S(1)}, u32[]{:S(2)}, u32[]{:S(2)}) collective-permute-start(f32[256,768]{1,0:T(8,128)S(1)} %get-tuple-element.105.refs_2_), channel_id=1, source_target_pairs={{0,2},{1,3},{2,0},{3,1},{4,6},{5,7},{6,4},{7,5}} | collective-permute-start | bytes 2359304 | tf_op jit(solution)/shard_map/ppermute | solution.py:653
  257.7 47.0 %collective-permute-start.20 = (f32[256,768]{1,0:T(8,128)S(1)}, f32[256,768]{1,0:T(8,128)S(1)}, u32[]{:S(2)}, u32[]{:S(2)}) collective-permute-start(f32[256,768]{1,0:T(8,128)S(1)} %get-tuple-element.105.refs_2_), channel_id=1, source_target_pairs={{0,1},{1,0},{2,3},{3,2},{4,5},{5,4},{6,7},{7,6}} | collective-permute-start | bytes 2359304 | tf_op jit(solution)/shard_map/ppermute | solution.py:650
  285.8 35.0 %collective-permute-start.15 = (bf16[256,2048]{1,0:T(8,128)(2,1)S(1)}, bf16[256,2048]{1,0:T(8,128)(2,1)S(1)}, u32[]{:S(2)}, u32[]{:S(2)}) collective-permute-start(bf16[256,2048]{1,0:T(8,128)(2,1)S(1)} %get-tuple-element.100), channel_id=1, source_target_pairs={{0,1},{1,0},{2,3},{3,2},{4,5},{5,4},{6,7},{7,6}} | collective-permute-start | bytes 3145736 | tf_op jit(solution)/shard_map/ppermute | solution.py:650
  287.8 35.9 %copy-start.27 = (f32[256,768]{1,0:T(8,128)}, f32[256,768]{1,0:T(8,128)S(1)}, u32[]{:S(2)}) copy-start(f32[256,768]{1,0:T(8,128)S(1)} %collective-permute-done.21.refs_6_) | copy-start | bytes 2359300
  287.8 31.6 %collective-permute-start.22 = (f32[256,768]{1,0:T(8,128)S(1)}, f32[256,768]{1,0:T(8,128)S(1)}, u32[]{:S(2)}, u32[]{:S(2)}) collective-permute-start(f32[256,768]{1,0:T(8,128)S(1)} %get-tuple-element.91.refs_1_), channel_id=1, source_target_pairs={{0,2},{1,3},{2,0},{3,1},{4,6},{5,7},{6,4},{7,5}} | collective-permute-start | bytes 2359304 | tf_op jit(solution)/shard_map/ppermute | solution.py:653
  287.8 34.8 %copy-start.28 = (f32[256,768]{1,0:T(8,128)}, f32[256,768]{1,0:T(8,128)S(1)}, u32[]{:S(2)}) copy-start(f32[256,768]{1,0:T(8,128)S(1)} %collective-permute-done.18.refs_3_) | copy-start | bytes 2359300
  287.8 32.8 %collective-permute-start.19 = (f32[256,768]{1,0:T(8,128)S(1)}, f32[256,768]{1,0:T(8,128)S(1)}, u32[]{:S(2)}, u32[]{:S(2)}) collective-permute-start(f32[256,768]{1,0:T(8,128)S(1)} %get-tuple-element.91.refs_1_), channel_id=1, source_target_pairs={{0,1},{1,0},{2,3},{3,2},{4,5},{5,4},{6,7},{7,6}} | collective-permute-start | bytes 2359304 | tf_op jit(solution)/shard_map/ppermute | solution.py:650
  302.6 41.1 %copy-start.29 = (f32[256,768]{1,0:T(8,128)}, f32[256,768]{1,0:T(8,128)S(1)}, u32[]{:S(2)}) copy-start(f32[256,768]{1,0:T(8,128)S(1)} %collective-permute-done.23.refs_8_) | copy-start | bytes 2359300
  302.6 20.1 %collective-permute-start.17 = (bf16[256,2048]{1,0:T(8,128)(2,1)S(1)}, bf16[256,2048]{1,0:T(8,128)(2,1)S(1)}, u32[]{:S(2)}, u32[]{:S(2)}) collective-permute-start(bf16[256,2048]{1,0:T(8,128)(2,1)S(1)} %get-tuple-element.102), channel_id=1, source_target_pairs={{0,1},{1,0},{2,3},{3,2},{4,5},{5,4},{6,7},{7,6}} | collective-permute-start | bytes 3145736 | tf_op jit(solution)/shard_map/ppermute | solution.py:650
  304.7 39.0 %copy-start.30 = (f32[256,768]{1,0:T(8,128)}, f32[256,768]{1,0:T(8,128)S(1)}, u32[]{:S(2)}) copy-start(f32[256,768]{1,0:T(8,128)S(1)} %collective-permute-done.20.refs_5_) | copy-start | bytes 2359300
  304.7 19.0 %collective-permute-start.16 = (bf16[256,2048]{1,0:T(8,128)(2,1)S(1)}, bf16[256,2048]{1,0:T(8,128)(2,1)S(1)}, u32[]{:S(2)}, u32[]{:S(2)}) collective-permute-start(bf16[256,2048]{1,0:T(8,128)(2,1)S(1)} %get-tuple-element.101), channel_id=1, source_target_pairs={{0,1},{1,0},{2,3},{3,2},{4,5},{5,4},{6,7},{7,6}} | collective-permute-start | bytes 3145736 | tf_op jit(solution)/shard_map/ppermute | solution.py:650
  319.5 24.2 %copy-start.31 = (f32[256,768]{1,0:T(8,128)}, f32[256,768]{1,0:T(8,128)S(1)}, u32[]{:S(2)}) copy-start(f32[256,768]{1,0:T(8,128)S(1)} %collective-permute-done.22.refs_7_) | copy-start | bytes 2359300
  319.5 51.3 %collective-permute-start.31 = (bf16[512,3072]{1,0:T(8,128)(2,1)}, bf16[512,3072]{1,0:T(8,128)(2,1)}, u32[]{:S(2)}, u32[]{:S(2)}) collective-permute-start(bf16[512,3072]{1,0:T(8,128)(2,1)} %get-tuple-element.111.dgate_ref), channel_id=1, source_target_pairs={{0,1},{1,0},{2,3},{3,2},{4,5},{5,4},{6,7},{7,6}} | collective-permute-start | bytes 9437192 | tf_op jit(solution)/shard_map/ppermute | solution.py:650
  320.7 50.0 %collective-permute-start.32 = (bf16[512,3072]{1,0:T(8,128)(2,1)}, bf16[512,3072]{1,0:T(8,128)(2,1)}, u32[]{:S(2)}, u32[]{:S(2)}) collective-permute-start(bf16[512,3072]{1,0:T(8,128)(2,1)} %get-tuple-element.112.dup_ref), channel_id=1, source_target_pairs={{0,1},{1,0},{2,3},{3,2},{4,5},{5,4},{6,7},{7,6}} | collective-permute-start | bytes 9437192 | tf_op jit(solution)/shard_map/ppermute | solution.py:650
  321.9 48.8 %collective-permute-start.33 = (bf16[3072,512]{1,0:T(8,128)(2,1)}, bf16[3072,512]{1,0:T(8,128)(2,1)}, u32[]{:S(2)}, u32[]{:S(2)}) collective-permute-start(bf16[3072,512]{1,0:T(8,128)(2,1)} %get-tuple-element.113.ut_ref), channel_id=1, source_target_pairs={{0,1},{1,0},{2,3},{3,2},{4,5},{5,4},{6,7},{7,6}} | collective-permute-start | bytes 9437192 | tf_op jit(solution)/shard_map/ppermute | solution.py:650
  322.7 13.6 %collective-permute-start.14 = (bf16[384,1024]{1,0:T(8,128)(2,1)S(1)}, bf16[384,1024]{1,0:T(8,128)(2,1)S(1)}, u32[]{:S(2)}, u32[]{:S(2)}) collective-permute-start(bf16[384,1024]{1,0:T(8,128)(2,1)S(1)} %sum_queries.1.mine_ref), channel_id=1, source_target_pairs={{0,1},{1,0},{2,3},{3,2},{4,5},{5,4},{6,7},{7,6}} | collective-permute-start | bytes 2359304 | tf_op jit(solution)/shard_map/ppermute | solution.py:650
  323.7 20.0 %copy-start.51 = (bf16[256,2048]{1,0:T(8,128)(2,1)}, bf16[256,2048]{1,0:T(8,128)(2,1)S(1)}, u32[]{:S(2)}) copy-start(bf16[256,2048]{1,0:T(8,128)(2,1)S(1)} %collective-permute-done.16.b1_ref) | copy-start | bytes 3145732
  323.7 13.7 %collective-permute-start.24 = (f32[256,768]{1,0:T(8,128)S(1)}, f32[256,768]{1,0:T(8,128)S(1)}, u32[]{:S(2)}, u32[]{:S(2)}) collective-permute-start(f32[256,768]{1,0:T(8,128)S(1)} %collective-permute-done.21.refs_6_), channel_id=1, source_target_pairs={{0,1},{1,0},{2,3},{3,2},{4,5},{5,4},{6,7},{7,6}} | collective-permute-start | bytes 2359304 | tf_op jit(solution)/shard_map/ppermute | solution.py:650
  336.3 7.4 %copy-start.21 = (bf16[384,1024]{1,0:T(8,128)(2,1)}, bf16[384,1024]{1,0:T(8,128)(2,1)S(1)}, u32[]{:S(2)}) copy-start(bf16[384,1024]{1,0:T(8,128)(2,1)S(1)} %collective-permute-done.14.near_ref) | copy-start | bytes 2359300
  336.3 2.3 collective-permute-start.26
  337.4 2.3 collective-permute-start.25
  338.6 32.1 %collective-permute-start.29 = (bf16[768,512]{1,0:T(8,128)(2,1)}, bf16[768,512]{1,0:T(8,128)(2,1)}, u32[]{:S(2)}, u32[]{:S(2)}) collective-permute-start(bf16[768,512]{1,0:T(8,128)(2,1)} %get-tuple-element.109.n2t_ref), channel_id=1, source_target_pairs={{0,1},{1,0},{2,3},{3,2},{4,5},{5,4},{6,7},{7,6}} | collective-permute-start | bytes 2359304 | tf_op jit(solution)/shard_map/ppermute | solution.py:650
  339.7 31.0 %collective-permute-start.30 = (bf16[512,768]{1,0:T(8,128)(2,1)}, bf16[512,768]{1,0:T(8,128)(2,1)}, u32[]{:S(2)}, u32[]{:S(2)}) collective-permute-start(bf16[512,768]{1,0:T(8,128)(2,1)} %get-tuple-element.110.gt_ref), channel_id=1, source_target_pairs={{0,1},{1,0},{2,3},{3,2},{4,5},{5,4},{6,7},{7,6}} | collective-permute-start | bytes 2359304 | tf_op jit(solution)/shard_map/ppermute | solution.py:650
  343.7 10.0 %copy-start.7 = (bf16[768,12,64]{0,2,1:T(8,128)(2,1)S(1)}, bf16[768,12,64]{0,2,1:T(8,128)(2,1)}, u32[]{:S(2)}) copy-start(bf16[768,12,64]{0,2,1:T(8,128)(2,1)} %param.18) | copy-start | bytes 3538948
  343.8 10.0 %copy-start.13 = (bf16[1024,768]{1,0:T(8,128)(2,1)S(1)}, bf16[1024,768]{1,0:T(8,128)(2,1)}, u32[]{:S(2)}) copy-start(bf16[1024,768]{1,0:T(8,128)(2,1)} %get-tuple-element.65.x_ref) | copy-start | bytes 4718596
  343.8 10.0 %copy-start.15 = (f32[1,768]{1,0:T(1,128)S(1)}, f32[1,768]{1,0:T(1,128)}, u32[]{:S(2)}) copy-start(f32[1,768]{1,0:T(1,128)} %reshape.82.gain_ref) | copy-start | bytes 9220
  343.8 10.0 %copy-start.16 = (s32[5]{0:T(128)S(1)}, s32[5]{0:T(128)}, u32[]{:S(2)}) copy-start(s32[5]{0:T(128)} %stack.32.place_ref) | copy-start | bytes 64
  370.7 21.4 %copy-start.1 = (bf16[12,64,768]{2,1,0:T(8,128)(2,1)S(1)}, bf16[12,64,768]{2,1,0:T(8,128)(2,1)}, u32[]{:S(2)}) copy-start(bf16[12,64,768]{2,1,0:T(8,128)(2,1)} %param.21) | copy-start | bytes 3538948
  (22 other events, 45.9 us)

commit v5 on v4

--- a/solution.py
+++ b/solution.py
@@ -99,33 +99,10 @@
                                     pl.BlockSpec((width, dim), lambda i, s: (s[n], 0))],
             out_specs=[put, put, pl.BlockSpec((rows, width), lambda i, s: (s[i], 0)),
                        pl.BlockSpec((width, rows), lambda i, s: (0, s[i]))]),
-        compiler_params=pltpu.CompilerParams(vmem_limit_bytes=60 << 20),
+        compiler_params=pltpu.CompilerParams(vmem_limit_bytes=24 << 20),
         cost_estimate=cost(2 * n * rows * dim * width, 6 << 20),
         name="queries",
     )(place, *parts, gain, wqt)
-
-
-def place_kernel(place_ref, x0_ref, x1_ref, o_ref):
-    for part, src in enumerate((x0_ref, x1_ref)):
-        @pl.when(pl.program_id(0) == part)
-        def _():
-            o_ref[...] = src[...]
-
-
-def place_rows(place, parts):
-    rows, dim = parts[0].shape
-    n = len(parts)
-    return pl.pallas_call(
-        place_kernel,
-        out_shape=jax.ShapeDtypeStruct((n * rows, dim), parts[0].dtype),
-        grid_spec=pltpu.PrefetchScalarGridSpec(
-            num_scalar_prefetch=1, grid=(n,),
-            in_specs=[pl.BlockSpec((rows, dim), lambda i, s: (0, 0))] * n,
-            out_specs=pl.BlockSpec((rows, dim), lambda i, s: (s[2 * i], 0))),
-        compiler_params=pltpu.CompilerParams(vmem_limit_bytes=62 << 20),
-        cost_estimate=cost(n * rows * dim, 6 << 20),
-        name="place_rows",
-    )(place, *parts)
 
 
 def fwd_kernel(len_ref, qt_ref, k_ref, vt_ref, o_ref, m_ref, l_ref, acc_ref, qz_ref, sa_ref, sb_ref):
@@ -215,7 +192,7 @@
         fwd_kernel,
         out_shape=jax.ShapeDtypeStruct((2 * pairs, OROWS, nq), F32),
         grid_spec=spec,
-        compiler_params=pltpu.CompilerParams(vmem_limit_bytes=24 << 20),
+        compiler_params=pltpu.CompilerParams(vmem_limit_bytes=67_000_000),
         cost_estimate=cost(work * 1024, 4 << 20, work),
         name="attn_fwd",
     )(lens, qt, k, vt)
@@ -324,7 +301,7 @@
         out_shape=[jax.ShapeDtypeStruct((2 * PAIR, rows // 2), BF)] * 2
                   + [jax.ShapeDtypeStruct((2, 64, nq), F32), jax.ShapeDtypeStruct((2 * PAIR, mem.shape[1]), F32)],
         grid_spec=spec,
-        compiler_params=pltpu.CompilerParams(vmem_limit_bytes=32 << 20),
+        compiler_params=pltpu.CompilerParams(vmem_limit_bytes=40 << 20),
         cost_estimate=cost(work * 2000, 8 << 20, work),
         name="attn_bwd",
     )(lens, qt, dot_t, lse, delta, k, v, kt, mem, mem_near)
@@ -352,7 +329,7 @@
         out_specs=[fix(2, 64, nq), fix(PAIR, nq), fix(2, 1, nq)],
         out_shape=[jax.ShapeDtypeStruct((2, 64, nq), F32), jax.ShapeDtypeStruct((PAIR, nq), BF),
                    jax.ShapeDtypeStruct((2, 1, nq), F32)],
-        compiler_params=pltpu.CompilerParams(vmem_limit_bytes=62 << 20),
+        compiler_params=pltpu.CompilerParams(vmem_limit_bytes=67_000_000),
         cost_estimate=cost(500 * nq, 2 << 20),
         name="combine",
     )(a, b)
@@ -380,11 +357,14 @@
     )(*mine, *far)
 
 
-def mlp_kernel(h_ref, g_ref, gain_ref, w1_ref, w3_ref, w2_ref,
+def mlp_kernel(place_ref, h_ref, g0_ref, g1_ref, gain_ref, w1_ref, w3_ref, w2_ref,
                n2t_ref, gt_ref, dgate_ref, dup_ref, ut_ref, dh_ref, dhb_ref, gn_ref, n2_ref, acc_ref):
     step = pl.program_id(0)
     rows = h_ref.shape[0]
-    chunk = 256
+    chunk = g0_ref.shape[0]
+
+    def grad_rows(c):
+        return jnp.where(place_ref[0] == c, g0_ref[...], g1_ref[...])
 
     @pl.when(step == 0)
     def _():
@@ -394,7 +374,7 @@
             n2 = (hid * inv_rms(hid) * gain_ref[...]).astype(BF)
             n2_ref[rs, :] = n2
             n2t_ref[:, rs] = n2.T
-            gt_ref[rs, :] = g_ref[rs, :].astype(BF)
+            gt_ref[rs, :] = grad_rows(c).astype(BF)
         acc_ref[...] = jnp.zeros(acc_ref.shape, F32)
 
     w1, w3, w2 = w1_ref[...], w3_ref[...], w2_ref[...]
@@ -423,34 +403,35 @@
             unit = hid * inv
             grad = acc_ref[rs, :]
             total += jnp.sum(grad * unit, axis=0, keepdims=True)
-            dh = g_ref[rs, :] + norm_back(unit, inv, gain_ref[...], grad)
+            dh = grad_rows(c) + norm_back(unit, inv, gain_ref[...], grad)
             dh_ref[rs, :] = dh
             dhb_ref[rs, :] = dh.astype(BF)
         gn_ref[...] = total
 
 
-def mlp(hidden, g_all, gain, w_gate, w_up, w_down):
+def mlp(place, hidden, g_parts, gain, w_gate, w_up, w_down):
     rows, dim = hidden.shape
     ff = w_gate.shape[1]
-    fix = lambda *shape: pl.BlockSpec(shape, lambda i: (0,) * len(shape))
-    wide = pl.BlockSpec((dim, FFB), lambda i: (0, i))
-    tall = pl.BlockSpec((FFB, dim), lambda i: (i, 0))
-    act = pl.BlockSpec((rows, FFB), lambda i: (0, i))
-    act_t = pl.BlockSpec((FFB, rows), lambda i: (i, 0))
+    fix = lambda *shape: pl.BlockSpec(shape, lambda i, s: (0,) * len(shape))
+    wide = pl.BlockSpec((dim, FFB), lambda i, s: (0, i))
+    tall = pl.BlockSpec((FFB, dim), lambda i, s: (i, 0))
+    act = pl.BlockSpec((rows, FFB), lambda i, s: (0, i))
+    act_t = pl.BlockSpec((FFB, rows), lambda i, s: (i, 0))
     return pl.pallas_call(
         mlp_kernel,
-        grid=(ff // FFB,),
-        in_specs=[fix(rows, dim), fix(rows, dim), fix(1, dim), wide, wide, tall],
-        out_specs=[fix(dim, rows), fix(rows, dim), act, act, act_t, fix(rows, dim), fix(rows, dim), fix(1, dim)],
+        grid_spec=pltpu.PrefetchScalarGridSpec(
+            num_scalar_prefetch=1, grid=(ff // FFB,),
+            in_specs=[fix(rows, dim), fix(rows // 2, dim), fix(rows // 2, dim), fix(1, dim), wide, wide, tall],
+            out_specs=[fix(dim, rows), fix(rows, dim), act, act, act_t, fix(rows, dim), fix(rows, dim), fix(1, dim)],
+            scratch_shapes=[pltpu.VMEM((rows, dim), BF), pltpu.VMEM((rows, dim), F32)]),
         out_shape=[jax.ShapeDtypeStruct((dim, rows), BF), jax.ShapeDtypeStruct((rows, dim), BF),
                    jax.ShapeDtypeStruct((rows, ff), BF), jax.ShapeDtypeStruct((rows, ff), BF),
                    jax.ShapeDtypeStruct((ff, rows), BF), jax.ShapeDtypeStruct((rows, dim), F32),
                    jax.ShapeDtypeStruct((rows, dim), BF), jax.ShapeDtypeStruct((1, dim), F32)],
-        scratch_shapes=[pltpu.VMEM((rows, dim), BF), pltpu.VMEM((rows, dim), F32)],
         compiler_params=pltpu.CompilerParams(vmem_limit_bytes=56 << 20),
         cost_estimate=cost(10 * rows * dim * ff, 40 << 20, rows * ff),
         name="mlp",
-    )(hidden, g_all, gain, w_gate, w_up, w_down)
+    )(place, hidden, *g_parts, gain, w_gate, w_up, w_down)
 
 
 def mlp_weights_kernel(n2t_ref, gt_ref, dgate_ref, dup_ref, ut_ref, n2t2_ref, gt2_ref, dgate2_ref, dup2_ref, ut2_ref,
@@ -502,7 +483,7 @@
             num_scalar_prefetch=1, grid=(rows // MB,),
             in_specs=[block] * 6 + [whole, whole],
             out_specs=pl.BlockSpec((MB, dim), lambda i, s: (i, 0))),
-        compiler_params=pltpu.CompilerParams(vmem_limit_bytes=60 << 20),
+        compiler_params=pltpu.CompilerParams(vmem_limit_bytes=32 << 20),
         cost_estimate=cost(4 * rows * dim * dim, 16 << 20),
         name="memory_grad",
     )(core, *mine, *near, wkt, wvt)
@@ -698,7 +679,6 @@
             lses.append(lse_piece)
         for pieces_of, axis in ((outs, 2), (outs_b, 1), (lses, 2)):
             pieces_of[-2:] = [jnp.concatenate(pieces_of[-2:], axis=axis)]
-        g_half = place_rows(place, g_parts)
         o_t = jnp.concatenate(outs, axis=0)
         lse = jnp.concatenate(lses, axis=0)
         o_t_b = jnp.concatenate(outs_b, axis=0)
@@ -713,7 +693,7 @@
         hidden = (x_all_b[:half].astype(F32) + mm(o_t_first, wo_m, 0, 0) + mm(o_near_first, wo_n, 0, 0)).astype(BF)
 
         n2t, g_top, d_gate, d_up, act_t, d_hid, d_hid_half, g_norm_half = mlp(
-            hidden, g_half, gain2, w_gate, w_up, w_down)
+            place, hidden, g_parts, gain2, w_gate, w_up, w_down)
         d_hid_b = jnp.concatenate([d_hid_half, to_near(d_hid_half)], axis=0)
         factors = (n2t, g_top, d_gate, d_up, act_t)
         factors_near = tuple(to_near(a) for a in factors)

time: 398 us -> 388 us (0.975)
  local copies, waits for them, and re-layouts: 20.2 us -> 12.7 us
  waiting for transfers between devices: 122 us -> 118 us
    pallas_call x4, Pallas kernels: 45.1 us -> 52.7 us  [attention_forward(): pl.pallas_call(fwd_kernel, out_shape=jax.ShapeDtypeStruct((2 * pairs, ORO...]
    unnamed x105 -> x103, local copies, waits for them, and re-layouts: 16.8 us -> 11.2 us
    ppermute x12, waiting for transfers between devices: 108 us -> 102 us  [to_far(): return lax.ppermute(a, 'seq', far)]
    pallas_call x2 -> x1, Pallas kernels: 25.1 us -> 22.7 us  [mlp(): pl.pallas_call(mlp_kernel, grid_spec=pltpu.PrefetchScalarGridSpec(num_sca...]
  transfers between devices with their start and end apart: 34 -> 34, of which waited for: 12 -> 12; matrix products, arithmetic and copies ran while one was open for 2% -> 3% of each run, Pallas kernels for 34% -> 33%
where the time goes in v5:
time: 388 us; the launch traced here: 382 us
  Pallas kernels  219 us (56%)
  waiting for transfers between devices  118 us (30%)
  starting transfers between devices  22 us (6%)
  local copies, waits for them, and re-layouts  12.7 us (3%)
  matrix products  5.04 us (1%)
    ppermute x12, waiting for transfers between devices, to_far(): return lax.ppermute(a, 'seq', far)  102 us
    pallas_call x3, Pallas kernels, attention_backward(): pl.pallas_call(bwd_kernel, out_shape=[jax.ShapeDtypeStruct((2 * PAIR, row...  72.3 us
    pallas_call x4, Pallas kernels, attention_forward(): pl.pallas_call(fwd_kernel, out_shape=jax.ShapeDtypeStruct((2 * pairs, ORO...  52.7 us
    pallas_call x1, Pallas kernels, mlp(): pl.pallas_call(mlp_kernel, grid_spec=pltpu.PrefetchScalarGridSpec(num_sca...  22.7 us
    pallas_call x1, Pallas kernels, mlp_weights(): pl.pallas_call(mlp_weights_kernel, grid=(ff // WFB,), in_specs=ins + ins,...  21.3 us
    ppermute x22, waiting for transfers between devices, to_near(): return lax.ppermute(a, 'seq', near)  16.5 us
    pallas_call x2, Pallas kernels, project(): pl.pallas_call(proj_kernel, out_shape=outs, grid_spec=pltpu.PrefetchScala...  14.7 us
    ppermute x22, starting transfers between devices, to_near(): return lax.ppermute(a, 'seq', near)  14.7 us
  transfers between devices with their start and end apart: 34, of which 12 were waited for; matrix products, arithmetic and copies ran while one was open for 3% of the time, Pallas kernels for 33%

profile of v5, /device:TPU:5, one launch (start us, length us, event | category | flops | bytes accessed | tf_op | source)
XLA Modules:
  0.0 382.4 jit_solution(17393411327175564550)
XLA Ops:
  0.6 0.7 collective-permute-start.3
  1.3 1.2 collective-permute-start.1
  2.9 9.3 %collective-permute-done.1.x2_ref = bf16[256,768]{1,0:T(8,128)(2,1)S(1)} collective-permute-done((bf16[256,768]{1,0:T(8,128)(2,1)}, bf16[256,768]{1,0:T(8,128)(2,1)S(1)}, u32[]{:S(2)}, u32[]{:S(2)}) %collective-permute-start.1) | collective-permute-done | bytes 393248 | tf_op jit(solution)/shard_map/ppermute | solution.py:634
  12.2 0.9 collective-permute-start.2
  13.7 0.7 reshape.82.gain_ref
  14.5 0.6 pad_add_fusion.len_ref
  15.1 7.3 %kv_proj.2 = (bf16[4096,384]{1,0:T(8,128)(2,1)}, bf16[4096,384]{1,0:T(8,128)(2,1)}, bf16[384,4096]{1,0:T(8,128)(2,1)}, bf16[384,4096]{1,0:T(8,128)(2,1)}) custom-call(s32[1]{0:T(128)} %bitcast.4.core_ref, bf16[2048,768]{1,0:T(8,128)(2,1)} %m0_ref.5, bf16[768,768]{1,0:T(8,128)(2,1)} %bitcast.35, bf16[768,768]{1,0:T(8,128)(2,1)} %bitcast.38), custom_call_target="tpu_custom_call" | custom-call | flops 2415919104 | bytes 12582912 | tf_op jit(solution)/shard_map/kv_proj/pallas_call | solution.py:57
  22.4 3.7 queries.1
  26.1 1.1 copy-done.10
  27.2 1.1 copy-done.16
  28.3 7.5 %kv_proj.3 = (bf16[4096,384]{1,0:T(8,128)(2,1)}, bf16[4096,384]{1,0:T(8,128)(2,1)}, bf16[384,4096]{1,0:T(8,128)(2,1)}, bf16[384,4096]{1,0:T(8,128)(2,1)}) custom-call(s32[1]{0:T(128)} %bitcast.4.core_ref, bf16[2048,768]{1,0:T(8,128)(2,1)} %collective-permute-done.3.m_ref.m1_ref, ...), custom_call_target="tpu_custom_call", output_to_operand_aliasing={{0}: (4, {}), {1}: (5, {}), {2}: (6, {}), {3}: (7, {})} | custom-call | flops 2415919104 | bytes 12582912 | tf_op jit(solution)/shard_map/kv_proj/pallas_call | solution.py:57
  35.8 9.8 %attn_fwd.6.a_ref = f32[2,72,512]{2,1,0:T(8,128)} custom-call(s32[2]{0:T(128)} %pad_add_fusion.len_ref, bf16[384,1024]{1,0:T(8,128)(2,1)} %copy-done.18, bf16[4096,384]{1,0:T(8,128)(2,1)} %get-tuple-element.70.k_ref, bf16[384,4096]{1,0:T(8,128)(2,1)} %get-tuple-element.71.vt_ref), custom_call_target="tpu_custom_call" | custom-call | flops 4294967296 | bytes 4194304 | tf_op jit(solution)/shard_map/attn_fwd/pallas_call | solution.py:191
  45.7 16.5 %attn_fwd.5.a_ref = f32[2,72,1024]{2,1,0:T(8,128)} custom-call(s32[2]{0:T(128)} %pad_add_fusion.len_ref, bf16[384,1024]{1,0:T(8,128)(2,1)} %copy-done.18, bf16[4096,384]{1,0:T(8,128)(2,1)} %get-tuple-element.70.k_ref, bf16[384,4096]{1,0:T(8,128)(2,1)} %get-tuple-element.71.vt_ref), custom_call_target="tpu_custom_call" | custom-call | flops 8589934592 | bytes 4194304 | tf_op jit(solution)/shard_map/attn_fwd/pallas_call | solution.py:191
  62.1 16.5 %attn_fwd.4.a_ref = f32[2,72,1024]{2,1,0:T(8,128)} custom-call(s32[2]{0:T(128)} %pad_add_fusion.len_ref, bf16[384,1024]{1,0:T(8,128)(2,1)} %copy-done.18, bf16[4096,384]{1,0:T(8,128)(2,1)} %get-tuple-element.70.k_ref, bf16[384,4096]{1,0:T(8,128)(2,1)} %get-tuple-element.71.vt_ref), custom_call_target="tpu_custom_call" | custom-call | flops 8589934592 | bytes 4194304 | tf_op jit(solution)/shard_map/attn_fwd/pallas_call | solution.py:191
  78.6 1.5 collective-permute-start.4
  80.1 9.9 %attn_fwd.7.a_ref = f32[2,72,512]{2,1,0:T(8,128)} custom-call(s32[2]{0:T(128)} %pad_add_fusion.len_ref, bf16[384,1024]{1,0:T(8,128)(2,1)} %copy-done.18, bf16[4096,384]{1,0:T(8,128)(2,1)} %get-tuple-element.70.k_ref, bf16[384,4096]{1,0:T(8,128)(2,1)} %get-tuple-element.71.vt_ref), custom_call_target="tpu_custom_call" | custom-call | flops 4294967296 | bytes 4194304 | tf_op jit(solution)/shard_map/attn_fwd/pallas_call | solution.py:191
  90.0 1.5 collective-permute-start.9
  91.5 1.9 combine.6
  93.3 25.7 %collective-permute-done.7.b_ref = f32[2,72,512]{2,1,0:T(8,128)} collective-permute-done((f32[2,72,512]{2,1,0:T(8,128)}, f32[2,72,512]{2,1,0:T(8,128)}, u32[]{:S(2)}, u32[]{:S(2)}) %collective-permute-start.7) | collective-permute-done | bytes 294944 | tf_op jit(solution)/shard_map/ppermute | solution.py:634
  119.1 1.9 combine.7
  121.0 2.2 combine.4
  123.2 2.2 combine.5
  125.4 1.2 maximum_maximum_fusion.mine_ref
  126.7 1.4 collective-permute-start.8
  128.2 0.6 reshape.84.gain_ref
  128.8 1.7 fusion.7
  130.5 2.6 add_convert_fusion.h_ref
  133.0 2.9 collective-permute-done.9.g1_ref
  135.9 22.7 %mlp.1 = (bf16[768,512]{1,0:T(8,128)(2,1)}, bf16[512,768]{1,0:T(8,128)(2,1)}, bf16[512,3072]{1,0:T(8,128)(2,1)}, bf16[512,3072]{1,0:T(8,128)(2,1)}, bf16[3072,51...) custom-call(s32[5]{0:T(128)} %copy-done.14, ...), custom_call_target="tpu_custom_call" | custom-call | flops 12079595520 | bytes 41943040 | tf_op jit(solution)/shard_map/mlp/pallas_call | solution.py:420
  158.7 0.9 collective-permute-start.10
  159.6 1.3 constant_dynamic-update-slice_fusion.1
  161.0 0.7 collective-permute-done.10
  161.8 0.8 fusion.14
  163.2 0.6 copy-done.1
  163.9 1.2 copy-done
  165.2 24.3 %attn_bwd.3 = (bf16[256,2048]{1,0:T(8,128)(2,1)S(1)}, bf16[256,2048]{1,0:T(8,128)(2,1)S(1)}, f32[2,64,1024]{2,1,0:T(8,128)S(1)}, f32[256,768]{1,0:T(8,128)S(1)}) custom-call(s32[2]{0:T(128)S(1)} %copy-done.20, bf16[384,1024]{1,0:T(8,128)(2,1)S(1)} %copy-done.19, bf16[384,1024]{1,0:T(8,128)(2,1)S(1)} %get-tuple-element.119.dot_ref, ...), custom_call_target="tpu_custom_call" | custom-call | flops 16777216000 | bytes 8388608 | tf_op jit(solution)/shard_map/attn_bwd/pallas_call | solution.py:299
  189.5 1.0 copy-done.22
  190.4 24.0 %attn_bwd.4 = (bf16[256,2048]{1,0:T(8,128)(2,1)S(1)}, bf16[256,2048]{1,0:T(8,128)(2,1)S(1)}, f32[2,64,1024]{2,1,0:T(8,128)S(1)}, f32[256,768]{1,0:T(8,128)S(1)}) custom-call(s32[2]{0:T(128)S(1)} %copy-done.20, bf16[384,1024]{1,0:T(8,128)(2,1)S(1)} %copy-done.19, bf16[384,1024]{1,0:T(8,128)(2,1)S(1)} %get-tuple-element.119.dot_ref, ...), custom_call_target="tpu_custom_call" | custom-call | flops 16777216000 | bytes 8388608 | tf_op jit(solution)/shard_map/attn_bwd/pallas_call | solution.py:299
  214.5 1.0 copy-done.24
  215.4 24.0 %attn_bwd.5 = (bf16[256,2048]{1,0:T(8,128)(2,1)S(1)}, bf16[256,2048]{1,0:T(8,128)(2,1)S(1)}, f32[2,64,1024]{2,1,0:T(8,128)S(1)}, f32[256,768]{1,0:T(8,128)S(1)}) custom-call(s32[2]{0:T(128)S(1)} %copy-done.20, bf16[384,1024]{1,0:T(8,128)(2,1)S(1)} %copy-done.19, bf16[384,1024]{1,0:T(8,128)(2,1)S(1)} %get-tuple-element.119.dot_ref, ...), custom_call_target="tpu_custom_call" | custom-call | flops 16777216000 | bytes 8388608 | tf_op jit(solution)/shard_map/attn_bwd/pallas_call | solution.py:299
  239.5 1.0 copy-done.26
  240.8 1.7 collective-permute-start.21
  243.4 0.9 collective-permute-start.23
  244.3 9.3 %collective-permute-done.13.b2_ref = f32[2,64,1024]{2,1,0:T(8,128)S(1)} collective-permute-done((f32[2,64,1024]{2,1,0:T(8,128)S(1)}, f32[2,64,1024]{2,1,0:T(8,128)S(1)}, u32[]{:S(2)}, u32[]{:S(2)}) %collective-permute-start.13) | collective-permute-done | bytes 524320 | tf_op jit(solution)/shard_map/ppermute | solution.py:634
  253.6 2.0 collective-permute-start.20
  255.6 26.1 %collective-permute-done.12.b1_ref = f32[2,64,1024]{2,1,0:T(8,128)S(1)} collective-permute-done((f32[2,64,1024]{2,1,0:T(8,128)S(1)}, f32[2,64,1024]{2,1,0:T(8,128)S(1)}, u32[]{:S(2)}, u32[]{:S(2)}) %collective-permute-start.12) | collective-permute-done | bytes 524320 | tf_op jit(solution)/shard_map/ppermute | solution.py:634
  281.7 2.0 collective-permute-start.15
  283.8 14.8 %collective-permute-done.23.refs_8_ = f32[256,768]{1,0:T(8,128)S(1)} collective-permute-done((f32[256,768]{1,0:T(8,128)S(1)}, f32[256,768]{1,0:T(8,128)S(1)}, u32[]{:S(2)}, u32[]{:S(2)}) %collective-permute-start.23) | collective-permute-done | bytes 786464 | tf_op jit(solution)/shard_map/ppermute | solution.py:634
  298.6 2.0 collective-permute-start.17
  300.6 0.9 copy-done.32
  301.5 13.9 %collective-permute-done.22.refs_7_ = f32[256,768]{1,0:T(8,128)S(1)} collective-permute-done((f32[256,768]{1,0:T(8,128)S(1)}, f32[256,768]{1,0:T(8,128)S(1)}, u32[]{:S(2)}, u32[]{:S(2)}) %collective-permute-start.22) | collective-permute-done | bytes 786464 | tf_op jit(solution)/shard_map/ppermute | solution.py:634
  315.4 1.2 collective-permute-start.31
  318.2 14.0 %collective-permute-done.14.near_ref = bf16[384,1024]{1,0:T(8,128)(2,1)S(1)} collective-permute-done((bf16[384,1024]{1,0:T(8,128)(2,1)S(1)}, bf16[384,1024]{1,0:T(8,128)(2,1)S(1)}, u32[]{:S(2)}, u32[]{:S(2)}) %collective-permute-start.14) | collective-permute-done | bytes 786464 | tf_op jit(solution)/shard_map/ppermute | solution.py:631
  332.6 0.7 collective-permute-done.24.refs_9_
  333.7 0.6 add_reduce_fusion
  334.9 0.7 collective-permute-done.25.refs_10_
  336.1 2.6 out_proj_grad.1
  338.7 0.6 copy-done.27
  339.4 7.5 %memory_grad.1 = f32[2048,768]{1,0:T(8,128)} custom-call(s32[1]{0:T(128)} %bitcast.4.core_ref, bf16[256,2048]{1,0:T(8,128)(2,1)S(1)} %copy-done.23, bf16[256,2048]{1,0:T(8,128)(2,1)S(1)} %copy-done.25, bf16[256,2048]{1,0:T(8,128)(2,1)S(1)} %copy-done.27, bf16[256,2048]{1,0:T(8,128)(2,1)S(1)} %collective-permute-done.15.b0_ref, ...), custom_call_target="tpu_custom_call" | custom-call | flops 4831838208 | bytes 16777216 | tf_op jit(solution)/shard_map/memory_grad/pallas_call | solution.py:479
  346.9 5.6 %query_grad.1 = (f32[768,768]{1,0:T(8,128)}, f32[256,768]{1,0:T(8,128)}, f32[1,768]{1,0:T(1,128)S(1)}) custom-call(s32[5]{0:T(128)S(1)} %copy-done.15, bf16[384,1024]{1,0:T(8,128)(2,1)S(1)} %sum_queries.1.mine_ref, bf16[384,1024]{1,0:T(8,128)(2,1)S(1)} %collective-permute-done.14.near_ref, bf16[1024,768]{1,0:T(8,128)(2,1)S(1)} %copy-done.17, ...), custom_call_target="tpu_custom_call" | custom-call | flops 2415919104 | bytes 10485760 | tf_op jit(solution)/shard_map/query_grad/pallas_call | solution.py:562
  352.5 0.6 reduce
  353.1 6.9 %key_weights.1 = (f32[768,768]{1,0:T(8,128)}, f32[768,768]{1,0:T(8,128)}) custom-call(s32[1]{0:T(128)} %bitcast.4.core_ref, f32[256,768]{1,0:T(8,128)} %copy-done.7, f32[256,768]{1,0:T(8,128)} %copy-done.8, f32[256,768]{1,0:T(8,128)} %copy-done.9, f32[256,768]{1,0:T(8,128)} %copy-done.30, f32[256,768]{1,0:T(8,128)} %copy-done.34, f32[256,768]{1,0:T(8,128)} %copy-done.32, ...), custom_call_target="tpu_custom_call" | custom-call | flops 1179648 | bytes 10485760 | tf_op jit(solution)/shard_map/key_weights/pallas_call | solution.py:593
  360.0 0.8 copy-done.50
  360.9 21.3 %mlp_weights.1 = (f32[768,3072]{1,0:T(8,128)}, f32[768,3072]{1,0:T(8,128)}, f32[3072,768]{1,0:T(8,128)}) custom-call(bf16[768,512]{1,0:T(8,128)(2,1)} %get-tuple-element.109.n2t_ref, bf16[512,768]{1,0:T(8,128)(2,1)} %get-tuple-element.110.gt_ref, bf16[512,3072]{1,0:T(8,128)(2,1)} %get-tuple-element.111.dgate_ref, ...), custom_call_target="tpu_custom_call" | custom-call | flops 14495514624 | bytes 52428800 | tf_op jit(solution)/shard_map/mlp_weights/pallas_call | solution.py:451
  (143 shorter events, 6.0 us)
Async XLA Ops:
  0.6 27.7 %collective-permute-start.3 = (bf16[2048,768]{1,0:T(8,128)(2,1)}, bf16[2048,768]{1,0:T(8,128)(2,1)}, u32[]{:S(2)}, u32[]{:S(2)}) collective-permute-start(bf16[2048,768]{1,0:T(8,128)(2,1)} %m0_ref.5), channel_id=1, source_target_pairs={{0,1},{1,0},{2,3},{3,2},{4,5},{5,4},{6,7},{7,6}} | collective-permute-start | bytes 9437192 | tf_op jit(solution)/shard_map/ppermute | solution.py:631
  1.3 10.8 %collective-permute-start.1 = (bf16[256,768]{1,0:T(8,128)(2,1)}, bf16[256,768]{1,0:T(8,128)(2,1)S(1)}, u32[]{:S(2)}, u32[]{:S(2)}) collective-permute-start(bf16[256,768]{1,0:T(8,128)(2,1)} %x0_ref.1), channel_id=1, source_target_pairs={{0,2},{1,3},{2,0},{3,1},{4,6},{5,7},{6,4},{7,5}} | collective-permute-start | bytes 1179656 | tf_op jit(solution)/shard_map/ppermute | solution.py:634
  2.6 19.8 %collective-permute-start = (bf16[256,768]{1,0:T(8,128)(2,1)}, bf16[256,768]{1,0:T(8,128)(2,1)S(1)}, u32[]{:S(2)}, u32[]{:S(2)}) collective-permute-start(bf16[256,768]{1,0:T(8,128)(2,1)} %x0_ref.1), channel_id=1, source_target_pairs={{0,1},{1,0},{2,3},{3,2},{4,5},{5,4},{6,7},{7,6}} | collective-permute-start | bytes 1179656 | tf_op jit(solution)/shard_map/ppermute | solution.py:631
  12.2 10.2 %collective-permute-start.2 = (bf16[256,768]{1,0:T(8,128)(2,1)S(1)}, bf16[256,768]{1,0:T(8,128)(2,1)S(1)}, u32[]{:S(2)}, u32[]{:S(2)}) collective-permute-start(bf16[256,768]{1,0:T(8,128)(2,1)S(1)} %collective-permute-done.1.x2_ref), channel_id=1, source_target_pairs={{0,1},{1,0},{2,3},{3,2},{4,5},{5,4},{6,7},{7,6}} | collective-permute-start | bytes 1179656 | tf_op jit(solution)/shard_map/ppermute | solution.py:631
  14.5 7.9 %copy-start.14 = (s32[5]{0:T(128)}, s32[5]{0:T(128)S(1)}, u32[]{:S(2)}) copy-start(s32[5]{0:T(128)S(1)} %stack.32.place_ref) | copy-start | bytes 64
  15.1 7.3 %copy-start.3 = (bf16[768,12,64]{0,2,1:T(8,128)(2,1)S(1)}, bf16[768,12,64]{0,2,1:T(8,128)(2,1)}, u32[]{:S(2)}) copy-start(bf16[768,12,64]{0,2,1:T(8,128)(2,1)} %param.18) | copy-start | bytes 3538948
  15.1 7.3 %copy-start.13 = (bf16[256,768]{1,0:T(8,128)(2,1)S(1)}, bf16[256,768]{1,0:T(8,128)(2,1)}, u32[]{:S(2)}) copy-start(bf16[256,768]{1,0:T(8,128)(2,1)} %x0_ref.1) | copy-start | bytes 1179652
  28.3 7.5 %copy-start.18 = (bf16[384,1024]{1,0:T(8,128)(2,1)}, bf16[384,1024]{1,0:T(8,128)(2,1)S(1)}, u32[]{:S(2)}) copy-start(bf16[384,1024]{1,0:T(8,128)(2,1)S(1)} %get-tuple-element.64.qt_ref) | copy-start | bytes 2359300
  78.6 12.8 %collective-permute-start.6 = (f32[2,72,512]{2,1,0:T(8,128)}, f32[2,72,512]{2,1,0:T(8,128)}, u32[]{:S(2)}, u32[]{:S(2)}) collective-permute-start(f32[2,72,512]{2,1,0:T(8,128)} %attn_fwd.6.a_ref), channel_id=1, source_target_pairs={{0,2},{1,3},{2,0},{3,1},{4,6},{5,7},{6,4},{7,5}} | collective-permute-start | bytes 884744 | tf_op jit(solution)/shard_map/ppermute | solution.py:634
  78.6 42.3 %collective-permute-start.4 = (f32[2,72,1024]{2,1,0:T(8,128)}, f32[2,72,1024]{2,1,0:T(8,128)}, u32[]{:S(2)}, u32[]{:S(2)}) collective-permute-start(f32[2,72,1024]{2,1,0:T(8,128)} %attn_fwd.4.a_ref), channel_id=1, source_target_pairs={{0,2},{1,3},{2,0},{3,1},{4,6},{5,7},{6,4},{7,5}} | collective-permute-start | bytes 1769480 | tf_op jit(solution)/shard_map/ppermute | solution.py:634
  80.1 43.1 %collective-permute-start.5 = (f32[2,72,1024]{2,1,0:T(8,128)}, f32[2,72,1024]{2,1,0:T(8,128)}, u32[]{:S(2)}, u32[]{:S(2)}) collective-permute-start(f32[2,72,1024]{2,1,0:T(8,128)} %attn_fwd.5.a_ref), channel_id=1, source_target_pairs={{0,2},{1,3},{2,0},{3,1},{4,6},{5,7},{6,4},{7,5}} | collective-permute-start | bytes 1769480 | tf_op jit(solution)/shard_map/ppermute | solution.py:634
  90.0 29.1 %collective-permute-start.7 = (f32[2,72,512]{2,1,0:T(8,128)}, f32[2,72,512]{2,1,0:T(8,128)}, u32[]{:S(2)}, u32[]{:S(2)}) collective-permute-start(f32[2,72,512]{2,1,0:T(8,128)} %attn_fwd.7.a_ref), channel_id=1, source_target_pairs={{0,2},{1,3},{2,0},{3,1},{4,6},{5,7},{6,4},{7,5}} | collective-permute-start | bytes 884744 | tf_op jit(solution)/shard_map/ppermute | solution.py:634
  90.0 45.9 %collective-permute-start.9 = (f32[256,768]{1,0:T(8,128)}, f32[256,768]{1,0:T(8,128)}, u32[]{:S(2)}, u32[]{:S(2)}) collective-permute-start(f32[256,768]{1,0:T(8,128)} %g0_ref.1), channel_id=1, source_target_pairs={{0,2},{1,3},{2,0},{3,1},{4,6},{5,7},{6,4},{7,5}} | collective-permute-start | bytes 2359304 | tf_op jit(solution)/shard_map/ppermute | solution.py:634
  126.7 3.7 copy-start.11
  126.7 3.7 collective-permute-start.8
  133.0 26.6 %copy-start.42 = (f32[2,1,1024]{2,1,0:T(1,128)S(1)}, f32[2,1,1024]{2,1,0:T(1,128)}, u32[]{:S(2)}) copy-start(f32[2,1,1024]{2,1,0:T(1,128)} %get-tuple-element.77) | copy-start | bytes 24580
  133.0 26.6 %copy-start.43 = (f32[2,1,1024]{2,1,0:T(1,128)S(1)}, f32[2,1,1024]{2,1,0:T(1,128)}, u32[]{:S(2)}) copy-start(f32[2,1,1024]{2,1,0:T(1,128)} %get-tuple-element.78) | copy-start | bytes 24580
  133.0 26.6 %copy-start.44 = (f32[2,1,512]{2,1,0:T(1,128)S(1)}, f32[2,1,512]{2,1,0:T(1,128)}, u32[]{:S(2)}) copy-start(f32[2,1,512]{2,1,0:T(1,128)} %get-tuple-element.79) | copy-start | bytes 12292
  133.0 26.6 %copy-start.45 = (f32[2,1,512]{2,1,0:T(1,128)S(1)}, f32[2,1,512]{2,1,0:T(1,128)}, u32[]{:S(2)}) copy-start(f32[2,1,512]{2,1,0:T(1,128)} %get-tuple-element.80) | copy-start | bytes 12292
  135.9 25.8 %copy-start.28 = (bf16[12,64,768]{2,1,0:T(8,128)(2,1)S(1)}, bf16[12,64,768]{2,1,0:T(8,128)(2,1)}, u32[]{:S(2)}) copy-start(bf16[12,64,768]{2,1,0:T(8,128)(2,1)} %param.21) | copy-start | bytes 3538948
  135.9 26.7 %copy-start.39 = (f32[2,64,1024]{2,1,0:T(8,128)S(1)}, f32[2,64,1024]{2,1,0:T(8,128)}, u32[]{:S(2)}) copy-start(f32[2,64,1024]{2,1,0:T(8,128)} %get-tuple-element.82) | copy-start | bytes 1572868
  135.9 26.7 %copy-start.40 = (f32[2,64,512]{2,1,0:T(8,128)S(1)}, f32[2,64,512]{2,1,0:T(8,128)}, u32[]{:S(2)}) copy-start(f32[2,64,512]{2,1,0:T(8,128)} %get-tuple-element.83) | copy-start | bytes 786436
  135.9 26.7 %copy-start.41 = (f32[2,64,512]{2,1,0:T(8,128)S(1)}, f32[2,64,512]{2,1,0:T(8,128)}, u32[]{:S(2)}) copy-start(f32[2,64,512]{2,1,0:T(8,128)} %get-tuple-element.84) | copy-start | bytes 786436
  158.7 3.0 collective-permute-start.10
  159.5 83.0 %collective-permute-start.27 = (bf16[384,512]{1,0:T(8,128)(2,1)S(1)}, bf16[384,512]{1,0:T(8,128)(2,1)S(1)}, u32[]{:S(2)}, u32[]{:S(2)}) collective-permute-start(bf16[384,512]{1,0:T(8,128)(2,1)S(1)} %get-tuple-element.117), channel_id=1, source_target_pairs={{0,1},{1,0},{2,3},{3,2},{4,5},{5,4},{6,7},{7,6}} | collective-permute-start | bytes 1179656 | tf_op jit(solution)/shard_map/ppermute | solution.py:631
  190.4 52.1 %copy-start.7 = (f32[256,768]{1,0:T(8,128)}, f32[256,768]{1,0:T(8,128)S(1)}, u32[]{:S(2)}) copy-start(f32[256,768]{1,0:T(8,128)S(1)} %get-tuple-element.88.refs_0_) | copy-start | bytes 2359300
  190.4 52.9 %collective-permute-start.11 = (f32[2,64,1024]{2,1,0:T(8,128)S(1)}, f32[2,64,1024]{2,1,0:T(8,128)S(1)}, u32[]{:S(2)}, u32[]{:S(2)}) collective-permute-start(f32[2,64,1024]{2,1,0:T(8,128)S(1)} %get-tuple-element.87.a0_ref), channel_id=1, source_target_pairs={{0,2},{1,3},{2,0},{3,1},{4,6},{5,7},{6,4},{7,5}} | collective-permute-start | bytes 1572872 | tf_op jit(solution)/shard_map/ppermute | solution.py:634
  215.4 68.3 %copy-start.8 = (f32[256,768]{1,0:T(8,128)}, f32[256,768]{1,0:T(8,128)S(1)}, u32[]{:S(2)}) copy-start(f32[256,768]{1,0:T(8,128)S(1)} %get-tuple-element.91.refs_1_) | copy-start | bytes 2359300
  215.4 25.0 %copy-start.46 = (f32[1,768]{1,0:T(1,128)S(1)}, f32[1,768]{1,0:T(1,128)}, u32[]{:S(2)}) copy-start(f32[1,768]{1,0:T(1,128)} %get-tuple-element.108) | copy-start | bytes 9220
  240.5 77.1 %copy-start.9 = (f32[256,768]{1,0:T(8,128)}, f32[256,768]{1,0:T(8,128)S(1)}, u32[]{:S(2)}) copy-start(f32[256,768]{1,0:T(8,128)S(1)} %get-tuple-element.105.refs_2_) | copy-start | bytes 2359300
  240.5 13.1 %collective-permute-start.13 = (f32[2,64,1024]{2,1,0:T(8,128)S(1)}, f32[2,64,1024]{2,1,0:T(8,128)S(1)}, u32[]{:S(2)}, u32[]{:S(2)}) collective-permute-start(f32[2,64,1024]{2,1,0:T(8,128)S(1)} %get-tuple-element.93.a2_ref), channel_id=1, source_target_pairs={{0,2},{1,3},{2,0},{3,1},{4,6},{5,7},{6,4},{7,5}} | collective-permute-start | bytes 1572872 | tf_op jit(solution)/shard_map/ppermute | solution.py:634
  240.5 2.4 collective-permute-start.28
  240.8 42.9 %collective-permute-start.21 = (f32[256,768]{1,0:T(8,128)S(1)}, f32[256,768]{1,0:T(8,128)S(1)}, u32[]{:S(2)}, u32[]{:S(2)}) collective-permute-start(f32[256,768]{1,0:T(8,128)S(1)} %get-tuple-element.88.refs_0_), channel_id=1, source_target_pairs={{0,2},{1,3},{2,0},{3,1},{4,6},{5,7},{6,4},{7,5}} | collective-permute-start | bytes 2359304 | tf_op jit(solution)/shard_map/ppermute | solution.py:634
  242.6 41.1 %collective-permute-start.18 = (f32[256,768]{1,0:T(8,128)S(1)}, f32[256,768]{1,0:T(8,128)S(1)}, u32[]{:S(2)}, u32[]{:S(2)}) collective-permute-start(f32[256,768]{1,0:T(8,128)S(1)} %get-tuple-element.88.refs_0_), channel_id=1, source_target_pairs={{0,1},{1,0},{2,3},{3,2},{4,5},{5,4},{6,7},{7,6}} | collective-permute-start | bytes 2359304 | tf_op jit(solution)/shard_map/ppermute | solution.py:631
  242.8 38.9 %collective-permute-start.12 = (f32[2,64,1024]{2,1,0:T(8,128)S(1)}, f32[2,64,1024]{2,1,0:T(8,128)S(1)}, u32[]{:S(2)}, u32[]{:S(2)}) collective-permute-start(f32[2,64,1024]{2,1,0:T(8,128)S(1)} %get-tuple-element.90.a1_ref), channel_id=1, source_target_pairs={{0,2},{1,3},{2,0},{3,1},{4,6},{5,7},{6,4},{7,5}} | collective-permute-start | bytes 1572872 | tf_op jit(solution)/shard_map/ppermute | solution.py:634
  243.4 55.2 %collective-permute-start.23 = (f32[256,768]{1,0:T(8,128)S(1)}, f32[256,768]{1,0:T(8,128)S(1)}, u32[]{:S(2)}, u32[]{:S(2)}) collective-permute-start(f32[256,768]{1,0:T(8,128)S(1)} %get-tuple-element.105.refs_2_), channel_id=1, source_target_pairs={{0,2},{1,3},{2,0},{3,1},{4,6},{5,7},{6,4},{7,5}} | collective-permute-start | bytes 2359304 | tf_op jit(solution)/shard_map/ppermute | solution.py:634
  253.6 46.9 %collective-permute-start.20 = (f32[256,768]{1,0:T(8,128)S(1)}, f32[256,768]{1,0:T(8,128)S(1)}, u32[]{:S(2)}, u32[]{:S(2)}) collective-permute-start(f32[256,768]{1,0:T(8,128)S(1)} %get-tuple-element.105.refs_2_), channel_id=1, source_target_pairs={{0,1},{1,0},{2,3},{3,2},{4,5},{5,4},{6,7},{7,6}} | collective-permute-start | bytes 2359304 | tf_op jit(solution)/shard_map/ppermute | solution.py:631
  281.7 34.9 %collective-permute-start.15 = (bf16[256,2048]{1,0:T(8,128)(2,1)S(1)}, bf16[256,2048]{1,0:T(8,128)(2,1)S(1)}, u32[]{:S(2)}, u32[]{:S(2)}) collective-permute-start(bf16[256,2048]{1,0:T(8,128)(2,1)S(1)} %get-tuple-element.100), channel_id=1, source_target_pairs={{0,1},{1,0},{2,3},{3,2},{4,5},{5,4},{6,7},{7,6}} | collective-permute-start | bytes 3145736 | tf_op jit(solution)/shard_map/ppermute | solution.py:631
  283.7 34.0 %copy-start.29 = (f32[256,768]{1,0:T(8,128)}, f32[256,768]{1,0:T(8,128)S(1)}, u32[]{:S(2)}) copy-start(f32[256,768]{1,0:T(8,128)S(1)} %collective-permute-done.21.refs_6_) | copy-start | bytes 2359300
  283.7 31.7 %collective-permute-start.22 = (f32[256,768]{1,0:T(8,128)S(1)}, f32[256,768]{1,0:T(8,128)S(1)}, u32[]{:S(2)}, u32[]{:S(2)}) collective-permute-start(f32[256,768]{1,0:T(8,128)S(1)} %get-tuple-element.91.refs_1_), channel_id=1, source_target_pairs={{0,2},{1,3},{2,0},{3,1},{4,6},{5,7},{6,4},{7,5}} | collective-permute-start | bytes 2359304 | tf_op jit(solution)/shard_map/ppermute | solution.py:634
  283.7 33.9 %copy-start.30 = (f32[256,768]{1,0:T(8,128)}, f32[256,768]{1,0:T(8,128)S(1)}, u32[]{:S(2)}) copy-start(f32[256,768]{1,0:T(8,128)S(1)} %collective-permute-done.18.refs_3_) | copy-start | bytes 2359300
  283.7 32.9 %collective-permute-start.19 = (f32[256,768]{1,0:T(8,128)S(1)}, f32[256,768]{1,0:T(8,128)S(1)}, u32[]{:S(2)}, u32[]{:S(2)}) collective-permute-start(f32[256,768]{1,0:T(8,128)S(1)} %get-tuple-element.91.refs_1_), channel_id=1, source_target_pairs={{0,1},{1,0},{2,3},{3,2},{4,5},{5,4},{6,7},{7,6}} | collective-permute-start | bytes 2359304 | tf_op jit(solution)/shard_map/ppermute | solution.py:631
  298.6 33.7 %copy-start.31 = (f32[256,768]{1,0:T(8,128)}, f32[256,768]{1,0:T(8,128)S(1)}, u32[]{:S(2)}) copy-start(f32[256,768]{1,0:T(8,128)S(1)} %collective-permute-done.23.refs_8_) | copy-start | bytes 2359300
  298.6 19.1 %collective-permute-start.17 = (bf16[256,2048]{1,0:T(8,128)(2,1)S(1)}, bf16[256,2048]{1,0:T(8,128)(2,1)S(1)}, u32[]{:S(2)}, u32[]{:S(2)}) collective-permute-start(bf16[256,2048]{1,0:T(8,128)(2,1)S(1)} %get-tuple-element.102), channel_id=1, source_target_pairs={{0,1},{1,0},{2,3},{3,2},{4,5},{5,4},{6,7},{7,6}} | collective-permute-start | bytes 3145736 | tf_op jit(solution)/shard_map/ppermute | solution.py:631
  301.5 16.2 %collective-permute-start.16 = (bf16[256,2048]{1,0:T(8,128)(2,1)S(1)}, bf16[256,2048]{1,0:T(8,128)(2,1)S(1)}, u32[]{:S(2)}, u32[]{:S(2)}) collective-permute-start(bf16[256,2048]{1,0:T(8,128)(2,1)S(1)} %get-tuple-element.101), channel_id=1, source_target_pairs={{0,1},{1,0},{2,3},{3,2},{4,5},{5,4},{6,7},{7,6}} | collective-permute-start | bytes 3145736 | tf_op jit(solution)/shard_map/ppermute | solution.py:631
  315.4 17.9 %copy-start.33 = (f32[256,768]{1,0:T(8,128)}, f32[256,768]{1,0:T(8,128)S(1)}, u32[]{:S(2)}) copy-start(f32[256,768]{1,0:T(8,128)S(1)} %collective-permute-done.22.refs_7_) | copy-start | bytes 2359300
  315.4 44.6 %collective-permute-start.31 = (bf16[512,3072]{1,0:T(8,128)(2,1)}, bf16[512,3072]{1,0:T(8,128)(2,1)}, u32[]{:S(2)}, u32[]{:S(2)}) collective-permute-start(bf16[512,3072]{1,0:T(8,128)(2,1)} %get-tuple-element.111.dgate_ref), channel_id=1, source_target_pairs={{0,1},{1,0},{2,3},{3,2},{4,5},{5,4},{6,7},{7,6}} | collective-permute-start | bytes 9437192 | tf_op jit(solution)/shard_map/ppermute | solution.py:631
  316.6 19.0 %copy-start.34 = (f32[256,768]{1,0:T(8,128)}, f32[256,768]{1,0:T(8,128)S(1)}, u32[]{:S(2)}) copy-start(f32[256,768]{1,0:T(8,128)S(1)} %collective-permute-done.19.refs_4_) | copy-start | bytes 2359300
  316.6 43.4 %collective-permute-start.32 = (bf16[512,3072]{1,0:T(8,128)(2,1)}, bf16[512,3072]{1,0:T(8,128)(2,1)}, u32[]{:S(2)}, u32[]{:S(2)}) collective-permute-start(bf16[512,3072]{1,0:T(8,128)(2,1)} %get-tuple-element.112.dup_ref), channel_id=1, source_target_pairs={{0,1},{1,0},{2,3},{3,2},{4,5},{5,4},{6,7},{7,6}} | collective-permute-start | bytes 9437192 | tf_op jit(solution)/shard_map/ppermute | solution.py:631
  316.7 17.9 %copy-start.48 = (bf16[768,512]{1,0:T(8,128)(2,1)S(1)}, bf16[768,512]{1,0:T(8,128)(2,1)}, u32[]{:S(2)}) copy-start(bf16[768,512]{1,0:T(8,128)(2,1)} %get-tuple-element.109.n2t_ref) | copy-start | bytes 2359300
  316.7 19.0 %copy-start.49 = (bf16[512,768]{1,0:T(8,128)(2,1)S(1)}, bf16[512,768]{1,0:T(8,128)(2,1)}, u32[]{:S(2)}) copy-start(bf16[512,768]{1,0:T(8,128)(2,1)} %get-tuple-element.110.gt_ref) | copy-start | bytes 2359300
  316.7 43.3 %collective-permute-start.33 = (bf16[3072,512]{1,0:T(8,128)(2,1)}, bf16[3072,512]{1,0:T(8,128)(2,1)}, u32[]{:S(2)}, u32[]{:S(2)}) collective-permute-start(bf16[3072,512]{1,0:T(8,128)(2,1)} %get-tuple-element.113.ut_ref), channel_id=1, source_target_pairs={{0,1},{1,0},{2,3},{3,2},{4,5},{5,4},{6,7},{7,6}} | collective-permute-start | bytes 9437192 | tf_op jit(solution)/shard_map/ppermute | solution.py:631
  317.6 14.6 %collective-permute-start.14 = (bf16[384,1024]{1,0:T(8,128)(2,1)S(1)}, bf16[384,1024]{1,0:T(8,128)(2,1)S(1)}, u32[]{:S(2)}, u32[]{:S(2)}) collective-permute-start(bf16[384,1024]{1,0:T(8,128)(2,1)S(1)} %sum_queries.1.mine_ref), channel_id=1, source_target_pairs={{0,1},{1,0},{2,3},{3,2},{4,5},{5,4},{6,7},{7,6}} | collective-permute-start | bytes 2359304 | tf_op jit(solution)/shard_map/ppermute | solution.py:631
  317.7 15.6 %collective-permute-start.24 = (f32[256,768]{1,0:T(8,128)S(1)}, f32[256,768]{1,0:T(8,128)S(1)}, u32[]{:S(2)}, u32[]{:S(2)}) collective-permute-start(f32[256,768]{1,0:T(8,128)S(1)} %collective-permute-done.21.refs_6_), channel_id=1, source_target_pairs={{0,1},{1,0},{2,3},{3,2},{4,5},{5,4},{6,7},{7,6}} | collective-permute-start | bytes 2359304 | tf_op jit(solution)/shard_map/ppermute | solution.py:631
  332.2 2.3 collective-permute-start.26
  333.4 5.4 %copy-start.35 = (f32[256,768]{1,0:T(8,128)}, f32[256,768]{1,0:T(8,128)S(1)}, u32[]{:S(2)}) copy-start(f32[256,768]{1,0:T(8,128)S(1)} %collective-permute-done.24.refs_9_) | copy-start | bytes 2359300
  333.4 2.3 collective-permute-start.25
  334.5 25.4 %collective-permute-start.29 = (bf16[768,512]{1,0:T(8,128)(2,1)S(1)}, bf16[768,512]{1,0:T(8,128)(2,1)S(1)}, u32[]{:S(2)}, u32[]{:S(2)}) collective-permute-start(bf16[768,512]{1,0:T(8,128)(2,1)S(1)} %copy-done.48), channel_id=1, source_target_pairs={{0,1},{1,0},{2,3},{3,2},{4,5},{5,4},{6,7},{7,6}} | collective-permute-start | bytes 2359304 | tf_op jit(solution)/shard_map/ppermute | solution.py:631
  335.7 24.2 %collective-permute-start.30 = (bf16[512,768]{1,0:T(8,128)(2,1)S(1)}, bf16[512,768]{1,0:T(8,128)(2,1)}, u32[]{:S(2)}, u32[]{:S(2)}) collective-permute-start(bf16[512,768]{1,0:T(8,128)(2,1)S(1)} %copy-done.49), channel_id=1, source_target_pairs={{0,1},{1,0},{2,3},{3,2},{4,5},{5,4},{6,7},{7,6}} | collective-permute-start | bytes 2359304 | tf_op jit(solution)/shard_map/ppermute | solution.py:631
  339.4 7.5 %copy-start.4 = (bf16[768,12,64]{0,2,1:T(8,128)(2,1)S(1)}, bf16[768,12,64]{0,2,1:T(8,128)(2,1)}, u32[]{:S(2)}) copy-start(bf16[768,12,64]{0,2,1:T(8,128)(2,1)} %param.18) | copy-start | bytes 3538948
  339.4 7.5 %copy-start.12 = (bf16[1024,768]{1,0:T(8,128)(2,1)S(1)}, bf16[1024,768]{1,0:T(8,128)(2,1)}, u32[]{:S(2)}) copy-start(bf16[1024,768]{1,0:T(8,128)(2,1)} %copy-done.10) | copy-start | bytes 4718596
  339.4 7.5 %copy-start.15 = (s32[5]{0:T(128)S(1)}, s32[5]{0:T(128)}, u32[]{:S(2)}) copy-start(s32[5]{0:T(128)} %copy-done.14) | copy-start | bytes 64
  339.4 7.5 %copy-start.17 = (bf16[1024,768]{1,0:T(8,128)(2,1)S(1)}, bf16[1024,768]{1,0:T(8,128)(2,1)}, u32[]{:S(2)}) copy-start(bf16[1024,768]{1,0:T(8,128)(2,1)} %copy-done.16) | copy-start | bytes 4718596
  339.4 7.5 %copy-start.21 = (f32[512,768]{1,0:T(8,128)S(1)}, f32[512,768]{1,0:T(8,128)}, u32[]{:S(2)}) copy-start(f32[512,768]{1,0:T(8,128)} %get-tuple-element.95.dh_ref) | copy-start | bytes 4718596
  (21 other events, 43.4 us)
